TPU v7x, 256 devices: a whole 4x4x8 slice. The times are simulated.
256 devices in a mesh: space: 32 (over x_lo, z, core), spec: 8 (over x_hi, y).
Axes of the slice: x: 4 (x_hi: 2, x_lo: 2; x = x_hi * 2 + x_lo), y: 4, z: 8, core: 2. Of those that a mesh axis runs over, the one named last changes fastest.
Arguments:
- tracers: float32 [240, 8, 256, 384], P('spec', None, 'space'), may hold values from 0.1 to 10
- courant: float32 [2, 8, 256, 384], P(None, None, 'space'), may hold values from -0.9 to 0.9
- layer_mass: float32 [8, 256, 384], P(None, 'space'), may hold values from 0.5 to 2
- pbl_top: int32 [256, 384], P('space'), may hold values from 1 to 8
- land_type: int32 [256, 384], P('space'), may hold values from 0 to 10
- rates: float32 [11, 240], replicated, may hold values from 0.05 to 3
- coupling: float32 [240, 240], replicated, may hold values from -0.375 to 0.375
Outputs:
- updated: float32 [240, 8, 256, 384], P('spec', None, 'space')
- deposited: float32 [240, 256, 384], P('spec', 'space')
All inputs are finite; a program needn't handle non-finite values.
Results may differ from a plain program's by a relative error of at most 0.0003.
Values sent between devices are 32-bit elements; how exact they have to be, the bound alone decides.
No kernel may reach another device: no remote copies, remote signals or barrier semaphores. Data moves between devices by JAX's collectives and lax.ppermute only.
A program may use at most 128 MiB of HBM per device.

v0:
```python
import jax
import jax.numpy as jnp
from jax import lax
from jax.sharding import PartitionSpec as P

STEPS = 2


def padded_2(array, sides, width):
    for axis, dim in sides:
        devices, length = (lax.axis_size(axis), array.shape[dim])
        up = [(i, (i + 1) % devices) for i in range(devices - 1)]
        down = [(j, i) for i, j in up]
        last = lax.slice_in_dim(array, length - width, length, axis=dim)
        leading = lax.slice_in_dim(array, 0, width, axis=dim)
        before = lax.ppermute(last, axis, up)
        after = lax.ppermute(leading, axis, down)
        array = jnp.concatenate([before, array, after], axis=dim)
    return array


def side_by_side(arrays, axis, split_dim, concat_dim, along):
    both = jnp.concatenate(arrays, axis=along)
    whole, at, finished = (
        lax.all_to_all(both, axis, split_axis=split_dim, concat_axis=concat_dim, tiled=True),
        0,
        [],
    )
    for a in arrays:
        finished.append(lax.slice_in_dim(whole, at, at + a.shape[along], axis=along))
        at += a.shape[along]
    return tuple(finished)


def sweep(field, speed, axis):
    count = field.shape[axis]

    def cut(a, lo, hi):
        return lax.slice_in_dim(a, lo, hi, axis=axis)

    edge = 7.0 / 12.0 * (cut(field, 1, count - 2) + cut(field, 2, count - 1)) - 1.0 / 12.0 * (
        cut(field, 0, count - 3) + cut(field, 3, count)
    )
    lower = cut(edge, 0, count - 4)
    upper = cut(edge, 1, count - 3)
    centre = cut(field, 2, count - 2)
    slope = upper - lower
    curve = 6.0 * (centre - 0.5 * (lower + upper))
    cells = count - 4
    face = cut(speed, 3, count - 2)
    upwind = face * (
        cut(upper, 0, cells - 1)
        - 0.5
        * face
        * (cut(slope, 0, cells - 1) - (1.0 - 2.0 * face / 3.0) * cut(curve, 0, cells - 1))
    )
    downwind = face * (
        cut(lower, 1, cells)
        - 0.5 * face * (cut(slope, 1, cells) + (1.0 + 2.0 * face / 3.0) * cut(curve, 1, cells))
    )
    flux = jnp.where(face >= 0.0, upwind, downwind)
    return cut(field, 3, count - 3) - (cut(flux, 1, count - 5) - cut(flux, 0, count - 6))


def across(field, speed):
    padded = jnp.pad(field, ((0, 0), (0, 0), (0, 0), (3, 3)))
    return sweep(padded, jnp.pad(speed, ((0, 0), (0, 0), (3, 3))), -1)


def mixing(field, layer_mass, pbl_top):
    levels = jnp.arange(field.shape[1], dtype=jnp.int32)[:, None, None]
    inside = levels < pbl_top[None]
    weights = jnp.where(inside, layer_mass, 0.0)
    average = jnp.sum(weights[None] * field, axis=1) / jnp.sum(weights, axis=0)[None]
    return jnp.where(inside[None], average[:, None], field)


def deposit(field, surface_mass, land_type, rates):
    kinds = jnp.arange(rates.shape[0], dtype=jnp.int32)[:, None]
    onehot = (land_type == kinds).astype(jnp.float32)
    loss = jnp.dot(rates.T, onehot, precision=lax.Precision.HIGHEST).reshape(
        field.shape[0], field.shape[2], field.shape[3]
    )
    bottom = field[:, 0]
    kept = bottom * jnp.exp(-loss)
    return (field.at[:, 0].set(kept), (bottom - kept) * surface_mass[None])


def on_device(tracers, courant, layer_mass, pbl_top, land_type, rates, coupling):
    field = tracers
    for step in range(STEPS):
        padded, speed = (padded_2(field, (("space", 2),), 3), padded_2(courant, (("space", 2),), 3))
        field = sweep(padded, speed[0], -2)
        field = across(field, courant[1])
    gathered = lax.all_to_all(field, "spec", split_axis=2, concat_axis=0, tiled=True)
    part = gathered.shape[2]
    start_row = lax.axis_index("spec") * part
    mass = lax.dynamic_slice_in_dim(layer_mass, start_row, part, 1)
    tops = lax.dynamic_slice_in_dim(pbl_top, start_row, part, 0)
    kinds = lax.dynamic_slice_in_dim(land_type, start_row, part, 0)
    mixed = mixing(gathered, mass, tops)
    coupled = mixed + jnp.dot(
        coupling, mixed.reshape(mixed.shape[0], -1), precision=lax.Precision.HIGHEST
    ).reshape(mixed.shape)
    column_out, column_flux = deposit(coupled, mass[0], kinds, rates)
    updated, returned = side_by_side((column_out, column_flux[:, None]), "spec", 0, 2, 1)
    deposited = returned[:, 0]
    return (updated, deposited)


def solution(mesh):
    return jax.shard_map(
        on_device,
        mesh=mesh,
        in_specs=(
            P("spec", None, "space", None),
            P(None, None, "space", None),
            P(None, "space", None),
            P("space", None),
            P("space", None),
            P(),
            P(),
        ),
        out_specs=(P("spec", None, "space", None), P("spec", "space", None)),
        check_vma=False,
    )
```

profile of v0, /device:TPU:96, one launch (start us, length us, event | category | flops | bytes accessed | tf_op | source)
XLA Modules:
  0.0 186.1 jit_solution(6596910352486164995)
XLA Ops:
  0.6 0.0 copy-start
  0.6 2.4 %copy.89 = f32[30,8,8,384]{3,1,0,2:T(8,128)S(1)} copy(f32[30,8,8,384]{3,2,1,0:T(8,128)} %param.9) | data formatting | bytes 5898240 | tf_op args[0]
  3.1 0.0 copy-start.3
  3.1 0.1 fusion.72
  3.3 0.0 copy-start.1
  3.3 2.2 %collective-permute-start.2 = (f32[30,8,3,384]{3,1,0,2:T(8,128)S(1)}, f32[30,8,3,384]{3,1,0,2:T(8,128)S(1)}, u32[]{:S(2)}, u32[]{:S(2)}) collective-permute-start(f32[30,8,3,384]{3,1,0,2:T(8,128)S(1)} %get-tuple-element.29), channel_id=1, source_target_pairs={{0,8},{8,16},{16,24},{24,32},{32,40},{40,48},{48,56},{56,64},{64,7... | collective-permute-start | bytes 3317768 | tf_op jit(solution)/shard_map/ppermute | solution.py:16
  5.5 3.6 %collective-permute-start.3 = (f32[30,8,3,384]{3,1,0,2:T(8,128)S(1)}, f32[30,8,3,384]{3,1,0,2:T(8,128)S(1)}, u32[]{:S(2)}, u32[]{:S(2)}) collective-permute-start(f32[30,8,3,384]{3,1,0,2:T(8,128)S(1)} %get-tuple-element.28), channel_id=1, source_target_pairs={{8,0},{16,8},{24,16},{32,24},{40,32},{48,40},{56,48},{64,56},{72,6... | collective-permute-start | bytes 3317768 | tf_op jit(solution)/shard_map/ppermute | solution.py:17
  9.2 3.4 %collective-permute-start = (f32[2,8,3,384]{3,1,2,0:T(8,128)S(1)}, f32[2,8,3,384]{3,1,2,0:T(8,128)S(1)}, u32[]{:S(2)}, u32[]{:S(2)}) collective-permute-start(f32[2,8,3,384]{3,1,2,0:T(8,128)S(1)} %get-tuple-element.30), channel_id=1, source_target_pairs={{0,8},{8,16},{16,24},{24,32},{32,40},{40,48},{48,56},{56,64},{64,7... | collective-permute-start | bytes 221192 | tf_op jit(solution)/shard_map/ppermute | solution.py:16
  12.6 2.1 %collective-permute-start.1 = (f32[2,8,3,384]{3,1,2,0:T(8,128)S(1)}, f32[2,8,3,384]{3,1,2,0:T(8,128)S(1)}, u32[]{:S(2)}, u32[]{:S(2)}) collective-permute-start(f32[2,8,3,384]{3,1,2,0:T(8,128)S(1)} %get-tuple-element.31), channel_id=1, source_target_pairs={{8,0},{16,8},{24,16},{32,24},{40,32},{48,40},{56,48},{64,56},{72,6... | collective-permute-start | bytes 221192 | tf_op jit(solution)/shard_map/ppermute | solution.py:17
  14.9 0.1 copy.91
  15.0 0.1 copy.92
  15.0 0.1 copy.93
  15.1 0.1 copy.94
  15.2 5.8 %collective-permute-done = f32[2,8,3,384]{3,1,2,0:T(8,128)S(1)} collective-permute-done((f32[2,8,3,384]{3,1,2,0:T(8,128)S(1)}, f32[2,8,3,384]{3,1,2,0:T(8,128)S(1)}, u32[]{:S(2)}, u32[]{:S(2)}) %collective-permute-start) | collective-permute-done | bytes 73760 | tf_op jit(solution)/shard_map/ppermute | solution.py:16
  21.1 1.8 collective-permute-done.1
  22.9 0.1 constant_dynamic-update-slice_fusion.2
  23.0 0.5 constant_dynamic-update-slice_fusion.1
  23.5 0.0 collective-permute-done.3
  23.5 0.1 constant_dynamic-update-slice_fusion
  23.6 1.2 fusion.3
  24.8 0.7 slice_subtract_fusion.5
  25.5 0.0 copy-start.2
  25.5 1.9 fusion.53
  27.4 0.6 fusion.61
  28.0 3.3 %fusion.8 = f32[30,8,8,387]{3,1,0,2:T(8,128)S(1)} fusion(f32[30,8,8,384]{3,1,0,2:T(8,128)S(1)} %fusion.61), kind=kLoop, calls=%fused_computation.23 | loop fusion | flops 3715200 | bytes 5921280 | tf_op jit(solution)/shard_map/sub | solution.py:41
  31.3 2.1 %slice_subtract_fusion.1 = (f32[30,8,8,386]{3,1,0,2:T(8,128)S(1)}, f32[30,8,8,386]{3,1,0,2:T(8,128)S(1)}) fusion(f32[30,8,8,387]{3,1,0,2:T(8,128)S(1)} %fusion.8, f32[30,8,8,384]{3,1,0,2:T(8,128)S(1)} %fusion.61), kind=kLoop, calls=%fused_computation.58 | loop fusion | flops 3705600 | bytes 14807040 | tf_op jit(solution)/shard_map/sub | solution.py:47
  33.4 3.2 %fusion.33 = f32[30,8,8,385]{3,1,0,2:T(8,128)S(1)} fusion(f32[30,8,8,386]{3,1,0,2:T(8,128)S(1)} %get-tuple-element.25, f32[30,8,8,386]{3,1,0,2:T(8,128)S(1)} %get-tuple-element.24, f32[30,8,8,387]{3,1,0,2:T(8,128)S(1)} %fusion.8, f32[8,8,385]{2,0,1:T(8,128)S(1)} %copy.94, f32[8,8,385]{2,0,1:T(8,128)S(1)} %copy.93, f32[8,8,385]{2,0,1:T(8,128)S(1)} %copy.92, ...), kind=kLoop, calls=%fused_computation.51 | loop fusion | flops 8131200 | bytes 18159680 | tf_op jit(solution)/shard_map/jit(_where)/select_n | solution.py:61
  36.6 1.0 fusion.60
  37.7 0.1 fusion.71
  37.8 6.5 %collective-permute-start.4 = (f32[30,8,3,384]{3,1,0,2:T(8,128)S(1)}, f32[30,8,3,384]{3,1,0,2:T(8,128)S(1)}, u32[]{:S(2)}, u32[]{:S(2)}) collective-permute-start(f32[30,8,3,384]{3,1,0,2:T(8,128)S(1)} %get-tuple-element.26), channel_id=1, source_target_pairs={{0,8},{8,16},{16,24},{24,32},{32,40},{40,48},{48,56},{56,64},{64,7... | collective-permute-start | bytes 3317768 | tf_op jit(solution)/shard_map/ppermute | solution.py:16
  44.4 2.1 %collective-permute-start.5 = (f32[30,8,3,384]{3,1,0,2:T(8,128)S(1)}, f32[30,8,3,384]{3,1,0,2:T(8,128)S(1)}, u32[]{:S(2)}, u32[]{:S(2)}) collective-permute-start(f32[30,8,3,384]{3,1,0,2:T(8,128)S(1)} %get-tuple-element.27), channel_id=1, source_target_pairs={{8,0},{16,8},{24,16},{32,24},{40,32},{48,40},{56,48},{64,56},{72,6... | collective-permute-start | bytes 3317768 | tf_op jit(solution)/shard_map/ppermute | solution.py:17
  46.5 8.3 %collective-permute-done.4 = f32[30,8,3,384]{3,1,0,2:T(8,128)S(1)} collective-permute-done((f32[30,8,3,384]{3,1,0,2:T(8,128)S(1)}, f32[30,8,3,384]{3,1,0,2:T(8,128)S(1)}, u32[]{:S(2)}, u32[]{:S(2)}) %collective-permute-start.4) | collective-permute-done | bytes 1105952 | tf_op jit(solution)/shard_map/ppermute | solution.py:16
  54.7 4.5 %collective-permute-done.5 = f32[30,8,3,384]{3,1,0,2:T(8,128)S(1)} collective-permute-done((f32[30,8,3,384]{3,1,0,2:T(8,128)S(1)}, f32[30,8,3,384]{3,1,0,2:T(8,128)S(1)}, u32[]{:S(2)}, u32[]{:S(2)}) %collective-permute-start.5) | collective-permute-done | bytes 1105952 | tf_op jit(solution)/shard_map/ppermute | solution.py:17
  59.2 0.3 pad_maximum_fusion
  59.5 1.2 fusion.1
  60.8 2.5 %slice_subtract_fusion.4 = (f32[30,8,10,384]{3,1,0,2:T(8,128)S(1)}, f32[30,8,10,384]{3,1,0,2:T(8,128)}) fusion(f32[30,8,11,384]{3,1,0,2:T(8,128)S(1)} %fusion.1, f32[30,8,14,384]{3,1,0,2:T(8,128)S(1)} %pad_maximum_fusion), kind=kLoop, calls=%fused_computation.63 | loop fusion | flops 4608000 | bytes 18432000 | tf_op jit(solution)/shard_map/sub | solution.py:47
  63.3 3.8 %fusion.44 = f32[30,8,9,384]{3,1,0,2:T(8,128)S(1)} fusion(f32[30,8,10,384]{3,1,0,2:T(8,128)} %get-tuple-element.19, f32[30,8,10,384]{3,1,0,2:T(8,128)S(1)} %get-tuple-element.18, f32[30,8,11,384]{3,1,0,2:T(8,128)S(1)} %fusion.1, f32[8,9,384]{2,0,1:T(8,128)S(1)} %get-tuple-element.35, f32[8,9,384]{2,0,1:T(8,128)S(1)} %get-tuple-element.34, ...), kind=kLoop, calls=%fused_computation.70 | loop fusion | flops 9123840 | bytes 20376576 | tf_op jit(solution)/shard_map/jit(_where)/select_n | solution.py:61
  67.1 0.3 fusion.59
  67.4 3.3 %fusion.15 = f32[30,8,8,387]{3,1,0,2:T(8,128)S(1)} fusion(f32[30,8,8,384]{3,1,0,2:T(8,128)S(1)} %fusion.59), kind=kLoop, calls=%fused_computation.30 | loop fusion | flops 3715200 | bytes 5921280 | tf_op jit(solution)/shard_map/sub | solution.py:41
  70.7 2.1 %slice_subtract_fusion = (f32[30,8,8,386]{3,1,0,2:T(8,128)S(1)}, f32[30,8,8,386]{3,1,0,2:T(8,128)S(1)}) fusion(f32[30,8,8,387]{3,1,0,2:T(8,128)S(1)} %fusion.15, f32[30,8,8,384]{3,1,0,2:T(8,128)S(1)} %fusion.59), kind=kLoop, calls=%fused_computation.57 | loop fusion | flops 3705600 | bytes 14807040 | tf_op jit(solution)/shard_map/sub | solution.py:47
  72.8 3.2 %fusion.24 = f32[30,8,8,385]{3,1,0,2:T(8,128)S(1)} fusion(f32[30,8,8,386]{3,1,0,2:T(8,128)S(1)} %get-tuple-element.23, f32[30,8,8,386]{3,1,0,2:T(8,128)S(1)} %get-tuple-element.22, f32[30,8,8,387]{3,1,0,2:T(8,128)S(1)} %fusion.15, f32[8,8,385]{2,0,1:T(8,128)S(1)} %copy.94, f32[8,8,385]{2,0,1:T(8,128)S(1)} %copy.93, f32[8,8,385]{2,0,1:T(8,128)S(1)} %copy.92, ...), kind=kLoop, calls=%fused_computation.40 | loop fusion | flops 8131200 | bytes 18159680 | tf_op jit(solution)/shard_map/jit(_where)/select_n | solution.py:61
  76.0 2.6 %fusion.58 = f32[30,8,8,384]{3,1,0,2:T(8,128)} fusion(f32[30,8,8,384]{3,1,0,2:T(8,128)S(1)} %fusion.59, f32[30,8,8,385]{3,1,0,2:T(8,128)S(1)} %fusion.24), kind=kLoop, calls=%fused_computation.90 | loop fusion | flops 1474560 | bytes 11796480 | tf_op jit(solution)/shard_map/sub | solution.py:62
  78.6 6.9 %all-to-all-start = ((f32[30,8,8,384]{3,1,0,2:T(8,128)}), f32[30,8,8,384]{3,1,0,2:T(8,128)S(1)}, u32[]{:S(2)}, u32[]{:S(2)}) async-start(f32[30,8,8,384]{3,1,0,2:T(8,128)} %fusion.58), calls=%async_computation | async-start | bytes 5898240 | tf_op jit(solution)/shard_map/all_to_all | solution.py:95
  85.5 0.7 dynamic-slice_reduce_fusion
  86.3 0.9 constant_dynamic-slice_fusion
  87.3 34.4 %all-to-all-done = f32[30,8,8,384]{3,1,0,2:T(8,128)S(1)} async-done(((f32[30,8,8,384]{3,1,0,2:T(8,128)}), f32[30,8,8,384]{3,1,0,2:T(8,128)S(1)}, u32[]{:S(2)}, u32[]{:S(2)}) %all-to-all-start) | async-done | bytes 2949152 | tf_op jit(solution)/shard_map/all_to_all | solution.py:95
  121.7 1.6 fusion.62
  123.3 1.8 reduce_sum.21
  125.1 1.0 broadcast_divide_fusion
  126.1 0.2 broadcast_in_dim.34.clone
  126.3 0.5 copy.102
  126.9 0.5 copy.103
  127.4 3.0 %fusion.63 = f32[3072,240]{0,1:T(8,128)S(1)} fusion(f32[240,240]{1,0:T(8,128)S(1)} %copy-done, f32[240,3072]{1,0:T(8,128)S(1)} %bitcast.59, f32[240,3072]{1,0:T(8,128)S(1)} %bitcast.61, pred[3072]{0:T(1024)(128)(4,1)S(1)} %lt.50), kind=kOutput, calls=%fused_computation.101 | convolution fusion | flops 2124103680 | bytes 9080832 | tf_op jit(solution)/shard_map/dot_general | solution.py:102
  130.4 0.5 copy.104
  131.0 0.0 copy-start.4
  131.0 1.0 copy_add_fusion
  132.0 0.4 fusion.68
  132.3 0.1 multiply_bitcast_fusion
  132.4 0.2 pad_maximum_fusion.1
  132.7 3.4 %copy.98 = f32[240,9,1,384]{3,2,1,0:T(1,128)S(1)} copy(f32[240,9,1,384]{3,0,2,1:T(8,128)S(1)} %pad_maximum_fusion.1) | data formatting | bytes 6635520 | tf_op jit(solution)/shard_map/concatenate | solution.py:23
  136.1 47.0 %all_to_all.39 = f32[240,9,1,384]{3,2,1,0:T(1,128)S(1)} all-to-all(f32[240,9,1,384]{3,2,1,0:T(1,128)S(1)} %copy.98), channel_id=1, replica_groups=mesh['space'=32,'spec'=8] {'spec'}, dimensions={0} | all-to-all | bytes 6635520 | tf_op jit(solution)/shard_map/all_to_all | solution.py:25
  183.1 0.2 copy.115
  183.3 2.0 %slice.368 = f32[30,8,8,384]{3,2,1,0:T(8,128)} slice(f32[30,9,8,384]{3,2,1,0:T(8,128)S(1)} %bitcast.56), slice={[0:30], [0:8], [0:8], [0:384]} | slice | bytes 5898240 | tf_op jit(solution)/shard_map/slice | solution.py:30
  185.3 0.8 slice_bitcast_fusion
  (21 shorter events, 0.3 us)
Async XLA Ops:
  0.6 126.8 %copy-start = (f32[240,240]{1,0:T(8,128)S(1)}, f32[240,240]{1,0:T(8,128)}, u32[]{:S(2)}) copy-start(f32[240,240]{1,0:T(8,128)} %param.15) | copy-start | bytes 691204
  3.1 6.0 %copy-start.3 = (f32[2,8,8,384]{3,2,1,0:T(8,128)S(1)}, f32[2,8,8,384]{3,2,1,0:T(8,128)}, u32[]{:S(2)}) copy-start(f32[2,8,8,384]{3,2,1,0:T(8,128)} %param.10) | copy-start | bytes 589828
  3.3 19.7 %copy-start.1 = (f32[30,8,8,384]{3,2,1,0:T(8,128)S(1)}, f32[30,8,8,384]{3,2,1,0:T(8,128)}, u32[]{:S(2)}) copy-start(f32[30,8,8,384]{3,2,1,0:T(8,128)} %param.9) | copy-start | bytes 8847364
  3.3 19.6 %collective-permute-start.2 = (f32[30,8,3,384]{3,1,0,2:T(8,128)S(1)}, f32[30,8,3,384]{3,1,0,2:T(8,128)S(1)}, u32[]{:S(2)}, u32[]{:S(2)}) collective-permute-start(f32[30,8,3,384]{3,1,0,2:T(8,128)S(1)} %get-tuple-element.29), channel_id=1, source_target_pairs={{0,8},{8,16},{16,24},{24,32},{32,40},{40,48},{48,56},{56,64},{64,7... | collective-permute-start | bytes 3317768 | tf_op jit(solution)/shard_map/ppermute | solution.py:16
  5.5 18.0 %collective-permute-start.3 = (f32[30,8,3,384]{3,1,0,2:T(8,128)S(1)}, f32[30,8,3,384]{3,1,0,2:T(8,128)S(1)}, u32[]{:S(2)}, u32[]{:S(2)}) collective-permute-start(f32[30,8,3,384]{3,1,0,2:T(8,128)S(1)} %get-tuple-element.28), channel_id=1, source_target_pairs={{8,0},{16,8},{24,16},{32,24},{40,32},{48,40},{56,48},{64,56},{72,6... | collective-permute-start | bytes 3317768 | tf_op jit(solution)/shard_map/ppermute | solution.py:17
  9.2 11.9 %collective-permute-start = (f32[2,8,3,384]{3,1,2,0:T(8,128)S(1)}, f32[2,8,3,384]{3,1,2,0:T(8,128)S(1)}, u32[]{:S(2)}, u32[]{:S(2)}) collective-permute-start(f32[2,8,3,384]{3,1,2,0:T(8,128)S(1)} %get-tuple-element.30), channel_id=1, source_target_pairs={{0,8},{8,16},{16,24},{24,32},{32,40},{40,48},{48,56},{56,64},{64,7... | collective-permute-start | bytes 221192 | tf_op jit(solution)/shard_map/ppermute | solution.py:16
  12.6 10.2 %collective-permute-start.1 = (f32[2,8,3,384]{3,1,2,0:T(8,128)S(1)}, f32[2,8,3,384]{3,1,2,0:T(8,128)S(1)}, u32[]{:S(2)}, u32[]{:S(2)}) collective-permute-start(f32[2,8,3,384]{3,1,2,0:T(8,128)S(1)} %get-tuple-element.31), channel_id=1, source_target_pairs={{8,0},{16,8},{24,16},{32,24},{40,32},{48,40},{56,48},{64,56},{72,6... | collective-permute-start | bytes 221192 | tf_op jit(solution)/shard_map/ppermute | solution.py:17
  25.5 1.9 %copy-start.2 = (f32[30,8,8,384]{3,2,1,0:T(8,128)S(1)}, f32[30,8,8,384]{3,2,1,0:T(8,128)}, u32[]{:S(2)}) copy-start(f32[30,8,8,384]{3,2,1,0:T(8,128)} %param.9) | copy-start | bytes 8847364
  37.8 16.9 %collective-permute-start.4 = (f32[30,8,3,384]{3,1,0,2:T(8,128)S(1)}, f32[30,8,3,384]{3,1,0,2:T(8,128)S(1)}, u32[]{:S(2)}, u32[]{:S(2)}) collective-permute-start(f32[30,8,3,384]{3,1,0,2:T(8,128)S(1)} %get-tuple-element.26), channel_id=1, source_target_pairs={{0,8},{8,16},{16,24},{24,32},{32,40},{40,48},{48,56},{56,64},{64,7... | collective-permute-start | bytes 3317768 | tf_op jit(solution)/shard_map/ppermute | solution.py:16
  44.4 14.8 %collective-permute-start.5 = (f32[30,8,3,384]{3,1,0,2:T(8,128)S(1)}, f32[30,8,3,384]{3,1,0,2:T(8,128)S(1)}, u32[]{:S(2)}, u32[]{:S(2)}) collective-permute-start(f32[30,8,3,384]{3,1,0,2:T(8,128)S(1)} %get-tuple-element.27), channel_id=1, source_target_pairs={{8,0},{16,8},{24,16},{32,24},{40,32},{48,40},{56,48},{64,56},{72,6... | collective-permute-start | bytes 3317768 | tf_op jit(solution)/shard_map/ppermute | solution.py:17
  78.6 43.1 %all-to-all-start = ((f32[30,8,8,384]{3,1,0,2:T(8,128)}), f32[30,8,8,384]{3,1,0,2:T(8,128)S(1)}, u32[]{:S(2)}, u32[]{:S(2)}) async-start(f32[30,8,8,384]{3,1,0,2:T(8,128)} %fusion.58), calls=%async_computation | async-start | bytes 5898240 | tf_op jit(solution)/shard_map/all_to_all | solution.py:95
  131.0 1.0 copy-start.4
where the time goes:
time: 187 us; the launch traced here: 186 us
  waiting for transfers between devices  54.7 us (29%)
  blocking collectives  47 us (25%)
  other arithmetic  37.4 us (20%)
  starting transfers between devices  26.9 us (14%)
  local copies, waits for them, and re-layouts  15.4 us (8%)
  matrix products  3.39 us (2%)
    all_to_all x1, blocking collectives, side_by_side(): lax.all_to_all(both, axis, split_axis=split_dim, concat_axis=concat_dim,...  47 us
    all_to_all x1, waiting for transfers between devices, on_device(): lax.all_to_all(field, 'spec', split_axis=2, concat_axis=0, tiled=True)  34.4 us
    ppermute x3, waiting for transfers between devices, padded_2(): before = lax.ppermute(last, axis, up)  14.1 us
    ppermute x3, starting transfers between devices, padded_2(): before = lax.ppermute(last, axis, up)  12.1 us
    select_n x4, other arithmetic, sweep(): flux = jnp.where(face >= 0.0, upwind, downwind)  12.1 us
    sub x4, other arithmetic, sweep(): 7.0 / 12.0 * (cut(field, 1, count - 2) + cut(field, 2, count - 1))  9.02 us
    ppermute x3, starting transfers between devices, padded_2(): after = lax.ppermute(leading, axis, down)  7.89 us
    sub x4, other arithmetic, sweep(): slope = upper - lower  7.37 us
  transfers between devices with their start and end apart: 7, of which 5 were waited for; matrix products, arithmetic and copies ran while one was open for 2% of the time, Pallas kernels for 0%

commit v1 on v0

v1 whole, which is shorter than its diff:
```python
import functools

import jax
import jax.numpy as jnp
from jax import lax
from jax.experimental import pallas as pl
from jax.experimental.pallas import tpu as pltpu
from jax.sharding import PartitionSpec as P

INTERPRET = False
F32 = jnp.float32
BF16 = jnp.bfloat16
TAPS = 7
HALO = 6


def call(body, out_shape, **kw):
    return pl.pallas_call(body, out_shape=out_shape, interpret=INTERPRET, **kw)


def pack_even(x, cf, own, up, down, speeds):
    tiles = own.shape[1] // 8
    width = own.shape[1]
    for r in range(8):
        for i in range(tiles):
            value = x[pl.ds(i * 128 + r, 8, stride=16), :]
            own[r, i * 8 : i * 8 + 8, :] = value
            if r >= 2:
                at = (r - 2) * width + i * 8
                up[at : at + 8, :] = value
            if r < 6:
                at = r * width + i * 8
                down[at : at + 8, :] = value
    for d in range(2):
        for parity in range(2):
            for row in range(4):
                at = HALO * width + ((d * 2 + parity) * 4 + row) * 4
                start = d * 64 + parity * 8 + row
                before = cf[pl.ds(start, 4, stride=16), :]
                after = cf[pl.ds(start + 4, 4, stride=16), :]
                down[at : at + 4, :] = before
                up[at : at + 4, :] = after
                for half in (slice(0, 4), slice(4, 8)):
                    speeds[parity, d, row, half, :] = before
                    speeds[parity, d, row + 4, half, :] = after


def pack_odd(x, own):
    for r in range(8):
        for i in range(own.shape[1] // 8):
            own[r, i * 8 : i * 8 + 8, :] = x[pl.ds(i * 128 + 8 + r, 8, stride=16), :]


def flux_taps(c):
    u = jnp.abs(c)
    square = u * u
    edge = c * (1.0 - u) * (1.0 - u)
    other = square * (1.0 - u)
    centre = square * (3.0 - 2.0 * u)
    ahead = c >= 0.0
    below = jnp.where(ahead, -other, 0.0)
    above = jnp.where(ahead, 0.0, other)
    lower = jnp.where(ahead, centre, 0.0)
    upper = jnp.where(ahead, 0.0, -centre)
    a, b = 7.0 / 12.0, 1.0 / 12.0
    return (
        -b * below,
        a * below - b * edge,
        a * (edge + below) - b * above + lower,
        a * (edge + above) - b * below + upper,
        a * above - b * edge,
        -b * above,
    )


def cell_taps(low, high):
    return (
        low[0],
        low[1] - high[0],
        low[2] - high[1],
        1.0 + low[3] - high[2],
        low[4] - high[3],
        low[5] - high[4],
        -high[5],
    )


def transport(parity, own, up, down, cup, cdown, cf, valid, out, c, wx, wy, mid):
    width = own.shape[1]
    ny = own.shape[2]
    for d in range(2):
        c[d, 4:12] = cf[parity, d]
        for row in range(4):
            at = ((d * 2 + parity) * 4 + row) * 4
            for half in (slice(0, 4), slice(4, 8)):
                c[d, row, half, :] = cup[at : at + 4, :]
                c[d, row + 12, half, :] = cdown[at : at + 4, :]
    lane = lax.broadcasted_iota(jnp.int32, (8, ny), 1)
    inside = valid[0, 0]
    for t in range(ny // 128):
        cols = slice(t * 128, t * 128 + 128)
        high = flux_taps(c[0, 1, :, cols])
        for row in range(14):
            low, high = high, flux_taps(c[0, row + 2, :, cols])
            for k, w in enumerate(cell_taps(low, high)):
                wx[row, k, :, cols] = w * inside if row < 3 else w

    def y_weights(row, carry):
        speed = c[1, row + 1]
        low = flux_taps(speed)
        high = flux_taps(jnp.where(lane == ny - 1, 0.0, pltpu.roll(speed, ny - 1, 1)))
        for k, w in enumerate(cell_taps(low, high)):
            shift = k - 3
            w = jnp.where((lane + shift >= 0) & (lane + shift < ny), w, 0.0)
            wy[row, k] = w
        return carry

    lax.fori_loop(0, 14, y_weights, 0)

    def across(value, row):
        total = wy[row, 3] * value
        for shift in (1, 2, 3):
            total += wy[row, 3 + shift] * pltpu.roll(value, ny - shift, 1)
            total += wy[row, 3 - shift] * pltpu.roll(value, shift, 1)
        return total

    def tile(i, carry):
        at = pl.multiple_of(i * 8, 8)

        def first(row, cols):
            if row < 0:
                return up[pl.ds((row + HALO) * width + at, 8), cols]
            if row < 8:
                return own[row, pl.ds(at, 8), cols]
            return down[pl.ds((row - 8) * width + at, 8), cols]

        def along(read, row):
            parts = []
            for t in range(ny // 128):
                cols = slice(t * 128, t * 128 + 128)
                total = wx[row + 3, 0, :, cols] * read(row - 3, cols)
                for k in range(1, TAPS):
                    total += wx[row + 3, k, :, cols] * read(row + k - 3, cols)
                parts.append(total)
            return jnp.concatenate(parts, axis=1)

        for row in range(-3, 11):
            mid[row + 3] = across(along(first, row), row + 3)
        for row in range(8):
            value = along(lambda at_row, cols: mid[at_row + 3, :, cols], row)
            out[row, pl.ds(at, 8), :] = across(value, row + 3)
        return carry

    lax.fori_loop(0, width // 8, tile, 0)


def halves(value):
    top = value.astype(BF16)
    return top, (value - top.astype(F32)).astype(BF16)


def couple(x, matrix, out, wide):
    species = matrix.shape[0]
    for j in range(4):
        wide[:, j * 128 : j * 128 + 128] = x[pl.ds(j, species, stride=4), :]
    value = wide[...]
    top, rest = halves(value)
    high, low = halves(matrix[...])
    total = jnp.dot(high, top, preferred_element_type=F32)
    total += jnp.dot(high, rest, preferred_element_type=F32)
    total += jnp.dot(low, top, preferred_element_type=F32)
    wide[...] = value + total
    for j in range(4):
        out[pl.ds(j, species, stride=4), :] = wide[:, j * 128 : j * 128 + 128]


def prepare(lm, pbl, land, rates, keep, weven, wodd):
    ny = lm.shape[1]
    kinds = lax.broadcasted_iota(jnp.int32, (rates.shape[1], ny), 0)
    levels = lax.broadcasted_iota(jnp.int32, (8, ny), 0)
    evens = 2 * lax.broadcasted_iota(jnp.int32, (4, ny), 0)
    for r in range(8):
        top = pbl[r : r + 1, :]
        mass = lm[pl.ds(r, 8, stride=8), :]
        total = jnp.sum(jnp.where(levels < top, mass, 0.0), axis=0, keepdims=True)
        scale = 1.0 / total
        even = jnp.where(evens < top, lm[pl.ds(r, 4, stride=16), :], 0.0) * scale
        odd = jnp.where(evens + 1 < top, lm[pl.ds(8 + r, 4, stride=16), :], 0.0) * scale
        weven[r, 0:4, :] = even
        weven[r, 4:8, :] = even
        wodd[r, 0:4, :] = odd
        wodd[r, 4:8, :] = odd
        onehot = (kinds == land[r : r + 1, :]).astype(F32)
        loss = jnp.dot(
            rates[...], onehot, precision=lax.Precision.HIGHEST, preferred_element_type=F32
        )
        keep[r] = jnp.exp(-loss)


def finish(even, odd, keep, weven, wodd, pbl, lm, out, dep, flux):
    ny = even.shape[2]
    sub = lax.broadcasted_iota(jnp.int32, (8, ny), 0)
    level = 2 * (sub % 4)
    first = sub % 2 == 0
    low = sub % 4 < 2
    for r in range(8):
        top = pbl[r : r + 1, :]
        for i in range(even.shape[1] // 8):
            at = slice(i * 8, i * 8 + 8)
            a, b = even[r, at, :], odd[r, at, :]
            total = weven[r] * a + wodd[r] * b
            total += jnp.where(first, pltpu.roll(total, 7, 0), pltpu.roll(total, 1, 0))
            total += jnp.where(low, pltpu.roll(total, 6, 0), pltpu.roll(total, 2, 0))
            a = jnp.where(level < top, total, a)
            b = jnp.where(level + 1 < top, total, b)
            kept = a * keep[r, at, :]
            flux[at, :] = (a - kept) * lm[r : r + 1, :]
            out[pl.ds(i * 128 + r, 8, stride=16), :] = kept
            out[pl.ds(i * 128 + 8 + r, 8, stride=16), :] = b
        count = even.shape[1] // 4
        dep[pl.ds(r, count, stride=8), :] = flux[pl.ds(0, count, stride=4), :]


def on_device(tracers, courant, layer_mass, pbl_top, land_type, rates, coupling):
    own_species, levels, rows, ny = tracers.shape
    species = coupling.shape[0]
    width = own_species * 4
    sds = jax.ShapeDtypeStruct
    n_space, n_spec = lax.axis_size("space"), lax.axis_size("spec")
    up_pairs = [(i, i + 1) for i in range(n_space - 1)]
    down_pairs = [(j, i) for i, j in up_pairs]
    flat = tracers.reshape(-1, ny)
    cf = courant.reshape(-1, ny)
    lm = layer_mass.reshape(-1, ny)
    valid = (lax.axis_index("space") > 0).astype(F32).reshape(1, 1)

    group = sds((rows, width, ny), F32)
    edge = sds((HALO * width + 64, ny), F32)
    speeds = sds((2, 2, rows, 8, ny), F32)
    strips = ny // 128

    def strip(*shape):
        return pl.BlockSpec((*shape, 128), lambda t: (0,) * len(shape) + (t,))

    even, send_up, send_down, speeds = call(
        pack_even,
        (group, edge, edge, speeds),
        grid=(strips,),
        in_specs=[strip(flat.shape[0]), strip(cf.shape[0])],
        out_specs=[
            strip(rows, width),
            strip(edge.shape[0]),
            strip(edge.shape[0]),
            strip(2, 2, rows, 8),
        ],
    )(flat, cf)
    up = lax.ppermute(send_up, "space", up_pairs)
    down = lax.ppermute(send_down, "space", down_pairs)
    odd = call(
        pack_odd,
        group,
        grid=(strips,),
        in_specs=[strip(flat.shape[0])],
        out_specs=strip(rows, width),
    )(flat)

    def exchange(a):
        return lax.all_to_all(a, "spec", split_axis=0, concat_axis=0, tiled=True)

    def coupled(a):
        block = strip(species * 4)
        whole = pl.BlockSpec((species, species), lambda t: (0, 0))
        got = call(
            couple,
            sds((species * 4, ny), F32),
            grid=(strips,),
            in_specs=[block, whole],
            out_specs=block,
            scratch_shapes=[pltpu.VMEM((species, 512), F32)],
        )(a.reshape(species * 4, ny), coupling)
        return got.reshape(a.shape)

    cup, cdown = up[HALO * width :], down[HALO * width :]

    def transported(parity, a, before, after):
        vmem = pl.BlockSpec(memory_space=pltpu.VMEM)
        return call(
            functools.partial(transport, parity),
            group,
            in_specs=[vmem] * 6 + [pl.BlockSpec(memory_space=pltpu.SMEM)],
            out_specs=vmem,
            scratch_shapes=[
                pltpu.VMEM((2, 16, 8, ny), F32),
                pltpu.VMEM((14, TAPS, 8, ny), F32),
                pltpu.VMEM((14, TAPS, 8, ny), F32),
                pltpu.VMEM((14, 8, ny), F32),
            ],
        )(a, before, after, cup, cdown, speeds, valid)

    start = lax.axis_index("spec") * own_species
    mine = lax.dynamic_slice_in_dim(rates, start, own_species, 1).T
    kinds = mine.shape[1]
    mine = jnp.pad(mine[:, None], ((0, 0), (0, 3), (0, 16 - kinds))).reshape(width, 16)
    tile = sds((rows, 8, ny), F32)
    keep, weven, wodd = call(
        prepare,
        (group, tile, tile),
        grid=(strips,),
        in_specs=[
            strip(lm.shape[0]),
            strip(rows),
            strip(rows),
            pl.BlockSpec(mine.shape, lambda t: (0, 0)),
        ],
        out_specs=[strip(rows, width), strip(rows, 8), strip(rows, 8)],
    )(lm, pbl_top, land_type, mine)

    odd = exchange(odd)
    even = transported(0, even, up, down)
    even = exchange(even)
    odd = exchange(coupled(odd))
    even = exchange(coupled(even))
    up = lax.ppermute(odd[2:].reshape(-1, ny), "space", up_pairs)
    down = lax.ppermute(odd[:HALO].reshape(-1, ny), "space", down_pairs)
    odd = transported(1, odd, up, down)

    part = 24
    block = pl.BlockSpec((rows, part, 128), lambda i, t: (0, i, t))
    fixed = pl.BlockSpec((rows, 8, 128), lambda i, t: (0, 0, t))
    plane = pl.BlockSpec((rows, 128), lambda i, t: (0, t))
    updated, deposited = call(
        finish,
        (sds(flat.shape, F32), sds((own_species * rows, ny), F32)),
        grid=(width // part, strips),
        in_specs=[block, block, block, fixed, fixed, plane, plane],
        out_specs=[
            pl.BlockSpec((part * 16, 128), lambda i, t: (i, t)),
            pl.BlockSpec((part * 2, 128), lambda i, t: (i, t)),
        ],
        scratch_shapes=[pltpu.VMEM((part, 128), F32)],
    )(even, odd, keep, weven, wodd, pbl_top, lm)
    return (updated.reshape(tracers.shape), deposited.reshape(own_species, rows, ny))


def solution(mesh):
    return jax.shard_map(
        on_device,
        mesh=mesh,
        in_specs=(
            P("spec", None, "space", None),
            P(None, None, "space", None),
            P(None, "space", None),
            P("space", None),
            P("space", None),
            P(),
            P(),
        ),
        out_specs=(P("spec", None, "space", None), P("spec", "space", None)),
        check_vma=False,
    )
```

time: 187 us -> 161 us (0.86)
  the two profiles are of different devices: /device:TPU:96 before, /device:TPU:101 now
where the time goes in v1:
time: 161 us; the launch traced here: 160 us
  Pallas kernels  56.5 us (35%)
  waiting for transfers between devices  55.1 us (34%)
  starting transfers between devices  39.7 us (25%)
  local copies, waits for them, and re-layouts  7.91 us (5%)
    all_to_all x4, waiting for transfers between devices, exchange(): return lax.all_to_all(a, 'spec', split_axis=0, concat_axis=0, tiled=True)  27.5 us
    pallas_call x2, Pallas kernels, transported(): call(functools.partial(transport, parity), group, in_specs=[vmem] * 6 + [...  25.1 us
    all_to_all x4, starting transfers between devices, exchange(): return lax.all_to_all(a, 'spec', split_axis=0, concat_axis=0, tiled=True)  24.2 us
    ppermute x1, waiting for transfers between devices, on_device(): up = lax.ppermute(send_up, 'space', up_pairs)  11.8 us
    pallas_call x1, Pallas kernels, on_device(): call(finish, (sds(flat.shape, F32), sds((own_species * rows, ny), F32)),...  10.3 us
    pallas_call x2, Pallas kernels, coupled(): call(couple, sds((species * 4, ny), F32), grid=(strips,), in_specs=[block...  7.78 us
    ppermute x1, starting transfers between devices, on_device(): up = lax.ppermute(send_up, 'space', up_pairs)  5.86 us
    ppermute x1, starting transfers between devices, on_device(): up = lax.ppermute(odd[2:].reshape(-1, ny), 'space', up_pairs)  5.8 us
  transfers between devices with their start and end apart: 8, of which 6 were waited for; matrix products, arithmetic and copies ran while one was open for 3% of the time, Pallas kernels for 26%

profile of v1, /device:TPU:101, one launch (start us, length us, event | category | flops | bytes accessed | tf_op | source)
XLA Modules:
  0.0 160.0 jit_solution(5105661261505445637)
XLA Ops:
  0.6 0.0 copy-start
  0.6 3.9 %shard_map.89 = f32[8,120,384]{2,1,0:T(8,128)} custom-call(f32[1920,384]{1,0:T(8,128)} %bitcast.17), custom_call_target="tpu_custom_call" | custom-call | tf_op jit(solution)/shard_map/pallas_call | solution.py:259
  4.6 6.9 %all-to-all-start.2 = ((f32[8,120,384]{2,1,0:T(8,128)}), f32[8,120,384]{2,1,0:T(8,128)S(1)}, u32[]{:S(2)}, u32[]{:S(2)}) async-start(f32[8,120,384]{2,1,0:T(8,128)} %shard_map.89), calls=%async_computation.2 | async-start | bytes 2949120 | tf_op jit(solution)/shard_map/all_to_all | solution.py:268
  11.5 4.9 %shard_map.86 = (f32[8,120,384]{2,1,0:T(8,128)}, f32[784,384]{1,0:T(8,128)}, f32[784,384]{1,0:T(8,128)}, f32[2,2,8,8,384]{4,3,2,1,0:T(8,128)}) custom-call(f32[1920,384]{1,0:T(8,128)} %bitcast.18, f32[128,384]{1,0:T(8,128)} %bitcast.26), custom_call_target="tpu_custom_call" | custom-call | tf_op jit(solution)/shard_map/pallas_call | solution.py:245
  16.3 5.9 %collective-permute-start = (f32[784,384]{1,0:T(8,128)}, f32[784,384]{1,0:T(8,128)S(1)}, u32[]{:S(2)}, u32[]{:S(2)}) collective-permute-start(f32[784,384]{1,0:T(8,128)} %get-tuple-element.12), channel_id=1, source_target_pairs={{0,8},{8,16},{16,24},{24,32},{32,40},{40,48},{48,56},{56,64},{64,7... | collective-permute-start | bytes 3612680 | tf_op jit(solution)/shard_map/ppermute | solution.py:257
  22.2 1.9 %collective-permute-start.1 = (f32[784,384]{1,0:T(8,128)}, f32[784,384]{1,0:T(8,128)}, u32[]{:S(2)}, u32[]{:S(2)}) collective-permute-start(f32[784,384]{1,0:T(8,128)} %get-tuple-element.13), channel_id=1, source_target_pairs={{8,0},{16,8},{24,16},{32,24},{40,32},{48,40},{56,48},{64,56},{72,6... | collective-permute-start | bytes 3612680 | tf_op jit(solution)/shard_map/ppermute | solution.py:258
  24.1 11.8 %collective-permute-done.up = f32[784,384]{1,0:T(8,128)S(1)} collective-permute-done((f32[784,384]{1,0:T(8,128)}, f32[784,384]{1,0:T(8,128)S(1)}, u32[]{:S(2)}, u32[]{:S(2)}) %collective-permute-start) | collective-permute-done | bytes 1204256 | tf_op jit(solution)/shard_map/ppermute | solution.py:257
  35.9 0.0 copy-start.5
  35.9 0.7 slice.16.cup
  36.6 4.9 %collective-permute-done.1.down = f32[784,384]{1,0:T(8,128)} collective-permute-done((f32[784,384]{1,0:T(8,128)}, f32[784,384]{1,0:T(8,128)}, u32[]{:S(2)}, u32[]{:S(2)}) %collective-permute-start.1) | collective-permute-done | bytes 1204256 | tf_op jit(solution)/shard_map/ppermute | solution.py:258
  41.5 1.5 slice.17.cdown
  43.0 0.0 copy-done.5
  43.0 12.6 %shard_map.87 = f32[8,120,384]{2,1,0:T(8,128)} custom-call(f32[8,120,384]{2,1,0:T(8,128)} %get-tuple-element.11.own, f32[784,384]{1,0:T(8,128)} %copy-done.5, f32[784,384]{1,0:T(8,128)} %collective-permute-done.1.down, f32[64,384]{1,0:T(8,128)} %slice.16.cup, f32[64,384]{1,0:T(8,128)} %slice.17.cdown, f32[2,2,8,8,384]{4,3,2,1,0:T(8,128)} %get-tuple-element.14.cf, ...), custom_call_target="tpu_custom_call" | custom-call | tf_op jit(solution)/shard_map/pallas_call | solution.py:287
  55.6 0.0 all-to-all-done.2
  55.6 0.0 copy-start.2
  55.7 1.1 copy-done.2
  56.8 6.6 %all-to-all-start = ((f32[8,120,384]{2,1,0:T(8,128)}), f32[8,120,384]{2,1,0:T(8,128)S(1)}, u32[]{:S(2)}, u32[]{:S(2)}) async-start(f32[8,120,384]{2,1,0:T(8,128)} %shard_map.87), calls=%async_computation | async-start | bytes 2949120 | tf_op jit(solution)/shard_map/all_to_all | solution.py:268
  63.4 3.9 %shard_map.90 = f32[960,384]{1,0:T(8,128)} custom-call(f32[960,384]{1,0:T(8,128)} %bitcast.20, f32[240,240]{1,0:T(8,128)} %matrix.3), custom_call_target="tpu_custom_call" | custom-call | tf_op jit(solution)/shard_map/pallas_call | solution.py:273
  67.3 12.1 %all-to-all-done = f32[8,120,384]{2,1,0:T(8,128)S(1)} async-done(((f32[8,120,384]{2,1,0:T(8,128)}), f32[8,120,384]{2,1,0:T(8,128)S(1)}, u32[]{:S(2)}, u32[]{:S(2)}) %all-to-all-start) | async-done | bytes 1474592 | tf_op jit(solution)/shard_map/all_to_all | solution.py:268
  79.4 0.0 copy-start.3
  79.4 1.1 copy-done.3
  80.5 5.3 %all-to-all-start.3 = ((f32[8,120,384]{2,1,0:T(8,128)}), f32[8,120,384]{2,1,0:T(8,128)S(1)}, u32[]{:S(2)}, u32[]{:S(2)}) async-start(f32[8,120,384]{2,1,0:T(8,128)} %bitcast.22), calls=%async_computation.3 | async-start | bytes 2949120 | tf_op jit(solution)/shard_map/all_to_all | solution.py:268
  85.8 3.9 %shard_map.88 = f32[960,384]{1,0:T(8,128)} custom-call(f32[960,384]{1,0:T(8,128)} %bitcast.21, f32[240,240]{1,0:T(8,128)} %matrix.3), custom_call_target="tpu_custom_call" | custom-call | tf_op jit(solution)/shard_map/pallas_call | solution.py:273
  89.6 15.4 %all-to-all-done.3.own = f32[8,120,384]{2,1,0:T(8,128)S(1)} async-done(((f32[8,120,384]{2,1,0:T(8,128)}), f32[8,120,384]{2,1,0:T(8,128)S(1)}, u32[]{:S(2)}, u32[]{:S(2)}) %all-to-all-start.3) | async-done | bytes 1474592 | tf_op jit(solution)/shard_map/all_to_all | solution.py:268
  105.0 0.0 copy-start.1
  105.0 5.4 %all-to-all-start.1 = ((f32[8,120,384]{2,1,0:T(8,128)}), f32[8,120,384]{2,1,0:T(8,128)S(1)}, u32[]{:S(2)}, u32[]{:S(2)}) async-start(f32[8,120,384]{2,1,0:T(8,128)} %bitcast.19), calls=%async_computation.1 | async-start | bytes 2949120 | tf_op jit(solution)/shard_map/all_to_all | solution.py:268
  110.4 0.0 copy-done.1
  110.5 1.5 fusion
  111.9 5.8 %collective-permute-start.2 = (f32[720,384]{1,0:T(8,128)}, f32[720,384]{1,0:T(8,128)S(1)}, u32[]{:S(2)}, u32[]{:S(2)}) collective-permute-start(f32[720,384]{1,0:T(8,128)} %bitcast.7), channel_id=1, source_target_pairs={{0,8},{8,16},{16,24},{24,32},{32,40},{40,48},{48,56},{56,64},{64,7... | collective-permute-start | bytes 3317768 | tf_op jit(solution)/shard_map/ppermute | solution.py:323
  117.8 1.9 %collective-permute-start.3 = (f32[720,384]{1,0:T(8,128)}, f32[720,384]{1,0:T(8,128)}, u32[]{:S(2)}, u32[]{:S(2)}) collective-permute-start(f32[720,384]{1,0:T(8,128)} %bitcast.8), channel_id=1, source_target_pairs={{8,0},{16,8},{24,16},{32,24},{40,32},{48,40},{56,48},{64,56},{72,6... | collective-permute-start | bytes 3317768 | tf_op jit(solution)/shard_map/ppermute | solution.py:324
  119.7 0.0 copy-done
  119.7 0.1 dynamic-slice_bitcast_fusion
  119.8 0.1 copy.10
  119.9 0.6 pad.4.clone
  120.5 4.5 %shard_map.92 = (f32[8,120,384]{2,1,0:T(8,128)}, f32[8,8,384]{2,1,0:T(8,128)}, f32[8,8,384]{2,1,0:T(8,128)}) custom-call(f32[64,384]{1,0:T(8,128)} %bitcast.23, s32[8,384]{1,0:T(8,128)} %pbl.3, s32[8,384]{1,0:T(8,128)} %land.1, f32[120,16]{1,0:T(8,128)} %bitcast.25), custom_call_target="tpu_custom_call" | custom-call | tf_op jit(solution)/shard_map/pallas_call | solution.py:305
  125.0 5.4 %collective-permute-done.2.up = f32[720,384]{1,0:T(8,128)S(1)} collective-permute-done((f32[720,384]{1,0:T(8,128)}, f32[720,384]{1,0:T(8,128)S(1)}, u32[]{:S(2)}, u32[]{:S(2)}) %collective-permute-start.2) | collective-permute-done | bytes 1105952 | tf_op jit(solution)/shard_map/ppermute | solution.py:323
  130.4 0.0 copy-start.6
  130.4 5.6 %collective-permute-done.3.down = f32[720,384]{1,0:T(8,128)} collective-permute-done((f32[720,384]{1,0:T(8,128)}, f32[720,384]{1,0:T(8,128)}, u32[]{:S(2)}, u32[]{:S(2)}) %collective-permute-start.3) | collective-permute-done | bytes 1105952 | tf_op jit(solution)/shard_map/ppermute | solution.py:324
  136.0 0.0 copy-done.6
  136.0 12.5 %shard_map.91.odd = f32[8,120,384]{2,1,0:T(8,128)} custom-call(f32[8,120,384]{2,1,0:T(8,128)} %copy-done.1, f32[720,384]{1,0:T(8,128)} %copy-done.6, f32[720,384]{1,0:T(8,128)} %collective-permute-done.3.down, f32[64,384]{1,0:T(8,128)} %slice.16.cup, f32[64,384]{1,0:T(8,128)} %slice.17.cdown, f32[2,2,8,8,384]{4,3,2,1,0:T(8,128)} %get-tuple-element.14.cf, ...), custom_call_target="tpu_custom_call" | custom-call | tf_op jit(solution)/shard_map/pallas_call | solution.py:287
  148.6 0.0 all-to-all-done.1.even
  148.6 0.0 copy-start.4
  148.6 1.1 copy-done.4
  149.7 10.3 %shard_map.93 = (f32[1920,384]{1,0:T(8,128)}, f32[240,384]{1,0:T(8,128)}) custom-call(f32[8,120,384]{2,1,0:T(8,128)} %copy-done.4, f32[8,120,384]{2,1,0:T(8,128)} %shard_map.91.odd, f32[8,120,384]{2,1,0:T(8,128)} %get-tuple-element.15.keep, f32[8,8,384]{2,1,0:T(8,128)} %get-tuple-element.16.weven, f32[8,8,384]{2,1,0:T(8,128)} %get-tuple-element.17.wodd, ...), custom_call_target="tpu_custom_call" | custom-call | tf_op jit(solution)/shard_map/pallas_call | solution.py:331
Async XLA Ops:
  0.6 119.1 %copy-start = (f32[11,240]{1,0:T(8,128)S(1)}, f32[11,240]{1,0:T(8,128)}, u32[]{:S(2)}) copy-start(f32[11,240]{1,0:T(8,128)} %param.12) | copy-start | bytes 31684
  4.6 51.1 %all-to-all-start.2 = ((f32[8,120,384]{2,1,0:T(8,128)}), f32[8,120,384]{2,1,0:T(8,128)S(1)}, u32[]{:S(2)}, u32[]{:S(2)}) async-start(f32[8,120,384]{2,1,0:T(8,128)} %shard_map.89), calls=%async_computation.2 | async-start | bytes 2949120 | tf_op jit(solution)/shard_map/all_to_all | solution.py:268
  16.3 19.6 %collective-permute-start = (f32[784,384]{1,0:T(8,128)}, f32[784,384]{1,0:T(8,128)S(1)}, u32[]{:S(2)}, u32[]{:S(2)}) collective-permute-start(f32[784,384]{1,0:T(8,128)} %get-tuple-element.12), channel_id=1, source_target_pairs={{0,8},{8,16},{16,24},{24,32},{32,40},{40,48},{48,56},{56,64},{64,7... | collective-permute-start | bytes 3612680 | tf_op jit(solution)/shard_map/ppermute | solution.py:257
  22.2 19.3 %collective-permute-start.1 = (f32[784,384]{1,0:T(8,128)}, f32[784,384]{1,0:T(8,128)}, u32[]{:S(2)}, u32[]{:S(2)}) collective-permute-start(f32[784,384]{1,0:T(8,128)} %get-tuple-element.13), channel_id=1, source_target_pairs={{8,0},{16,8},{24,16},{32,24},{40,32},{48,40},{56,48},{64,56},{72,6... | collective-permute-start | bytes 3612680 | tf_op jit(solution)/shard_map/ppermute | solution.py:258
  35.9 7.1 %copy-start.5 = (f32[784,384]{1,0:T(8,128)}, f32[784,384]{1,0:T(8,128)S(1)}, u32[]{:S(2)}) copy-start(f32[784,384]{1,0:T(8,128)S(1)} %collective-permute-done.up) | copy-start | bytes 3612676
  55.6 1.1 copy-start.2
  56.8 22.6 %all-to-all-start = ((f32[8,120,384]{2,1,0:T(8,128)}), f32[8,120,384]{2,1,0:T(8,128)S(1)}, u32[]{:S(2)}, u32[]{:S(2)}) async-start(f32[8,120,384]{2,1,0:T(8,128)} %shard_map.87), calls=%async_computation | async-start | bytes 2949120 | tf_op jit(solution)/shard_map/all_to_all | solution.py:268
  79.4 1.1 copy-start.3
  80.5 24.5 %all-to-all-start.3 = ((f32[8,120,384]{2,1,0:T(8,128)}), f32[8,120,384]{2,1,0:T(8,128)S(1)}, u32[]{:S(2)}, u32[]{:S(2)}) async-start(f32[8,120,384]{2,1,0:T(8,128)} %bitcast.22), calls=%async_computation.3 | async-start | bytes 2949120 | tf_op jit(solution)/shard_map/all_to_all | solution.py:268
  105.0 5.4 %copy-start.1 = (f32[8,120,384]{2,1,0:T(8,128)}, f32[8,120,384]{2,1,0:T(8,128)S(1)}, u32[]{:S(2)}) copy-start(f32[8,120,384]{2,1,0:T(8,128)S(1)} %all-to-all-done.3.own) | copy-start | bytes 4423684
  105.0 43.5 %all-to-all-start.1 = ((f32[8,120,384]{2,1,0:T(8,128)}), f32[8,120,384]{2,1,0:T(8,128)S(1)}, u32[]{:S(2)}, u32[]{:S(2)}) async-start(f32[8,120,384]{2,1,0:T(8,128)} %bitcast.19), calls=%async_computation.1 | async-start | bytes 2949120 | tf_op jit(solution)/shard_map/all_to_all | solution.py:268
  111.9 18.5 %collective-permute-start.2 = (f32[720,384]{1,0:T(8,128)}, f32[720,384]{1,0:T(8,128)S(1)}, u32[]{:S(2)}, u32[]{:S(2)}) collective-permute-start(f32[720,384]{1,0:T(8,128)} %bitcast.7), channel_id=1, source_target_pairs={{0,8},{8,16},{16,24},{24,32},{32,40},{40,48},{48,56},{56,64},{64,7... | collective-permute-start | bytes 3317768 | tf_op jit(solution)/shard_map/ppermute | solution.py:323
  117.8 18.3 %collective-permute-start.3 = (f32[720,384]{1,0:T(8,128)}, f32[720,384]{1,0:T(8,128)}, u32[]{:S(2)}, u32[]{:S(2)}) collective-permute-start(f32[720,384]{1,0:T(8,128)} %bitcast.8), channel_id=1, source_target_pairs={{8,0},{16,8},{24,16},{32,24},{40,32},{48,40},{56,48},{64,56},{72,6... | collective-permute-start | bytes 3317768 | tf_op jit(solution)/shard_map/ppermute | solution.py:324
  130.4 5.6 %copy-start.6 = (f32[720,384]{1,0:T(8,128)}, f32[720,384]{1,0:T(8,128)S(1)}, u32[]{:S(2)}) copy-start(f32[720,384]{1,0:T(8,128)S(1)} %collective-permute-done.2.up) | copy-start | bytes 3317764
  148.6 1.1 copy-start.4

commit v2 on v1

--- a/solution.py
+++ b/solution.py
@@ -19,11 +19,11 @@
 
 
 def pack_even(x, cf, own, up, down, speeds):
-    tiles = own.shape[1] // 8
     width = own.shape[1]
+    x = x.reshape(width * 8, 128)
     for r in range(8):
-        for i in range(tiles):
-            value = x[pl.ds(i * 128 + r, 8, stride=16), :]
+        for i in range(width // 8):
+            value = x[pl.ds(i * 64 + r, 8, stride=8), :]
             own[r, i * 8 : i * 8 + 8, :] = value
             if r >= 2:
                 at = (r - 2) * width + i * 8
@@ -46,9 +46,10 @@
 
 
 def pack_odd(x, own):
+    x = x.reshape(own.shape[1] * 8, 128)
     for r in range(8):
         for i in range(own.shape[1] // 8):
-            own[r, i * 8 : i * 8 + 8, :] = x[pl.ds(i * 128 + 8 + r, 8, stride=16), :]
+            own[r, i * 8 : i * 8 + 8, :] = x[pl.ds(i * 64 + r, 8, stride=8), :]
 
 
 def flux_taps(c):
@@ -86,8 +87,8 @@
 
 
 def transport(parity, own, up, down, cup, cdown, cf, valid, out, c, wx, wy, mid):
-    width = own.shape[1]
-    ny = own.shape[2]
+    width = own.shape[2]
+    ny = own.shape[3]
     for d in range(2):
         c[d, 4:12] = cf[parity, d]
         for row in range(4):
@@ -117,41 +118,54 @@
 
     lax.fori_loop(0, 14, y_weights, 0)
 
-    def across(value, row):
-        total = wy[row, 3] * value
+    group = range(3)
+
+    def across(values, row):
+        w = wy[row, 3]
+        totals = [w * v for v in values]
         for shift in (1, 2, 3):
-            total += wy[row, 3 + shift] * pltpu.roll(value, ny - shift, 1)
-            total += wy[row, 3 - shift] * pltpu.roll(value, shift, 1)
-        return total
+            w = wy[row, 3 + shift]
+            totals = [t + w * pltpu.roll(v, ny - shift, 1) for t, v in zip(totals, values)]
+            w = wy[row, 3 - shift]
+            totals = [t + w * pltpu.roll(v, shift, 1) for t, v in zip(totals, values)]
+        return totals
 
     def tile(i, carry):
-        at = pl.multiple_of(i * 8, 8)
-
-        def first(row, cols):
+        places = [pl.multiple_of(i * 24 + 8 * u, 8) for u in group]
+
+        def first(row, cols, u):
+            at = places[u]
             if row < 0:
                 return up[pl.ds((row + HALO) * width + at, 8), cols]
             if row < 8:
-                return own[row, pl.ds(at, 8), cols]
+                return own[row, 0, pl.ds(at, 8), cols]
             return down[pl.ds((row - 8) * width + at, 8), cols]
 
+        def second(row, cols, u):
+            return mid[row + 3, u, :, cols]
+
         def along(read, row):
-            parts = []
+            parts = [[] for _ in group]
             for t in range(ny // 128):
                 cols = slice(t * 128, t * 128 + 128)
-                total = wx[row + 3, 0, :, cols] * read(row - 3, cols)
+                w = wx[row + 3, 0, :, cols]
+                totals = [w * read(row - 3, cols, u) for u in group]
                 for k in range(1, TAPS):
-                    total += wx[row + 3, k, :, cols] * read(row + k - 3, cols)
-                parts.append(total)
-            return jnp.concatenate(parts, axis=1)
+                    w = wx[row + 3, k, :, cols]
+                    totals = [v + w * read(row + k - 3, cols, u) for u, v in enumerate(totals)]
+                for part, v in zip(parts, totals):
+                    part.append(v)
+            return [jnp.concatenate(part, axis=1) for part in parts]
 
         for row in range(-3, 11):
-            mid[row + 3] = across(along(first, row), row + 3)
+            for u, v in enumerate(across(along(first, row), row + 3)):
+                mid[row + 3, u] = v
         for row in range(8):
-            value = along(lambda at_row, cols: mid[at_row + 3, :, cols], row)
-            out[row, pl.ds(at, 8), :] = across(value, row + 3)
+            for u, v in enumerate(across(along(second, row), row + 3)):
+                out[row, 0, pl.ds(places[u], 8), :] = v
         return carry
 
-    lax.fori_loop(0, width // 8, tile, 0)
+    lax.fori_loop(0, width // 24, tile, 0)
 
 
 def halves(value):
@@ -159,8 +173,11 @@
     return top, (value - top.astype(F32)).astype(BF16)
 
 
-def couple(x, matrix, out, wide):
+def couple(x, matrix, *refs):
+    out, wide = refs[-2:]
     species = matrix.shape[0]
+    x = x.reshape(species * 4, 128)
+    out = out.reshape(species * 4, 128)
     for j in range(4):
         wide[:, j * 128 : j * 128 + 128] = x[pl.ds(j, species, stride=4), :]
     value = wide[...]
@@ -229,7 +246,7 @@
     n_space, n_spec = lax.axis_size("space"), lax.axis_size("spec")
     up_pairs = [(i, i + 1) for i in range(n_space - 1)]
     down_pairs = [(j, i) for i, j in up_pairs]
-    flat = tracers.reshape(-1, ny)
+    split = tracers.reshape(own_species, 4, 2, rows, ny)
     cf = courant.reshape(-1, ny)
     lm = layer_mass.reshape(-1, ny)
     valid = (lax.axis_index("space") > 0).astype(F32).reshape(1, 1)
@@ -242,58 +259,74 @@
     def strip(*shape):
         return pl.BlockSpec((*shape, 128), lambda t: (0,) * len(shape) + (t,))
 
+    def level_group(parity):
+        shape = (own_species, 4, 1, rows, 128)
+        return pl.BlockSpec(shape, lambda t: (0, 0, parity, 0, t))
+
     even, send_up, send_down, speeds = call(
         pack_even,
         (group, edge, edge, speeds),
         grid=(strips,),
-        in_specs=[strip(flat.shape[0]), strip(cf.shape[0])],
+        in_specs=[level_group(0), strip(cf.shape[0])],
         out_specs=[
             strip(rows, width),
             strip(edge.shape[0]),
             strip(edge.shape[0]),
             strip(2, 2, rows, 8),
         ],
-    )(flat, cf)
+    )(split, cf)
     up = lax.ppermute(send_up, "space", up_pairs)
     down = lax.ppermute(send_down, "space", down_pairs)
     odd = call(
         pack_odd,
         group,
         grid=(strips,),
-        in_specs=[strip(flat.shape[0])],
+        in_specs=[level_group(1)],
         out_specs=strip(rows, width),
-    )(flat)
+    )(split)
 
     def exchange(a):
         return lax.all_to_all(a, "spec", split_axis=0, concat_axis=0, tiled=True)
 
-    def coupled(a):
-        block = strip(species * 4)
+    pair = sds((rows, 2, width, ny), F32)
+
+    def half(index):
+        return pl.BlockSpec((rows, 1, width, 128), lambda t: (0, index, 0, t))
+
+    def coupled(a, index, shape, out_index, *into):
         whole = pl.BlockSpec((species, species), lambda t: (0, 0))
-        got = call(
+        return call(
             couple,
-            sds((species * 4, ny), F32),
+            shape,
             grid=(strips,),
-            in_specs=[block, whole],
-            out_specs=block,
+            in_specs=[half(index), whole] + [pl.BlockSpec(memory_space=pl.ANY)] * len(into),
+            out_specs=half(out_index),
             scratch_shapes=[pltpu.VMEM((species, 512), F32)],
-        )(a.reshape(species * 4, ny), coupling)
-        return got.reshape(a.shape)
+            input_output_aliases={2: 0} if into else {},
+        )(a, coupling, *into)
 
     cup, cdown = up[HALO * width :], down[HALO * width :]
 
-    def transported(parity, a, before, after):
-        vmem = pl.BlockSpec(memory_space=pltpu.VMEM)
+    def transported(parity, a, index, shape, before, after):
+        def plane(i):
+            return pl.BlockSpec((rows, 1, width, ny), lambda t: (0, i, 0, 0))
+
+        def whole(array):
+            return pl.BlockSpec(array.shape, lambda t: (0,) * array.ndim)
+
         return call(
             functools.partial(transport, parity),
-            group,
-            in_specs=[vmem] * 6 + [pl.BlockSpec(memory_space=pltpu.SMEM)],
-            out_specs=vmem,
+            shape,
+            grid=(1,),
+            in_specs=[plane(index)]
+            + [whole(v) for v in (before, after, cup, cdown, speeds)]
+            + [pl.BlockSpec(memory_space=pltpu.SMEM)],
+            out_specs=plane(0),
             scratch_shapes=[
                 pltpu.VMEM((2, 16, 8, ny), F32),
                 pltpu.VMEM((14, TAPS, 8, ny), F32),
                 pltpu.VMEM((14, TAPS, 8, ny), F32),
-                pltpu.VMEM((14, 8, ny), F32),
+                pltpu.VMEM((14, 3, 8, ny), F32),
             ],
         )(a, before, after, cup, cdown, speeds, valid)
 
@@ -315,29 +348,23 @@
         out_specs=[strip(rows, width), strip(rows, 8), strip(rows, 8)],
     )(lm, pbl_top, land_type, mine)
 
+    single = sds((rows, 1, width, ny), F32)
     odd = exchange(odd)
-    even = transported(0, even, up, down)
-    even = exchange(even)
-    odd = exchange(coupled(odd))
-    even = exchange(coupled(even))
-    up = lax.ppermute(odd[2:].reshape(-1, ny), "space", up_pairs)
-    down = lax.ppermute(odd[:HALO].reshape(-1, ny), "space", down_pairs)
-    odd = transported(1, odd, up, down)
-
-    part = 24
-    block = pl.BlockSpec((rows, part, 128), lambda i, t: (0, i, t))
-    fixed = pl.BlockSpec((rows, 8, 128), lambda i, t: (0, 0, t))
-    plane = pl.BlockSpec((rows, 128), lambda i, t: (0, t))
+    both = transported(0, even[:, None], 0, pair, up, down)
+    both = coupled(odd[:, None], 0, pair, 1, both)
+    both = exchange(both)
+    even = exchange(coupled(both, 0, single, 0))[:, 0]
+    up = lax.ppermute(both[2:, 1].reshape(-1, ny), "space", up_pairs)
+    down = lax.ppermute(both[:HALO, 1].reshape(-1, ny), "space", down_pairs)
+    odd = transported(1, both, 1, single, up, down)[:, 0]
+
     updated, deposited = call(
         finish,
-        (sds(flat.shape, F32), sds((own_species * rows, ny), F32)),
-        grid=(width // part, strips),
-        in_specs=[block, block, block, fixed, fixed, plane, plane],
-        out_specs=[
-            pl.BlockSpec((part * 16, 128), lambda i, t: (i, t)),
-            pl.BlockSpec((part * 2, 128), lambda i, t: (i, t)),
-        ],
-        scratch_shapes=[pltpu.VMEM((part, 128), F32)],
+        (sds((tracers.size // ny, ny), F32), sds((own_species * rows, ny), F32)),
+        grid=(strips,),
+        in_specs=[strip(rows, width)] * 3 + [strip(rows, 8)] * 2 + [strip(rows)] * 2,
+        out_specs=[strip(tracers.size // ny), strip(own_species * rows)],
+        scratch_shapes=[pltpu.VMEM((width, 128), F32)],
     )(even, odd, keep, weven, wodd, pbl_top, lm)
     return (updated.reshape(tracers.shape), deposited.reshape(own_species, rows, ny))
 

time: 161 us -> 154 us (0.957)
  blocking collectives: 0 us -> 38.6 us
  waiting for transfers between devices: 55.1 us -> 27.5 us
  starting transfers between devices: 39.7 us -> 29.4 us
  Pallas kernels: 56.5 us -> 50.1 us
    all_to_all x0 -> x1, blocking collectives: none -> 38.6 us  [exchange(): return lax.all_to_all(a, 'spec', split_axis=0, concat_axis=0, tiled=True)]
    all_to_all x4 -> x2, waiting for transfers between devices: 27.5 us -> 0.01 us  [exchange(): return lax.all_to_all(a, 'spec', split_axis=0, concat_axis=0, tiled=True)]
    all_to_all x4 -> x2, starting transfers between devices: 24.2 us -> 14 us  [exchange(): return lax.all_to_all(a, 'spec', split_axis=0, concat_axis=0, tiled=True)]
    pallas_call x7, Pallas kernels: 52 us -> 45.5 us  [the longest x2 24.9 us: transported(): call(functools.partial(transport, parity), shape, grid=(1,), in_specs=[pl...]
    unnamed x15 -> x13, local copies, waits for them, and re-layouts: 3.48 us -> 2.33 us
  transfers between devices with their start and end apart: 8 -> 6, of which waited for: 6 -> 4; matrix products, arithmetic and copies ran while one was open for 3% -> 3% of each run, Pallas kernels for 26% -> 22%
where the time goes in v2:
time: 154 us; the launch traced here: 153 us
  Pallas kernels  50.1 us (33%)
  blocking collectives  38.6 us (25%)
  starting transfers between devices  29.4 us (19%)
  waiting for transfers between devices  27.5 us (18%)
  local copies, waits for them, and re-layouts  6.79 us (4%)
    all_to_all x1, blocking collectives, exchange(): return lax.all_to_all(a, 'spec', split_axis=0, concat_axis=0, tiled=True)  38.6 us
    pallas_call x2, Pallas kernels, transported(): call(functools.partial(transport, parity), shape, grid=(1,), in_specs=[pl...  24.9 us
    all_to_all x2, starting transfers between devices, exchange(): return lax.all_to_all(a, 'spec', split_axis=0, concat_axis=0, tiled=True)  14 us
    ppermute x1, waiting for transfers between devices, on_device(): up = lax.ppermute(send_up, 'space', up_pairs)  11.8 us
    pallas_call x2, Pallas kernels, coupled(): call(couple, shape, grid=(strips,), in_specs=[half(index), whole] + [pl.B...  7.73 us
    ppermute x1, starting transfers between devices, on_device(): up = lax.ppermute(send_up, 'space', up_pairs)  5.86 us
    ppermute x1, starting transfers between devices, on_device(): up = lax.ppermute(both[2:, 1].reshape(-1, ny), 'space', up_pairs)  5.64 us
    ppermute x1, waiting for transfers between devices, on_device(): down = lax.ppermute(both[:HALO, 1].reshape(-1, ny), 'space', down_pairs)  5.5 us
  transfers between devices with their start and end apart: 6, of which 4 were waited for; matrix products, arithmetic and copies ran while one was open for 3% of the time, Pallas kernels for 22%

profile of v2, /device:TPU:101, one launch (start us, length us, event | category | flops | bytes accessed | tf_op | source)
XLA Modules:
  0.0 153.1 jit_solution(7490280471914678652)
XLA Ops:
  0.6 0.0 copy-start
  0.6 3.5 %shard_map.86 = f32[8,120,384]{2,1,0:T(8,128)} custom-call(f32[30,4,2,8,384]{4,3,2,1,0:T(8,128)} %bitcast.17), custom_call_target="tpu_custom_call" | custom-call | tf_op jit(solution)/shard_map/pallas_call | solution.py:280
  4.1 6.9 %all-to-all-start = ((f32[8,120,384]{2,1,0:T(8,128)}), f32[8,120,384]{2,1,0:T(8,128)S(1)}, u32[]{:S(2)}, u32[]{:S(2)}) async-start(f32[8,120,384]{2,1,0:T(8,128)} %shard_map.86), calls=%async_computation | async-start | bytes 2949120 | tf_op jit(solution)/shard_map/all_to_all | solution.py:289
  11.0 3.9 %shard_map.87 = (f32[8,120,384]{2,1,0:T(8,128)}, f32[784,384]{1,0:T(8,128)}, f32[784,384]{1,0:T(8,128)}, f32[2,2,8,8,384]{4,3,2,1,0:T(8,128)}) custom-call(f32[30,4,2,8,384]{4,3,2,1,0:T(8,128)} %bitcast.18, f32[128,384]{1,0:T(8,128)} %bitcast.25), custom_call_target="tpu_custom_call" | custom-call | tf_op jit(solution)/shard_map/pallas_call | solution.py:266
  15.0 5.9 %collective-permute-start = (f32[784,384]{1,0:T(8,128)}, f32[784,384]{1,0:T(8,128)S(1)}, u32[]{:S(2)}, u32[]{:S(2)}) collective-permute-start(f32[784,384]{1,0:T(8,128)} %get-tuple-element.12), channel_id=1, source_target_pairs={{0,8},{8,16},{16,24},{24,32},{32,40},{40,48},{48,56},{56,64},{64,7... | collective-permute-start | bytes 3612680 | tf_op jit(solution)/shard_map/ppermute | solution.py:278
  20.8 1.9 %collective-permute-start.1 = (f32[784,384]{1,0:T(8,128)}, f32[784,384]{1,0:T(8,128)}, u32[]{:S(2)}, u32[]{:S(2)}) collective-permute-start(f32[784,384]{1,0:T(8,128)} %get-tuple-element.13), channel_id=1, source_target_pairs={{8,0},{16,8},{24,16},{32,24},{40,32},{48,40},{56,48},{64,56},{72,6... | collective-permute-start | bytes 3612680 | tf_op jit(solution)/shard_map/ppermute | solution.py:279
  22.8 11.8 %collective-permute-done.up = f32[784,384]{1,0:T(8,128)S(1)} collective-permute-done((f32[784,384]{1,0:T(8,128)}, f32[784,384]{1,0:T(8,128)S(1)}, u32[]{:S(2)}, u32[]{:S(2)}) %collective-permute-start) | collective-permute-done | bytes 1204256 | tf_op jit(solution)/shard_map/ppermute | solution.py:278
  34.5 0.0 copy-start.3
  34.5 0.7 slice.16.cup
  35.2 4.9 %collective-permute-done.1.down = f32[784,384]{1,0:T(8,128)} collective-permute-done((f32[784,384]{1,0:T(8,128)}, f32[784,384]{1,0:T(8,128)}, u32[]{:S(2)}, u32[]{:S(2)}) %collective-permute-start.1) | collective-permute-done | bytes 1204256 | tf_op jit(solution)/shard_map/ppermute | solution.py:279
  40.1 1.5 %slice.17.cdown = f32[64,384]{1,0:T(8,128)} slice(f32[784,384]{1,0:T(8,128)} %collective-permute-done.1.down), slice={[720:784], [0:384]} | slice | bytes 196608 | tf_op jit(solution)/shard_map/slice | solution.py:308
  41.7 0.0 copy-done.3
  41.7 12.5 %shard_map.88.refs_0_ = f32[8,2,120,384]{3,2,1,0:T(8,128)} custom-call(f32[8,1,120,384]{3,2,1,0:T(8,128)} %bitcast.21, f32[784,384]{1,0:T(8,128)} %copy-done.3, f32[784,384]{1,0:T(8,128)} %collective-permute-done.1.down, f32[64,384]{1,0:T(8,128)} %slice.16.cup, f32[64,384]{1,0:T(8,128)} %slice.17.cdown, f32[2,2,8,8,384]{4,3,2,1,0:T(8,128)} %get-tuple-element.14.cf, ...), custom_call_target="tpu_custom_call" | custom-call | tf_op jit(solution)/shard_map/pallas_call | solution.py:317
  54.1 0.0 all-to-all-done
  54.1 0.0 copy-start.2
  54.1 1.1 copy-done.2
  55.3 3.9 %shard_map.89 = f32[8,2,120,384]{3,2,1,0:T(8,128)} custom-call(f32[8,1,120,384]{3,2,1,0:T(8,128)} %bitcast.20, f32[240,240]{1,0:T(8,128)} %matrix.3, f32[8,2,120,384]{3,2,1,0:T(8,128)} %shard_map.88.refs_0_), custom_call_target="tpu_custom_call", output_to_operand_aliasing={{}: (2, {})} | custom-call | tf_op jit(solution)/shard_map/pallas_call | solution.py:298
  59.1 38.6 %all_to_all.15.x.own = f32[8,2,120,384]{3,2,1,0:T(8,128)} all-to-all(f32[8,2,120,384]{3,2,1,0:T(8,128)} %shard_map.89), channel_id=1, replica_groups=mesh['space'=32,'spec'=8] {'spec'}, dimensions={0} | all-to-all | bytes 5898240 | tf_op jit(solution)/shard_map/all_to_all | solution.py:289
  97.8 3.9 %shard_map.90 = f32[8,1,120,384]{3,2,1,0:T(8,128)} custom-call(f32[8,2,120,384]{3,2,1,0:T(8,128)} %all_to_all.15.x.own, f32[240,240]{1,0:T(8,128)} %matrix.3), custom_call_target="tpu_custom_call" | custom-call | tf_op jit(solution)/shard_map/pallas_call | solution.py:298
  101.6 0.0 copy-start.1
  101.6 7.1 %all-to-all-start.2 = ((f32[8,1,120,384]{3,2,1,0:T(8,128)}), f32[8,1,120,384]{3,2,1,0:T(8,128)}, u32[]{:S(2)}, u32[]{:S(2)}) async-start(f32[8,1,120,384]{3,2,1,0:T(8,128)} %shard_map.90), calls=%async_computation.2 | async-start | bytes 2949120 | tf_op jit(solution)/shard_map/all_to_all | solution.py:289
  108.8 0.0 copy-done.1
  108.8 1.5 fusion
  110.3 5.6 %collective-permute-start.2 = (f32[720,384]{1,0:T(8,128)}, f32[720,384]{1,0:T(8,128)S(1)}, u32[]{:S(2)}, u32[]{:S(2)}) collective-permute-start(f32[720,384]{1,0:T(8,128)} %bitcast.6), channel_id=1, source_target_pairs={{0,8},{8,16},{16,24},{24,32},{32,40},{40,48},{48,56},{56,64},{64,7... | collective-permute-start | bytes 3317768 | tf_op jit(solution)/shard_map/ppermute | solution.py:357
  115.9 1.9 %collective-permute-start.3 = (f32[720,384]{1,0:T(8,128)}, f32[720,384]{1,0:T(8,128)S(1)}, u32[]{:S(2)}, u32[]{:S(2)}) collective-permute-start(f32[720,384]{1,0:T(8,128)} %bitcast.7), channel_id=1, source_target_pairs={{8,0},{16,8},{24,16},{32,24},{40,32},{48,40},{56,48},{64,56},{72,6... | collective-permute-start | bytes 3317768 | tf_op jit(solution)/shard_map/ppermute | solution.py:358
  117.9 0.0 copy-done
  117.9 0.1 dynamic-slice_bitcast_fusion
  118.0 0.1 copy.13
  118.1 0.6 pad.4.clone
  118.7 4.6 %shard_map.92 = (f32[8,120,384]{2,1,0:T(8,128)}, f32[8,8,384]{2,1,0:T(8,128)}, f32[8,8,384]{2,1,0:T(8,128)}) custom-call(f32[64,384]{1,0:T(8,128)} %bitcast.22, s32[8,384]{1,0:T(8,128)} %pbl.3, s32[8,384]{1,0:T(8,128)} %land.1, f32[120,16]{1,0:T(8,128)} %bitcast.24), custom_call_target="tpu_custom_call" | custom-call | tf_op jit(solution)/shard_map/pallas_call | solution.py:338
  123.3 5.3 %collective-permute-done.2.up = f32[720,384]{1,0:T(8,128)S(1)} collective-permute-done((f32[720,384]{1,0:T(8,128)}, f32[720,384]{1,0:T(8,128)S(1)}, u32[]{:S(2)}, u32[]{:S(2)}) %collective-permute-start.2) | collective-permute-done | bytes 1105952 | tf_op jit(solution)/shard_map/ppermute | solution.py:357
  128.6 0.0 copy-start.4
  128.6 5.5 %collective-permute-done.3.down = f32[720,384]{1,0:T(8,128)S(1)} collective-permute-done((f32[720,384]{1,0:T(8,128)}, f32[720,384]{1,0:T(8,128)S(1)}, u32[]{:S(2)}, u32[]{:S(2)}) %collective-permute-start.3) | collective-permute-done | bytes 1105952 | tf_op jit(solution)/shard_map/ppermute | solution.py:358
  134.1 0.0 copy-done.4
  134.1 0.0 copy-start.5
  134.1 1.1 copy-done.5
  135.2 12.4 %shard_map.91 = f32[8,1,120,384]{3,2,1,0:T(8,128)} custom-call(f32[8,2,120,384]{3,2,1,0:T(8,128)} %all_to_all.15.x.own, f32[720,384]{1,0:T(8,128)} %copy-done.4, f32[720,384]{1,0:T(8,128)} %copy-done.5, f32[64,384]{1,0:T(8,128)} %slice.16.cup, f32[64,384]{1,0:T(8,128)} %slice.17.cdown, f32[2,2,8,8,384]{4,3,2,1,0:T(8,128)} %get-tuple-element.14.cf, ...), custom_call_target="tpu_custom_call" | custom-call | tf_op jit(solution)/shard_map/pallas_call | solution.py:317
  147.6 0.0 all-to-all-done.2
  147.6 5.5 %shard_map.93 = (f32[1920,384]{1,0:T(8,128)}, f32[240,384]{1,0:T(8,128)}) custom-call(f32[8,120,384]{2,1,0:T(8,128)} %bitcast.5.even, f32[8,120,384]{2,1,0:T(8,128)} %bitcast.19, f32[8,120,384]{2,1,0:T(8,128)} %get-tuple-element.15.keep, f32[8,8,384]{2,1,0:T(8,128)} %get-tuple-element.16.weven, f32[8,8,384]{2,1,0:T(8,128)} %get-tuple-element.17.wodd, ...), custom_call_target="tpu_custom_call" | custom-call | tf_op jit(solution)/shard_map/pallas_call | solution.py:361
Async XLA Ops:
  0.6 117.2 %copy-start = (f32[11,240]{1,0:T(8,128)S(1)}, f32[11,240]{1,0:T(8,128)}, u32[]{:S(2)}) copy-start(f32[11,240]{1,0:T(8,128)} %param.12) | copy-start | bytes 31684
  4.1 50.0 %all-to-all-start = ((f32[8,120,384]{2,1,0:T(8,128)}), f32[8,120,384]{2,1,0:T(8,128)S(1)}, u32[]{:S(2)}, u32[]{:S(2)}) async-start(f32[8,120,384]{2,1,0:T(8,128)} %shard_map.86), calls=%async_computation | async-start | bytes 2949120 | tf_op jit(solution)/shard_map/all_to_all | solution.py:289
  15.0 19.6 %collective-permute-start = (f32[784,384]{1,0:T(8,128)}, f32[784,384]{1,0:T(8,128)S(1)}, u32[]{:S(2)}, u32[]{:S(2)}) collective-permute-start(f32[784,384]{1,0:T(8,128)} %get-tuple-element.12), channel_id=1, source_target_pairs={{0,8},{8,16},{16,24},{24,32},{32,40},{40,48},{48,56},{56,64},{64,7... | collective-permute-start | bytes 3612680 | tf_op jit(solution)/shard_map/ppermute | solution.py:278
  20.8 19.3 %collective-permute-start.1 = (f32[784,384]{1,0:T(8,128)}, f32[784,384]{1,0:T(8,128)}, u32[]{:S(2)}, u32[]{:S(2)}) collective-permute-start(f32[784,384]{1,0:T(8,128)} %get-tuple-element.13), channel_id=1, source_target_pairs={{8,0},{16,8},{24,16},{32,24},{40,32},{48,40},{56,48},{64,56},{72,6... | collective-permute-start | bytes 3612680 | tf_op jit(solution)/shard_map/ppermute | solution.py:279
  34.5 7.1 %copy-start.3 = (f32[784,384]{1,0:T(8,128)}, f32[784,384]{1,0:T(8,128)S(1)}, u32[]{:S(2)}) copy-start(f32[784,384]{1,0:T(8,128)S(1)} %collective-permute-done.up) | copy-start | bytes 3612676
  54.1 1.1 copy-start.2
  101.6 7.1 %copy-start.1 = (f32[8,2,120,384]{3,2,1,0:T(8,128)S(1)}, f32[8,2,120,384]{3,2,1,0:T(8,128)}, u32[]{:S(2)}) copy-start(f32[8,2,120,384]{3,2,1,0:T(8,128)} %all_to_all.15.x.own) | copy-start | bytes 8847364
  101.6 46.0 %all-to-all-start.2 = ((f32[8,1,120,384]{3,2,1,0:T(8,128)}), f32[8,1,120,384]{3,2,1,0:T(8,128)}, u32[]{:S(2)}, u32[]{:S(2)}) async-start(f32[8,1,120,384]{3,2,1,0:T(8,128)} %shard_map.90), calls=%async_computation.2 | async-start | bytes 2949120 | tf_op jit(solution)/shard_map/all_to_all | solution.py:289
  110.3 18.3 %collective-permute-start.2 = (f32[720,384]{1,0:T(8,128)}, f32[720,384]{1,0:T(8,128)S(1)}, u32[]{:S(2)}, u32[]{:S(2)}) collective-permute-start(f32[720,384]{1,0:T(8,128)} %bitcast.6), channel_id=1, source_target_pairs={{0,8},{8,16},{16,24},{24,32},{32,40},{40,48},{48,56},{56,64},{64,7... | collective-permute-start | bytes 3317768 | tf_op jit(solution)/shard_map/ppermute | solution.py:357
  115.9 18.2 %collective-permute-start.3 = (f32[720,384]{1,0:T(8,128)}, f32[720,384]{1,0:T(8,128)S(1)}, u32[]{:S(2)}, u32[]{:S(2)}) collective-permute-start(f32[720,384]{1,0:T(8,128)} %bitcast.7), channel_id=1, source_target_pairs={{8,0},{16,8},{24,16},{32,24},{40,32},{48,40},{56,48},{64,56},{72,6... | collective-permute-start | bytes 3317768 | tf_op jit(solution)/shard_map/ppermute | solution.py:358
  128.6 5.5 %copy-start.4 = (f32[720,384]{1,0:T(8,128)}, f32[720,384]{1,0:T(8,128)S(1)}, u32[]{:S(2)}) copy-start(f32[720,384]{1,0:T(8,128)S(1)} %collective-permute-done.2.up) | copy-start | bytes 3317764
  134.1 1.1 copy-start.5

commit v3 on v2

--- a/solution.py
+++ b/solution.py
@@ -6,6 +6,7 @@
 from jax.experimental import pallas as pl
 from jax.experimental.pallas import tpu as pltpu
 from jax.sharding import PartitionSpec as P
+
 
 INTERPRET = False
 F32 = jnp.float32
@@ -86,27 +87,41 @@
     )
 
 
-def transport(parity, own, up, down, cup, cdown, cf, valid, out, c, wx, wy, mid):
+def transport(
+    parity, index, own, up, down, cup, cdown, cf, valid, out, q, c, ends, wx, wy, mid, new, sems
+):
     width = own.shape[2]
     ny = own.shape[3]
+    group = 24
+    strip = HALO * width
+    moves = [
+        pltpu.make_async_copy(cf.at[parity], c.at[:, pl.ds(4, 8)], sems.at[0]),
+        pltpu.make_async_copy(cup.at[pl.ds(strip, 64)], ends.at[0], sems.at[1]),
+        pltpu.make_async_copy(cdown.at[pl.ds(strip, 64)], ends.at[1], sems.at[2]),
+        pltpu.make_async_copy(up.at[pl.ds(0, strip)], q.at[pl.ds(0, strip)], sems.at[3]),
+        pltpu.make_async_copy(down.at[pl.ds(0, strip)], q.at[pl.ds(strip + 8 * width, strip)], sems.at[4]),
+    ]
+    for row in range(8):
+        dst = q.at[pl.ds(strip + row * width, width)]
+        moves.append(pltpu.make_async_copy(own.at[row, index], dst, sems.at[5 + row]))
+    for move in moves:
+        move.start()
+    for move in moves[:3]:
+        move.wait()
     for d in range(2):
-        c[d, 4:12] = cf[parity, d]
         for row in range(4):
             at = ((d * 2 + parity) * 4 + row) * 4
             for half in (slice(0, 4), slice(4, 8)):
-                c[d, row, half, :] = cup[at : at + 4, :]
-                c[d, row + 12, half, :] = cdown[at : at + 4, :]
+                c[d, row, half, :] = ends[0, at : at + 4, :]
+                c[d, row + 12, half, :] = ends[1, at : at + 4, :]
     lane = lax.broadcasted_iota(jnp.int32, (8, ny), 1)
     inside = valid[0, 0]
-    for t in range(ny // 128):
-        cols = slice(t * 128, t * 128 + 128)
-        high = flux_taps(c[0, 1, :, cols])
-        for row in range(14):
-            low, high = high, flux_taps(c[0, row + 2, :, cols])
-            for k, w in enumerate(cell_taps(low, high)):
-                wx[row, k, :, cols] = w * inside if row < 3 else w
-
-    def y_weights(row, carry):
+
+    def weights(row, carry):
+        keep = jnp.where(row < 3, inside, 1.0)
+        taps = cell_taps(flux_taps(c[0, row + 1]), flux_taps(c[0, row + 2]))
+        for k, w in enumerate(taps):
+            wx[row, k] = w * keep
         speed = c[1, row + 1]
         low = flux_taps(speed)
         high = flux_taps(jnp.where(lane == ny - 1, 0.0, pltpu.roll(speed, ny - 1, 1)))
@@ -116,9 +131,10 @@
             wy[row, k] = w
         return carry
 
-    lax.fori_loop(0, 14, y_weights, 0)
-
-    group = range(3)
+    lax.fori_loop(0, 14, weights, 0)
+    for move in moves[3:]:
+        move.wait()
+    parts = range(group // 8)
 
     def across(values, row):
         w = wy[row, 3]
@@ -130,42 +146,47 @@
             totals = [t + w * pltpu.roll(v, shift, 1) for t, v in zip(totals, values)]
         return totals
 
-    def tile(i, carry):
-        places = [pl.multiple_of(i * 24 + 8 * u, 8) for u in group]
+    def along(read, row, base):
+        done = [[] for _ in parts]
+        for t in range(ny // 128):
+            cols = slice(t * 128, t * 128 + 128)
+            w = wx[row, 0, :, cols]
+            totals = [w * read(base, cols, u) for u in parts]
+            for k in range(1, TAPS):
+                w = wx[row, k, :, cols]
+                totals = [v + w * read(base + k, cols, u) for u, v in enumerate(totals)]
+            for u in parts:
+                done[u].append(totals[u])
+        return [jnp.concatenate(pieces, axis=1) for pieces in done]
+
+    def back(i):
+        span = pl.ds(i * group, group)
+        return pltpu.make_async_copy(new.at[:, span], out.at[:, 0, span], sems.at[i])
+
+    for i in range(width // group):
 
         def first(row, cols, u):
-            at = places[u]
-            if row < 0:
-                return up[pl.ds((row + HALO) * width + at, 8), cols]
-            if row < 8:
-                return own[row, 0, pl.ds(at, 8), cols]
-            return down[pl.ds((row - 8) * width + at, 8), cols]
+            at = pl.multiple_of(row * width + i * group + u * 8, 8)
+            return q[pl.ds(at, 8), cols]
 
         def second(row, cols, u):
-            return mid[row + 3, u, :, cols]
-
-        def along(read, row):
-            parts = [[] for _ in group]
-            for t in range(ny // 128):
-                cols = slice(t * 128, t * 128 + 128)
-                w = wx[row + 3, 0, :, cols]
-                totals = [w * read(row - 3, cols, u) for u in group]
-                for k in range(1, TAPS):
-                    w = wx[row + 3, k, :, cols]
-                    totals = [v + w * read(row + k - 3, cols, u) for u, v in enumerate(totals)]
-                for part, v in zip(parts, totals):
-                    part.append(v)
-            return [jnp.concatenate(part, axis=1) for part in parts]
-
-        for row in range(-3, 11):
-            for u, v in enumerate(across(along(first, row), row + 3)):
-                mid[row + 3, u] = v
-        for row in range(8):
-            for u, v in enumerate(across(along(second, row), row + 3)):
-                out[row, 0, pl.ds(places[u], 8), :] = v
-        return carry
-
-    lax.fori_loop(0, width // 24, tile, 0)
+            return mid[row, u, :, cols]
+
+        def step_one(row, carry):
+            for u, v in enumerate(across(along(first, row, row), row)):
+                mid[row, u] = v
+            return carry
+
+        def step_two(row, carry):
+            for u, v in enumerate(across(along(second, row + 3, row), row + 3)):
+                new[row, i * group + u * 8 : i * group + u * 8 + 8, :] = v
+            return carry
+
+        lax.fori_loop(0, 14, step_one, 0)
+        lax.fori_loop(0, 8, step_two, 0)
+        back(i).start()
+    for i in range(width // group):
+        back(i).wait()
 
 
 def halves(value):
@@ -239,11 +260,11 @@
 
 
 def on_device(tracers, courant, layer_mass, pbl_top, land_type, rates, coupling):
-    own_species, levels, rows, ny = tracers.shape
+    own_species, _, rows, ny = tracers.shape
     species = coupling.shape[0]
     width = own_species * 4
     sds = jax.ShapeDtypeStruct
-    n_space, n_spec = lax.axis_size("space"), lax.axis_size("spec")
+    n_space = lax.axis_size("space")
     up_pairs = [(i, i + 1) for i in range(n_space - 1)]
     down_pairs = [(j, i) for i, j in up_pairs]
     split = tracers.reshape(own_species, 4, 2, rows, ny)
@@ -305,28 +326,24 @@
             input_output_aliases={2: 0} if into else {},
         )(a, coupling, *into)
 
-    cup, cdown = up[HALO * width :], down[HALO * width :]
+    cup, cdown = up, down
 
     def transported(parity, a, index, shape, before, after):
-        def plane(i):
-            return pl.BlockSpec((rows, 1, width, ny), lambda t: (0, i, 0, 0))
-
-        def whole(array):
-            return pl.BlockSpec(array.shape, lambda t: (0,) * array.ndim)
-
+        anywhere = pl.BlockSpec(memory_space=pl.ANY)
         return call(
-            functools.partial(transport, parity),
+            functools.partial(transport, parity, index),
             shape,
-            grid=(1,),
-            in_specs=[plane(index)]
-            + [whole(v) for v in (before, after, cup, cdown, speeds)]
-            + [pl.BlockSpec(memory_space=pltpu.SMEM)],
-            out_specs=plane(0),
+            in_specs=[anywhere] * 6 + [pl.BlockSpec(memory_space=pltpu.SMEM)],
+            out_specs=anywhere,
             scratch_shapes=[
+                pltpu.VMEM((20 * width, ny), F32),
                 pltpu.VMEM((2, 16, 8, ny), F32),
+                pltpu.VMEM((2, 64, ny), F32),
                 pltpu.VMEM((14, TAPS, 8, ny), F32),
                 pltpu.VMEM((14, TAPS, 8, ny), F32),
                 pltpu.VMEM((14, 3, 8, ny), F32),
+                pltpu.VMEM((rows, width, ny), F32),
+                pltpu.SemaphoreType.DMA((13,)),
             ],
         )(a, before, after, cup, cdown, speeds, valid)
 
@@ -353,9 +370,10 @@
     both = transported(0, even[:, None], 0, pair, up, down)
     both = coupled(odd[:, None], 0, pair, 1, both)
     both = exchange(both)
-    even = exchange(coupled(both, 0, single, 0))[:, 0]
     up = lax.ppermute(both[2:, 1].reshape(-1, ny), "space", up_pairs)
     down = lax.ppermute(both[:HALO, 1].reshape(-1, ny), "space", down_pairs)
+    even = coupled(both, 0, single, 0)
+    even = exchange(even)[:, 0]
     odd = transported(1, both, 1, single, up, down)[:, 0]
 
     updated, deposited = call(

time: 154 us -> 166 us (1.078)
  Pallas kernels: 50.1 us -> 63.4 us
  local copies, waits for them, and re-layouts: 6.79 us -> 4.42 us
    pallas_call x2, Pallas kernels: 24.9 us -> 38.2 us  [transported(): call(functools.partial(transport, parity, index), shape, in_specs=[anywhe...]
    slice x2 -> x0, local copies, waits for them, and re-layouts: 2.22 us -> none  [on_device(): cup, cdown = (up[HALO * width:], down[HALO * width:])]
  transfers between devices with their start and end apart: 6 -> 6, of which waited for: 4 -> 4; matrix products, arithmetic and copies ran while one was open for 3% -> 1% of each run, Pallas kernels for 22% -> 28%
where the time goes in v3:
time: 166 us; the launch traced here: 165 us
  Pallas kernels  63.4 us (38%)
  blocking collectives  38.8 us (23%)
  starting transfers between devices  29.2 us (18%)
  waiting for transfers between devices  28.1 us (17%)
  local copies, waits for them, and re-layouts  4.42 us (3%)
    all_to_all x1, blocking collectives, exchange(): return lax.all_to_all(a, 'spec', split_axis=0, concat_axis=0, tiled=True)  38.8 us
    pallas_call x2, Pallas kernels, transported(): call(functools.partial(transport, parity, index), shape, in_specs=[anywhe...  38.2 us
    all_to_all x2, starting transfers between devices, exchange(): return lax.all_to_all(a, 'spec', split_axis=0, concat_axis=0, tiled=True)  14 us
    ppermute x1, waiting for transfers between devices, on_device(): up = lax.ppermute(send_up, 'space', up_pairs)  11.8 us
    pallas_call x2, Pallas kernels, coupled(): call(couple, shape, grid=(strips,), in_specs=[half(index), whole] + [pl.B...  7.75 us
    ppermute x1, starting transfers between devices, on_device(): up = lax.ppermute(send_up, 'space', up_pairs)  5.86 us
    ppermute x1, starting transfers between devices, on_device(): up = lax.ppermute(both[2:, 1].reshape(-1, ny), 'space', up_pairs)  5.54 us
    ppermute x1, waiting for transfers between devices, on_device(): down = lax.ppermute(both[:HALO, 1].reshape(-1, ny), 'space', down_pairs)  5.5 us
  transfers between devices with their start and end apart: 6, of which 4 were waited for; matrix products, arithmetic and copies ran while one was open for 1% of the time, Pallas kernels for 28%

profile of v3, /device:TPU:101, one launch (start us, length us, event | category | flops | bytes accessed | tf_op | source)
XLA Modules:
  0.0 164.7 jit_solution(14775390311414189033)
XLA Ops:
  0.6 0.0 copy-start
  0.6 3.5 %shard_map.86 = f32[8,120,384]{2,1,0:T(8,128)} custom-call(f32[30,4,2,8,384]{4,3,2,1,0:T(8,128)} %bitcast.17), custom_call_target="tpu_custom_call" | custom-call | tf_op jit(solution)/shard_map/pallas_call | solution.py:301
  4.1 6.9 %all-to-all-start = ((f32[8,120,384]{2,1,0:T(8,128)}), f32[8,120,384]{2,1,0:T(8,128)}, u32[]{:S(2)}, u32[]{:S(2)}) async-start(f32[8,120,384]{2,1,0:T(8,128)} %shard_map.86), calls=%async_computation | async-start | bytes 2949120 | tf_op jit(solution)/shard_map/all_to_all | solution.py:310
  11.0 3.9 %shard_map.87 = (f32[8,120,384]{2,1,0:T(8,128)}, f32[784,384]{1,0:T(8,128)}, f32[784,384]{1,0:T(8,128)}, f32[2,2,8,8,384]{4,3,2,1,0:T(8,128)}) custom-call(f32[30,4,2,8,384]{4,3,2,1,0:T(8,128)} %bitcast.18, f32[128,384]{1,0:T(8,128)} %bitcast.24), custom_call_target="tpu_custom_call" | custom-call | tf_op jit(solution)/shard_map/pallas_call | solution.py:287
  14.9 5.9 %collective-permute-start = (f32[784,384]{1,0:T(8,128)}, f32[784,384]{1,0:T(8,128)S(1)}, u32[]{:S(2)}, u32[]{:S(2)}) collective-permute-start(f32[784,384]{1,0:T(8,128)} %get-tuple-element.12), channel_id=1, source_target_pairs={{0,8},{8,16},{16,24},{24,32},{32,40},{40,48},{48,56},{56,64},{64,7... | collective-permute-start | bytes 3612680 | tf_op jit(solution)/shard_map/ppermute | solution.py:299
  20.8 1.9 %collective-permute-start.1 = (f32[784,384]{1,0:T(8,128)}, f32[784,384]{1,0:T(8,128)S(1)}, u32[]{:S(2)}, u32[]{:S(2)}) collective-permute-start(f32[784,384]{1,0:T(8,128)} %get-tuple-element.13), channel_id=1, source_target_pairs={{8,0},{16,8},{24,16},{32,24},{40,32},{48,40},{56,48},{64,56},{72,6... | collective-permute-start | bytes 3612680 | tf_op jit(solution)/shard_map/ppermute | solution.py:300
  22.7 11.8 %collective-permute-done.up.cup = f32[784,384]{1,0:T(8,128)S(1)} collective-permute-done((f32[784,384]{1,0:T(8,128)}, f32[784,384]{1,0:T(8,128)S(1)}, u32[]{:S(2)}, u32[]{:S(2)}) %collective-permute-start) | collective-permute-done | bytes 1204256 | tf_op jit(solution)/shard_map/ppermute | solution.py:299
  34.5 0.0 copy-start.2
  34.5 5.5 %collective-permute-done.1.down.cdown = f32[784,384]{1,0:T(8,128)S(1)} collective-permute-done((f32[784,384]{1,0:T(8,128)}, f32[784,384]{1,0:T(8,128)S(1)}, u32[]{:S(2)}, u32[]{:S(2)}) %collective-permute-start.1) | collective-permute-done | bytes 1204256 | tf_op jit(solution)/shard_map/ppermute | solution.py:300
  40.0 0.0 copy-start.3
  40.0 0.0 copy-done.2
  40.0 1.1 copy-done.3
  41.1 19.1 %shard_map.88.refs_0_ = f32[8,2,120,384]{3,2,1,0:T(8,128)} custom-call(f32[8,1,120,384]{3,2,1,0:T(8,128)} %bitcast.20, f32[784,384]{1,0:T(8,128)} %copy-done.2, f32[784,384]{1,0:T(8,128)} %copy-done.3, f32[784,384]{1,0:T(8,128)} %copy-done.2, f32[784,384]{1,0:T(8,128)} %copy-done.3, f32[2,2,8,8,384]{4,3,2,1,0:T(8,128)} %get-tuple-element.14.cf, ...), custom_call_target="tpu_custom_call" | custom-call | tf_op jit(solution)/shard_map/pallas_call | solution.py:333
  60.2 0.0 all-to-all-done
  60.2 3.9 %shard_map.89 = f32[8,2,120,384]{3,2,1,0:T(8,128)} custom-call(f32[8,1,120,384]{3,2,1,0:T(8,128)} %bitcast.1.x, f32[240,240]{1,0:T(8,128)} %matrix.3, f32[8,2,120,384]{3,2,1,0:T(8,128)} %shard_map.88.refs_0_), custom_call_target="tpu_custom_call", output_to_operand_aliasing={{}: (2, {})} | custom-call | tf_op jit(solution)/shard_map/pallas_call | solution.py:319
  64.1 38.8 %all_to_all.15.x.own = f32[8,2,120,384]{3,2,1,0:T(8,128)} all-to-all(f32[8,2,120,384]{3,2,1,0:T(8,128)} %shard_map.89), channel_id=1, replica_groups=mesh['space'=32,'spec'=8] {'spec'}, dimensions={0} | all-to-all | bytes 5898240 | tf_op jit(solution)/shard_map/all_to_all | solution.py:310
  102.8 3.9 %shard_map.90 = f32[8,1,120,384]{3,2,1,0:T(8,128)} custom-call(f32[8,2,120,384]{3,2,1,0:T(8,128)} %all_to_all.15.x.own, f32[240,240]{1,0:T(8,128)} %matrix.3), custom_call_target="tpu_custom_call" | custom-call | tf_op jit(solution)/shard_map/pallas_call | solution.py:319
  106.7 0.0 copy-start.1
  106.7 7.1 %all-to-all-start.2 = ((f32[8,1,120,384]{3,2,1,0:T(8,128)}), f32[8,1,120,384]{3,2,1,0:T(8,128)}, u32[]{:S(2)}, u32[]{:S(2)}) async-start(f32[8,1,120,384]{3,2,1,0:T(8,128)} %shard_map.90), calls=%async_computation.2 | async-start | bytes 2949120 | tf_op jit(solution)/shard_map/all_to_all | solution.py:310
  113.8 0.0 copy-done.1
  113.8 1.5 fusion
  115.4 5.5 %collective-permute-start.2 = (f32[720,384]{1,0:T(8,128)}, f32[720,384]{1,0:T(8,128)S(1)}, u32[]{:S(2)}, u32[]{:S(2)}) collective-permute-start(f32[720,384]{1,0:T(8,128)} %bitcast.6), channel_id=1, source_target_pairs={{0,8},{8,16},{16,24},{24,32},{32,40},{40,48},{48,56},{56,64},{64,7... | collective-permute-start | bytes 3317768 | tf_op jit(solution)/shard_map/ppermute | solution.py:373
  120.9 1.9 %collective-permute-start.3 = (f32[720,384]{1,0:T(8,128)}, f32[720,384]{1,0:T(8,128)S(1)}, u32[]{:S(2)}, u32[]{:S(2)}) collective-permute-start(f32[720,384]{1,0:T(8,128)} %bitcast.7), channel_id=1, source_target_pairs={{8,0},{16,8},{24,16},{32,24},{40,32},{48,40},{56,48},{64,56},{72,6... | collective-permute-start | bytes 3317768 | tf_op jit(solution)/shard_map/ppermute | solution.py:374
  122.8 0.0 copy-done
  122.8 0.1 dynamic-slice_bitcast_fusion
  122.9 0.1 copy.13
  123.0 0.6 pad.4.clone
  123.7 4.5 %shard_map.92 = (f32[8,120,384]{2,1,0:T(8,128)}, f32[8,8,384]{2,1,0:T(8,128)}, f32[8,8,384]{2,1,0:T(8,128)}) custom-call(f32[64,384]{1,0:T(8,128)} %bitcast.21, s32[8,384]{1,0:T(8,128)} %pbl.3, s32[8,384]{1,0:T(8,128)} %land.1, f32[120,16]{1,0:T(8,128)} %bitcast.23), custom_call_target="tpu_custom_call" | custom-call | tf_op jit(solution)/shard_map/pallas_call | solution.py:355
  128.2 5.3 %collective-permute-done.2.up = f32[720,384]{1,0:T(8,128)S(1)} collective-permute-done((f32[720,384]{1,0:T(8,128)}, f32[720,384]{1,0:T(8,128)S(1)}, u32[]{:S(2)}, u32[]{:S(2)}) %collective-permute-start.2) | collective-permute-done | bytes 1105952 | tf_op jit(solution)/shard_map/ppermute | solution.py:373
  133.6 0.0 copy-start.4
  133.6 5.5 %collective-permute-done.3.down = f32[720,384]{1,0:T(8,128)S(1)} collective-permute-done((f32[720,384]{1,0:T(8,128)}, f32[720,384]{1,0:T(8,128)S(1)}, u32[]{:S(2)}, u32[]{:S(2)}) %collective-permute-start.3) | collective-permute-done | bytes 1105952 | tf_op jit(solution)/shard_map/ppermute | solution.py:374
  139.1 0.0 copy-done.4
  139.1 0.0 copy-start.5
  139.1 1.0 copy-done.5
  140.0 19.1 %shard_map.91 = f32[8,1,120,384]{3,2,1,0:T(8,128)} custom-call(f32[8,2,120,384]{3,2,1,0:T(8,128)} %all_to_all.15.x.own, f32[720,384]{1,0:T(8,128)} %copy-done.4, f32[720,384]{1,0:T(8,128)} %copy-done.5, f32[784,384]{1,0:T(8,128)} %copy-done.2, f32[784,384]{1,0:T(8,128)} %copy-done.3, f32[2,2,8,8,384]{4,3,2,1,0:T(8,128)} %get-tuple-element.14.cf, ...), custom_call_target="tpu_custom_call" | custom-call | tf_op jit(solution)/shard_map/pallas_call | solution.py:333
  159.2 0.0 all-to-all-done.2
  159.2 5.5 %shard_map.93 = (f32[1920,384]{1,0:T(8,128)}, f32[240,384]{1,0:T(8,128)}) custom-call(f32[8,120,384]{2,1,0:T(8,128)} %bitcast.5.even, f32[8,120,384]{2,1,0:T(8,128)} %bitcast.19, f32[8,120,384]{2,1,0:T(8,128)} %get-tuple-element.15.keep, f32[8,8,384]{2,1,0:T(8,128)} %get-tuple-element.16.weven, f32[8,8,384]{2,1,0:T(8,128)} %get-tuple-element.17.wodd, ...), custom_call_target="tpu_custom_call" | custom-call | tf_op jit(solution)/shard_map/pallas_call | solution.py:379
Async XLA Ops:
  0.6 122.2 %copy-start = (f32[11,240]{1,0:T(8,128)S(1)}, f32[11,240]{1,0:T(8,128)}, u32[]{:S(2)}) copy-start(f32[11,240]{1,0:T(8,128)} %param.12) | copy-start | bytes 31684
  4.1 56.1 %all-to-all-start = ((f32[8,120,384]{2,1,0:T(8,128)}), f32[8,120,384]{2,1,0:T(8,128)}, u32[]{:S(2)}, u32[]{:S(2)}) async-start(f32[8,120,384]{2,1,0:T(8,128)} %shard_map.86), calls=%async_computation | async-start | bytes 2949120 | tf_op jit(solution)/shard_map/all_to_all | solution.py:310
  14.9 19.6 %collective-permute-start = (f32[784,384]{1,0:T(8,128)}, f32[784,384]{1,0:T(8,128)S(1)}, u32[]{:S(2)}, u32[]{:S(2)}) collective-permute-start(f32[784,384]{1,0:T(8,128)} %get-tuple-element.12), channel_id=1, source_target_pairs={{0,8},{8,16},{16,24},{24,32},{32,40},{40,48},{48,56},{56,64},{64,7... | collective-permute-start | bytes 3612680 | tf_op jit(solution)/shard_map/ppermute | solution.py:299
  20.8 19.2 %collective-permute-start.1 = (f32[784,384]{1,0:T(8,128)}, f32[784,384]{1,0:T(8,128)S(1)}, u32[]{:S(2)}, u32[]{:S(2)}) collective-permute-start(f32[784,384]{1,0:T(8,128)} %get-tuple-element.13), channel_id=1, source_target_pairs={{8,0},{16,8},{24,16},{32,24},{40,32},{48,40},{56,48},{64,56},{72,6... | collective-permute-start | bytes 3612680 | tf_op jit(solution)/shard_map/ppermute | solution.py:300
  34.5 5.5 %copy-start.2 = (f32[784,384]{1,0:T(8,128)}, f32[784,384]{1,0:T(8,128)S(1)}, u32[]{:S(2)}) copy-start(f32[784,384]{1,0:T(8,128)S(1)} %collective-permute-done.up.cup) | copy-start | bytes 3612676
  40.0 1.1 copy-start.3
  106.7 7.1 %copy-start.1 = (f32[8,2,120,384]{3,2,1,0:T(8,128)S(1)}, f32[8,2,120,384]{3,2,1,0:T(8,128)}, u32[]{:S(2)}) copy-start(f32[8,2,120,384]{3,2,1,0:T(8,128)} %all_to_all.15.x.own) | copy-start | bytes 8847364
  106.7 52.5 %all-to-all-start.2 = ((f32[8,1,120,384]{3,2,1,0:T(8,128)}), f32[8,1,120,384]{3,2,1,0:T(8,128)}, u32[]{:S(2)}, u32[]{:S(2)}) async-start(f32[8,1,120,384]{3,2,1,0:T(8,128)} %shard_map.90), calls=%async_computation.2 | async-start | bytes 2949120 | tf_op jit(solution)/shard_map/all_to_all | solution.py:310
  115.4 18.2 %collective-permute-start.2 = (f32[720,384]{1,0:T(8,128)}, f32[720,384]{1,0:T(8,128)S(1)}, u32[]{:S(2)}, u32[]{:S(2)}) collective-permute-start(f32[720,384]{1,0:T(8,128)} %bitcast.6), channel_id=1, source_target_pairs={{0,8},{8,16},{16,24},{24,32},{32,40},{40,48},{48,56},{56,64},{64,7... | collective-permute-start | bytes 3317768 | tf_op jit(solution)/shard_map/ppermute | solution.py:373
  120.9 18.2 %collective-permute-start.3 = (f32[720,384]{1,0:T(8,128)}, f32[720,384]{1,0:T(8,128)S(1)}, u32[]{:S(2)}, u32[]{:S(2)}) collective-permute-start(f32[720,384]{1,0:T(8,128)} %bitcast.7), channel_id=1, source_target_pairs={{8,0},{16,8},{24,16},{32,24},{40,32},{48,40},{56,48},{64,56},{72,6... | collective-permute-start | bytes 3317768 | tf_op jit(solution)/shard_map/ppermute | solution.py:374
  133.6 5.5 %copy-start.4 = (f32[720,384]{1,0:T(8,128)}, f32[720,384]{1,0:T(8,128)S(1)}, u32[]{:S(2)}) copy-start(f32[720,384]{1,0:T(8,128)S(1)} %collective-permute-done.2.up) | copy-start | bytes 3317764
  139.1 1.0 copy-start.5

commit v4 on v3

--- a/solution.py
+++ b/solution.py
@@ -20,37 +20,36 @@
 
 
 def pack_even(x, cf, own, up, down, speeds):
-    width = own.shape[1]
+    width = own.shape[2]
     x = x.reshape(width * 8, 128)
     for r in range(8):
         for i in range(width // 8):
             value = x[pl.ds(i * 64 + r, 8, stride=8), :]
-            own[r, i * 8 : i * 8 + 8, :] = value
+            rows = slice(i * 8, i * 8 + 8)
+            own[r, 0, rows, :] = value
             if r >= 2:
-                at = (r - 2) * width + i * 8
-                up[at : at + 8, :] = value
+                up[r - 2, 0, rows, :] = value
             if r < 6:
-                at = r * width + i * 8
-                down[at : at + 8, :] = value
+                down[r, 0, rows, :] = value
     for d in range(2):
         for parity in range(2):
             for row in range(4):
-                at = HALO * width + ((d * 2 + parity) * 4 + row) * 4
+                at = ((d * 2 + parity) * 4 + row) * 4
                 start = d * 64 + parity * 8 + row
                 before = cf[pl.ds(start, 4, stride=16), :]
                 after = cf[pl.ds(start + 4, 4, stride=16), :]
-                down[at : at + 4, :] = before
-                up[at : at + 4, :] = after
+                down[HALO, 0, at : at + 4, :] = before
+                up[HALO, 0, at : at + 4, :] = after
                 for half in (slice(0, 4), slice(4, 8)):
                     speeds[parity, d, row, half, :] = before
                     speeds[parity, d, row + 4, half, :] = after
 
 
 def pack_odd(x, own):
-    x = x.reshape(own.shape[1] * 8, 128)
+    x = x.reshape(own.shape[2] * 8, 128)
     for r in range(8):
-        for i in range(own.shape[1] // 8):
-            own[r, i * 8 : i * 8 + 8, :] = x[pl.ds(i * 64 + r, 8, stride=8), :]
+        for i in range(own.shape[2] // 8):
+            own[r, 0, i * 8 : i * 8 + 8, :] = x[pl.ds(i * 64 + r, 8, stride=8), :]
 
 
 def flux_taps(c):
@@ -90,20 +89,18 @@
 def transport(
     parity, index, own, up, down, cup, cdown, cf, valid, out, q, c, ends, wx, wy, mid, new, sems
 ):
-    width = own.shape[2]
-    ny = own.shape[3]
-    group = 24
-    strip = HALO * width
+    width = own.shape[3]
+    strips = own.shape[2]
+    ny = strips * 128
+    group = 8
     moves = [
         pltpu.make_async_copy(cf.at[parity], c.at[:, pl.ds(4, 8)], sems.at[0]),
-        pltpu.make_async_copy(cup.at[pl.ds(strip, 64)], ends.at[0], sems.at[1]),
-        pltpu.make_async_copy(cdown.at[pl.ds(strip, 64)], ends.at[1], sems.at[2]),
-        pltpu.make_async_copy(up.at[pl.ds(0, strip)], q.at[pl.ds(0, strip)], sems.at[3]),
-        pltpu.make_async_copy(down.at[pl.ds(0, strip)], q.at[pl.ds(strip + 8 * width, strip)], sems.at[4]),
+        pltpu.make_async_copy(cup.at[HALO, :, pl.ds(0, 64)], ends.at[0], sems.at[1]),
+        pltpu.make_async_copy(cdown.at[HALO, :, pl.ds(0, 64)], ends.at[1], sems.at[2]),
+        pltpu.make_async_copy(up.at[pl.ds(0, HALO)], q.at[pl.ds(0, HALO)], sems.at[3]),
+        pltpu.make_async_copy(own.at[:, index], q.at[pl.ds(HALO, 8)], sems.at[4]),
+        pltpu.make_async_copy(down.at[pl.ds(0, HALO)], q.at[pl.ds(HALO + 8, HALO)], sems.at[5]),
     ]
-    for row in range(8):
-        dst = q.at[pl.ds(strip + row * width, width)]
-        moves.append(pltpu.make_async_copy(own.at[row, index], dst, sems.at[5 + row]))
     for move in moves:
         move.start()
     for move in moves[:3]:
@@ -111,9 +108,11 @@
     for d in range(2):
         for row in range(4):
             at = ((d * 2 + parity) * 4 + row) * 4
-            for half in (slice(0, 4), slice(4, 8)):
-                c[d, row, half, :] = ends[0, at : at + 4, :]
-                c[d, row + 12, half, :] = ends[1, at : at + 4, :]
+            for t in range(strips):
+                cols = slice(t * 128, t * 128 + 128)
+                for half in (slice(0, 4), slice(4, 8)):
+                    c[d, row, half, cols] = ends[0, t, at : at + 4, :]
+                    c[d, row + 12, half, cols] = ends[1, t, at : at + 4, :]
     lane = lax.broadcasted_iota(jnp.int32, (8, ny), 1)
     inside = valid[0, 0]
 
@@ -128,6 +127,10 @@
         for k, w in enumerate(cell_taps(low, high)):
             shift = k - 3
             w = jnp.where((lane + shift >= 0) & (lane + shift < ny), w, 0.0)
+            if shift >= 2:
+                w = pltpu.roll(w, 3, 1)
+            if shift <= -2:
+                w = pltpu.roll(w, ny - 3, 1)
             wy[row, k] = w
         return carry
 
@@ -137,54 +140,55 @@
     parts = range(group // 8)
 
     def across(values, row):
-        w = wy[row, 3]
-        totals = [w * v for v in values]
-        for shift in (1, 2, 3):
-            w = wy[row, 3 + shift]
-            totals = [t + w * pltpu.roll(v, ny - shift, 1) for t, v in zip(totals, values)]
-            w = wy[row, 3 - shift]
-            totals = [t + w * pltpu.roll(v, shift, 1) for t, v in zip(totals, values)]
+        after = [pltpu.roll(v, ny - 1, 1) for v in values]
+        before = [pltpu.roll(v, 1, 1) for v in values]
+        w = [wy[row, k] for k in range(TAPS)]
+        totals = []
+        for v, p, m in zip(values, after, before):
+            total = w[3] * v + w[4] * p + w[2] * m
+            total += pltpu.roll(w[5] * m + w[6] * v, ny - 3, 1)
+            total += pltpu.roll(w[1] * p + w[0] * v, 3, 1)
+            totals.append(total)
         return totals
 
     def along(read, row, base):
         done = [[] for _ in parts]
-        for t in range(ny // 128):
+        for t in range(strips):
             cols = slice(t * 128, t * 128 + 128)
             w = wx[row, 0, :, cols]
-            totals = [w * read(base, cols, u) for u in parts]
+            totals = [w * read(base, t, u) for u in parts]
             for k in range(1, TAPS):
                 w = wx[row, k, :, cols]
-                totals = [v + w * read(base + k, cols, u) for u, v in enumerate(totals)]
+                totals = [v + w * read(base + k, t, u) for u, v in enumerate(totals)]
             for u in parts:
                 done[u].append(totals[u])
         return [jnp.concatenate(pieces, axis=1) for pieces in done]
 
     def back(i):
-        span = pl.ds(i * group, group)
-        return pltpu.make_async_copy(new.at[:, span], out.at[:, 0, span], sems.at[i])
-
-    for i in range(width // group):
-
-        def first(row, cols, u):
-            at = pl.multiple_of(row * width + i * group + u * 8, 8)
-            return q[pl.ds(at, 8), cols]
-
-        def second(row, cols, u):
-            return mid[row, u, :, cols]
-
-        def step_one(row, carry):
+        span = pl.ds(pl.multiple_of(i * group, 8), group)
+        return pltpu.make_async_copy(new.at[:, :, span], out.at[:, 0, :, span], sems.at[i])
+
+    def block(i, carry):
+        places = [pl.multiple_of(i * group + u * 8, 8) for u in parts]
+
+        def first(row, t, u):
+            return q[row, t, pl.ds(places[u], 8), :]
+
+        def second(row, t, u):
+            return mid[row, u, :, t * 128 : t * 128 + 128]
+
+        for row in range(14):
             for u, v in enumerate(across(along(first, row, row), row)):
                 mid[row, u] = v
-            return carry
-
-        def step_two(row, carry):
-            for u, v in enumerate(across(along(second, row + 3, row), row + 3)):
-                new[row, i * group + u * 8 : i * group + u * 8 + 8, :] = v
-            return carry
-
-        lax.fori_loop(0, 14, step_one, 0)
-        lax.fori_loop(0, 8, step_two, 0)
+            late = row - 6
+            if late >= 0:
+                for u, v in enumerate(across(along(second, late + 3, late), late + 3)):
+                    for t in range(strips):
+                        new[late, t, pl.ds(places[u], 8), :] = v[:, t * 128 : t * 128 + 128]
         back(i).start()
+        return carry
+
+    lax.fori_loop(0, width // group, block, 0)
     for i in range(width // group):
         back(i).wait()
 
@@ -232,30 +236,31 @@
         loss = jnp.dot(
             rates[...], onehot, precision=lax.Precision.HIGHEST, preferred_element_type=F32
         )
-        keep[r] = jnp.exp(-loss)
+        keep[r, 0] = jnp.exp(-loss)
 
 
 def finish(even, odd, keep, weven, wodd, pbl, lm, out, dep, flux):
-    ny = even.shape[2]
+    ny = even.shape[3]
+    width = even.shape[2]
     sub = lax.broadcasted_iota(jnp.int32, (8, ny), 0)
     level = 2 * (sub % 4)
     first = sub % 2 == 0
     low = sub % 4 < 2
     for r in range(8):
         top = pbl[r : r + 1, :]
-        for i in range(even.shape[1] // 8):
+        for i in range(width // 8):
             at = slice(i * 8, i * 8 + 8)
-            a, b = even[r, at, :], odd[r, at, :]
+            a, b = even[r, 0, at, :], odd[r, 0, at, :]
             total = weven[r] * a + wodd[r] * b
             total += jnp.where(first, pltpu.roll(total, 7, 0), pltpu.roll(total, 1, 0))
             total += jnp.where(low, pltpu.roll(total, 6, 0), pltpu.roll(total, 2, 0))
             a = jnp.where(level < top, total, a)
             b = jnp.where(level + 1 < top, total, b)
-            kept = a * keep[r, at, :]
+            kept = a * keep[r, 0, at, :]
             flux[at, :] = (a - kept) * lm[r : r + 1, :]
             out[pl.ds(i * 128 + r, 8, stride=16), :] = kept
             out[pl.ds(i * 128 + 8 + r, 8, stride=16), :] = b
-        count = even.shape[1] // 4
+        count = width // 4
         dep[pl.ds(r, count, stride=8), :] = flux[pl.ds(0, count, stride=4), :]
 
 
@@ -272,13 +277,16 @@
     lm = layer_mass.reshape(-1, ny)
     valid = (lax.axis_index("space") > 0).astype(F32).reshape(1, 1)
 
-    group = sds((rows, width, ny), F32)
-    edge = sds((HALO * width + 64, ny), F32)
+    strips = ny // 128
+    group = sds((rows, strips, width, 128), F32)
+    edge = sds((HALO + 1, strips, width, 128), F32)
     speeds = sds((2, 2, rows, 8, ny), F32)
-    strips = ny // 128
 
     def strip(*shape):
         return pl.BlockSpec((*shape, 128), lambda t: (0,) * len(shape) + (t,))
+
+    def columns(count):
+        return pl.BlockSpec((count, 1, width, 128), lambda t: (0, t, 0, 0))
 
     def level_group(parity):
         shape = (own_species, 4, 1, rows, 128)
@@ -290,9 +298,9 @@
         grid=(strips,),
         in_specs=[level_group(0), strip(cf.shape[0])],
         out_specs=[
-            strip(rows, width),
-            strip(edge.shape[0]),
-            strip(edge.shape[0]),
+            columns(rows),
+            columns(HALO + 1),
+            columns(HALO + 1),
             strip(2, 2, rows, 8),
         ],
     )(split, cf)
@@ -303,16 +311,16 @@
         group,
         grid=(strips,),
         in_specs=[level_group(1)],
-        out_specs=strip(rows, width),
+        out_specs=columns(rows),
     )(split)
 
     def exchange(a):
         return lax.all_to_all(a, "spec", split_axis=0, concat_axis=0, tiled=True)
 
-    pair = sds((rows, 2, width, ny), F32)
+    pair = sds((rows, 2, strips, width, 128), F32)
 
     def half(index):
-        return pl.BlockSpec((rows, 1, width, 128), lambda t: (0, index, 0, t))
+        return pl.BlockSpec((rows, 1, 1, width, 128), lambda t: (0, index, t, 0, 0))
 
     def coupled(a, index, shape, out_index, *into):
         whole = pl.BlockSpec((species, species), lambda t: (0, 0))
@@ -336,14 +344,14 @@
             in_specs=[anywhere] * 6 + [pl.BlockSpec(memory_space=pltpu.SMEM)],
             out_specs=anywhere,
             scratch_shapes=[
-                pltpu.VMEM((20 * width, ny), F32),
+                pltpu.VMEM((20, strips, width, 128), F32),
                 pltpu.VMEM((2, 16, 8, ny), F32),
-                pltpu.VMEM((2, 64, ny), F32),
+                pltpu.VMEM((2, strips, 64, 128), F32),
                 pltpu.VMEM((14, TAPS, 8, ny), F32),
                 pltpu.VMEM((14, TAPS, 8, ny), F32),
-                pltpu.VMEM((14, 3, 8, ny), F32),
-                pltpu.VMEM((rows, width, ny), F32),
-                pltpu.SemaphoreType.DMA((13,)),
+                pltpu.VMEM((14, 1, 8, ny), F32),
+                pltpu.VMEM((rows, strips, width, 128), F32),
+                pltpu.SemaphoreType.DMA((15,)),
             ],
         )(a, before, after, cup, cdown, speeds, valid)
 
@@ -362,16 +370,16 @@
             strip(rows),
             pl.BlockSpec(mine.shape, lambda t: (0, 0)),
         ],
-        out_specs=[strip(rows, width), strip(rows, 8), strip(rows, 8)],
+        out_specs=[columns(rows), strip(rows, 8), strip(rows, 8)],
     )(lm, pbl_top, land_type, mine)
 
-    single = sds((rows, 1, width, ny), F32)
+    single = sds((rows, 1, strips, width, 128), F32)
     odd = exchange(odd)
     both = transported(0, even[:, None], 0, pair, up, down)
     both = coupled(odd[:, None], 0, pair, 1, both)
     both = exchange(both)
-    up = lax.ppermute(both[2:, 1].reshape(-1, ny), "space", up_pairs)
-    down = lax.ppermute(both[:HALO, 1].reshape(-1, ny), "space", down_pairs)
+    up = lax.ppermute(both[2:, 1], "space", up_pairs)
+    down = lax.ppermute(both[:HALO, 1], "space", down_pairs)
     even = coupled(both, 0, single, 0)
     even = exchange(even)[:, 0]
     odd = transported(1, both, 1, single, up, down)[:, 0]
@@ -380,7 +388,7 @@
         finish,
         (sds((tracers.size // ny, ny), F32), sds((own_species * rows, ny), F32)),
         grid=(strips,),
-        in_specs=[strip(rows, width)] * 3 + [strip(rows, 8)] * 2 + [strip(rows)] * 2,
+        in_specs=[columns(rows)] * 3 + [strip(rows, 8)] * 2 + [strip(rows)] * 2,
         out_specs=[strip(tracers.size // ny), strip(own_species * rows)],
         scratch_shapes=[pltpu.VMEM((width, 128), F32)],
     )(even, odd, keep, weven, wodd, pbl_top, lm)

time: 166 us -> 145 us (0.87)
  Pallas kernels: 63.4 us -> 52 us
  waiting for transfers between devices: 28.1 us -> 19.1 us
    pallas_call x2, Pallas kernels: 38.2 us -> 26.9 us  [transported(): call(functools.partial(transport, parity, index), shape, in_specs=[anywhe...]
    ppermute x1, waiting for transfers between devices: 11.8 us -> 2.38 us  [on_device(): up = lax.ppermute(send_up, 'space', up_pairs)]
  transfers between devices with their start and end apart: 6 -> 6, of which waited for: 4 -> 4; matrix products, arithmetic and copies ran while one was open for 1% -> 2% of each run, Pallas kernels for 28% -> 24%
where the time goes in v4:
time: 145 us; the launch traced here: 144 us
  Pallas kernels  52 us (36%)
  blocking collectives  38.6 us (27%)
  starting transfers between devices  29.1 us (20%)
  waiting for transfers between devices  19.1 us (13%)
  local copies, waits for them, and re-layouts  4.42 us (3%)
    all_to_all x1, blocking collectives, exchange(): return lax.all_to_all(a, 'spec', split_axis=0, concat_axis=0, tiled=True)  38.6 us
    pallas_call x2, Pallas kernels, transported(): call(functools.partial(transport, parity, index), shape, in_specs=[anywhe...  26.9 us
    all_to_all x2, starting transfers between devices, exchange(): return lax.all_to_all(a, 'spec', split_axis=0, concat_axis=0, tiled=True)  14 us
    pallas_call x2, Pallas kernels, coupled(): call(couple, shape, grid=(strips,), in_specs=[half(index), whole] + [pl.B...  7.73 us
    ppermute x1, starting transfers between devices, on_device(): up = lax.ppermute(both[2:, 1], 'space', up_pairs)  5.94 us
    ppermute x1, waiting for transfers between devices, on_device(): down = lax.ppermute(send_down, 'space', down_pairs)  5.9 us
    ppermute x1, waiting for transfers between devices, on_device(): down = lax.ppermute(both[:HALO, 1], 'space', down_pairs)  5.5 us
    pallas_call x1, Pallas kernels, on_device(): call(finish, (sds((tracers.size // ny, ny), F32), sds((own_species * rows...  5.39 us
  transfers between devices with their start and end apart: 6, of which 4 were waited for; matrix products, arithmetic and copies ran while one was open for 2% of the time, Pallas kernels for 24%

profile of v4, /device:TPU:101, one launch (start us, length us, event | category | flops | bytes accessed | tf_op | source)
XLA Modules:
  0.0 143.9 jit_solution(4049512024069476266)
XLA Ops:
  0.6 0.0 copy-start
  0.6 3.9 %shard_map.87 = (f32[8,3,120,128]{3,2,1,0:T(8,128)}, f32[7,3,120,128]{3,2,1,0:T(8,128)}, f32[7,3,120,128]{3,2,1,0:T(8,128)}, f32[2,2,8,8,384]{4,3,2,1,0:T(8,128)}) custom-call(f32[30,4,2,8,384]{4,3,2,1,0:T(8,128)} %bitcast.23, f32[128,384]{1,0:T(8,128)} %bitcast.30), custom_call_target="tpu_custom_call" | custom-call | tf_op jit(solution)/shard_map/pallas_call | solution.py:295
  4.6 5.3 %collective-permute-start = (f32[7,3,120,128]{3,2,1,0:T(8,128)}, f32[7,3,120,128]{3,2,1,0:T(8,128)S(1)}, u32[]{:S(2)}, u32[]{:S(2)}) collective-permute-start(f32[7,3,120,128]{3,2,1,0:T(8,128)} %get-tuple-element.12), channel_id=1, source_target_pairs={{0,8},{8,16},{16,24},{24,32},{32,40},{40,48},{48,56},{56,64},{64,7... | collective-permute-start | bytes 3870728 | tf_op jit(solution)/shard_map/ppermute | solution.py:307
  9.9 1.9 %collective-permute-start.1 = (f32[7,3,120,128]{3,2,1,0:T(8,128)}, f32[7,3,120,128]{3,2,1,0:T(8,128)S(1)}, u32[]{:S(2)}, u32[]{:S(2)}) collective-permute-start(f32[7,3,120,128]{3,2,1,0:T(8,128)} %get-tuple-element.13), channel_id=1, source_target_pairs={{8,0},{16,8},{24,16},{32,24},{40,32},{48,40},{56,48},{64,56},{72,6... | collective-permute-start | bytes 3870728 | tf_op jit(solution)/shard_map/ppermute | solution.py:308
  11.8 3.4 %shard_map.86 = f32[8,3,120,128]{3,2,1,0:T(8,128)} custom-call(f32[30,4,2,8,384]{4,3,2,1,0:T(8,128)} %bitcast.24), custom_call_target="tpu_custom_call" | custom-call | tf_op jit(solution)/shard_map/pallas_call | solution.py:309
  15.3 6.9 %all-to-all-start = ((f32[8,3,120,128]{3,2,1,0:T(8,128)}), f32[8,3,120,128]{3,2,1,0:T(8,128)}, u32[]{:S(2)}, u32[]{:S(2)}) async-start(f32[8,3,120,128]{3,2,1,0:T(8,128)} %shard_map.86), calls=%async_computation | async-start | bytes 2949120 | tf_op jit(solution)/shard_map/all_to_all | solution.py:318
  22.1 2.4 %collective-permute-done.up.cup = f32[7,3,120,128]{3,2,1,0:T(8,128)S(1)} collective-permute-done((f32[7,3,120,128]{3,2,1,0:T(8,128)}, f32[7,3,120,128]{3,2,1,0:T(8,128)S(1)}, u32[]{:S(2)}, u32[]{:S(2)}) %collective-permute-start) | collective-permute-done | bytes 1290272 | tf_op jit(solution)/shard_map/ppermute | solution.py:307
  24.5 0.0 copy-start.2
  24.5 5.9 %collective-permute-done.1.down.cdown = f32[7,3,120,128]{3,2,1,0:T(8,128)S(1)} collective-permute-done((f32[7,3,120,128]{3,2,1,0:T(8,128)}, f32[7,3,120,128]{3,2,1,0:T(8,128)S(1)}, u32[]{:S(2)}, u32[]{:S(2)}) %collective-permute-start.1) | collective-permute-done | bytes 1290272 | tf_op jit(solution)/shard_map/ppermute | solution.py:308
  30.4 0.0 copy-start.3
  30.4 0.0 copy-done.2
  30.4 1.1 copy-done.3
  31.5 14.0 %shard_map.88.refs_0_ = f32[8,2,3,120,128]{4,3,2,1,0:T(8,128)} custom-call(f32[8,1,3,120,128]{4,3,2,1,0:T(8,128)} %bitcast.26, f32[7,3,120,128]{3,2,1,0:T(8,128)} %copy-done.2, f32[7,3,120,128]{3,2,1,0:T(8,128)} %copy-done.3, f32[7,3,120,128]{3,2,1,0:T(8,128)} %copy-done.2, f32[7,3,120,128]{3,2,1,0:T(8,128)} %copy-done.3, ...), custom_call_target="tpu_custom_call" | custom-call | tf_op jit(solution)/shard_map/pallas_call | solution.py:341
  45.5 0.0 all-to-all-done
  45.5 3.9 %shard_map.89 = f32[8,2,3,120,128]{4,3,2,1,0:T(8,128)} custom-call(f32[8,1,3,120,128]{4,3,2,1,0:T(8,128)} %bitcast.1.x, f32[240,240]{1,0:T(8,128)} %matrix.3, f32[8,2,3,120,128]{4,3,2,1,0:T(8,128)} %shard_map.88.refs_0_), custom_call_target="tpu_custom_call", output_to_operand_aliasing={{}: (2, {})} | custom-call | tf_op jit(solution)/shard_map/pallas_call | solution.py:327
  49.4 38.6 %all_to_all.15.x.own = f32[8,2,3,120,128]{4,3,2,1,0:T(8,128)} all-to-all(f32[8,2,3,120,128]{4,3,2,1,0:T(8,128)} %shard_map.89), channel_id=1, replica_groups=mesh['space'=32,'spec'=8] {'spec'}, dimensions={0} | all-to-all | bytes 5898240 | tf_op jit(solution)/shard_map/all_to_all | solution.py:318
  88.0 3.9 %shard_map.90 = f32[8,1,3,120,128]{4,3,2,1,0:T(8,128)} custom-call(f32[8,2,3,120,128]{4,3,2,1,0:T(8,128)} %all_to_all.15.x.own, f32[240,240]{1,0:T(8,128)} %matrix.3), custom_call_target="tpu_custom_call" | custom-call | tf_op jit(solution)/shard_map/pallas_call | solution.py:327
  91.8 0.0 copy-start.1
  91.8 7.1 %all-to-all-start.2 = ((f32[8,1,3,120,128]{4,3,2,1,0:T(8,128)}), f32[8,1,3,120,128]{4,3,2,1,0:T(8,128)}, u32[]{:S(2)}, u32[]{:S(2)}) async-start(f32[8,1,3,120,128]{4,3,2,1,0:T(8,128)} %shard_map.90), calls=%async_computation.2 | async-start | bytes 2949120 | tf_op jit(solution)/shard_map/all_to_all | solution.py:318
  98.9 0.0 copy-done.1
  99.0 1.5 %slice_bitcast_fusion = (f32[6,3,120,128]{3,2,1,0:T(8,128)}, f32[6,3,120,128]{3,2,1,0:T(8,128)}) fusion(f32[8,2,3,120,128]{4,3,2,1,0:T(8,128)S(1)} %copy-done.1), kind=kLoop, calls=%fused_computation | loop fusion | bytes 4423680 | tf_op jit(solution)/shard_map/squeeze | solution.py:382
  100.5 5.9 %collective-permute-start.2 = (f32[6,3,120,128]{3,2,1,0:T(8,128)}, f32[6,3,120,128]{3,2,1,0:T(8,128)S(1)}, u32[]{:S(2)}, u32[]{:S(2)}) collective-permute-start(f32[6,3,120,128]{3,2,1,0:T(8,128)} %get-tuple-element.21), channel_id=1, source_target_pairs={{0,8},{8,16},{16,24},{24,32},{32,40},{40,48},{48,56},{56,64},{64,7... | collective-permute-start | bytes 3317768 | tf_op jit(solution)/shard_map/ppermute | solution.py:381
  106.4 1.9 %collective-permute-start.3 = (f32[6,3,120,128]{3,2,1,0:T(8,128)}, f32[6,3,120,128]{3,2,1,0:T(8,128)S(1)}, u32[]{:S(2)}, u32[]{:S(2)}) collective-permute-start(f32[6,3,120,128]{3,2,1,0:T(8,128)} %get-tuple-element.20), channel_id=1, source_target_pairs={{8,0},{16,8},{24,16},{32,24},{40,32},{48,40},{56,48},{64,56},{72,6... | collective-permute-start | bytes 3317768 | tf_op jit(solution)/shard_map/ppermute | solution.py:382
  108.3 0.0 copy-done
  108.4 0.1 dynamic-slice_bitcast_fusion
  108.4 0.1 copy.20
  108.5 0.6 pad.4.clone
  109.2 4.6 %shard_map.92 = (f32[8,3,120,128]{3,2,1,0:T(8,128)}, f32[8,8,384]{2,1,0:T(8,128)}, f32[8,8,384]{2,1,0:T(8,128)}) custom-call(f32[64,384]{1,0:T(8,128)} %bitcast.27, s32[8,384]{1,0:T(8,128)} %pbl.3, s32[8,384]{1,0:T(8,128)} %land.1, f32[120,16]{1,0:T(8,128)} %bitcast.29), custom_call_target="tpu_custom_call" | custom-call | tf_op jit(solution)/shard_map/pallas_call | solution.py:363
  113.8 5.3 %collective-permute-done.2.up = f32[6,3,120,128]{3,2,1,0:T(8,128)S(1)} collective-permute-done((f32[6,3,120,128]{3,2,1,0:T(8,128)}, f32[6,3,120,128]{3,2,1,0:T(8,128)S(1)}, u32[]{:S(2)}, u32[]{:S(2)}) %collective-permute-start.2) | collective-permute-done | bytes 1105952 | tf_op jit(solution)/shard_map/ppermute | solution.py:381
  119.1 0.0 copy-start.4
  119.1 5.5 %collective-permute-done.3.down = f32[6,3,120,128]{3,2,1,0:T(8,128)S(1)} collective-permute-done((f32[6,3,120,128]{3,2,1,0:T(8,128)}, f32[6,3,120,128]{3,2,1,0:T(8,128)S(1)}, u32[]{:S(2)}, u32[]{:S(2)}) %collective-permute-start.3) | collective-permute-done | bytes 1105952 | tf_op jit(solution)/shard_map/ppermute | solution.py:382
  124.6 0.0 copy-done.4
  124.6 0.0 copy-start.5
  124.6 1.0 copy-done.5
  125.6 12.9 %shard_map.91 = f32[8,1,3,120,128]{4,3,2,1,0:T(8,128)} custom-call(f32[8,2,3,120,128]{4,3,2,1,0:T(8,128)} %all_to_all.15.x.own, f32[6,3,120,128]{3,2,1,0:T(8,128)} %copy-done.4, f32[6,3,120,128]{3,2,1,0:T(8,128)} %copy-done.5, f32[7,3,120,128]{3,2,1,0:T(8,128)} %copy-done.2, f32[7,3,120,128]{3,2,1,0:T(8,128)} %copy-done.3, ...), custom_call_target="tpu_custom_call" | custom-call | tf_op jit(solution)/shard_map/pallas_call | solution.py:341
  138.5 0.0 all-to-all-done.2
  138.5 5.4 %shard_map.93 = (f32[1920,384]{1,0:T(8,128)}, f32[240,384]{1,0:T(8,128)}) custom-call(f32[8,3,120,128]{3,2,1,0:T(8,128)} %bitcast.5.even, f32[8,3,120,128]{3,2,1,0:T(8,128)} %bitcast.25, f32[8,3,120,128]{3,2,1,0:T(8,128)} %get-tuple-element.15.keep, f32[8,8,384]{2,1,0:T(8,128)} %get-tuple-element.16.weven, f32[8,8,384]{2,1,0:T(8,128)} %get-tuple-element.17.wodd, ...), custom_call_target="tpu_custom_call" | custom-call | tf_op jit(solution)/shard_map/pallas_call | solution.py:387
Async XLA Ops:
  0.6 107.7 %copy-start = (f32[11,240]{1,0:T(8,128)S(1)}, f32[11,240]{1,0:T(8,128)}, u32[]{:S(2)}) copy-start(f32[11,240]{1,0:T(8,128)} %param.12) | copy-start | bytes 31684
  4.6 19.9 %collective-permute-start = (f32[7,3,120,128]{3,2,1,0:T(8,128)}, f32[7,3,120,128]{3,2,1,0:T(8,128)S(1)}, u32[]{:S(2)}, u32[]{:S(2)}) collective-permute-start(f32[7,3,120,128]{3,2,1,0:T(8,128)} %get-tuple-element.12), channel_id=1, source_target_pairs={{0,8},{8,16},{16,24},{24,32},{32,40},{40,48},{48,56},{56,64},{64,7... | collective-permute-start | bytes 3870728 | tf_op jit(solution)/shard_map/ppermute | solution.py:307
  9.9 20.5 %collective-permute-start.1 = (f32[7,3,120,128]{3,2,1,0:T(8,128)}, f32[7,3,120,128]{3,2,1,0:T(8,128)S(1)}, u32[]{:S(2)}, u32[]{:S(2)}) collective-permute-start(f32[7,3,120,128]{3,2,1,0:T(8,128)} %get-tuple-element.13), channel_id=1, source_target_pairs={{8,0},{16,8},{24,16},{32,24},{40,32},{48,40},{56,48},{64,56},{72,6... | collective-permute-start | bytes 3870728 | tf_op jit(solution)/shard_map/ppermute | solution.py:308
  15.3 30.2 %all-to-all-start = ((f32[8,3,120,128]{3,2,1,0:T(8,128)}), f32[8,3,120,128]{3,2,1,0:T(8,128)}, u32[]{:S(2)}, u32[]{:S(2)}) async-start(f32[8,3,120,128]{3,2,1,0:T(8,128)} %shard_map.86), calls=%async_computation | async-start | bytes 2949120 | tf_op jit(solution)/shard_map/all_to_all | solution.py:318
  24.5 5.9 %copy-start.2 = (f32[7,3,120,128]{3,2,1,0:T(8,128)}, f32[7,3,120,128]{3,2,1,0:T(8,128)S(1)}, u32[]{:S(2)}) copy-start(f32[7,3,120,128]{3,2,1,0:T(8,128)S(1)} %collective-permute-done.up.cup) | copy-start | bytes 3870724
  30.4 1.1 copy-start.3
  91.8 7.1 %copy-start.1 = (f32[8,2,3,120,128]{4,3,2,1,0:T(8,128)S(1)}, f32[8,2,3,120,128]{4,3,2,1,0:T(8,128)}, u32[]{:S(2)}) copy-start(f32[8,2,3,120,128]{4,3,2,1,0:T(8,128)} %all_to_all.15.x.own) | copy-start | bytes 8847364
  91.8 46.7 %all-to-all-start.2 = ((f32[8,1,3,120,128]{4,3,2,1,0:T(8,128)}), f32[8,1,3,120,128]{4,3,2,1,0:T(8,128)}, u32[]{:S(2)}, u32[]{:S(2)}) async-start(f32[8,1,3,120,128]{4,3,2,1,0:T(8,128)} %shard_map.90), calls=%async_computation.2 | async-start | bytes 2949120 | tf_op jit(solution)/shard_map/all_to_all | solution.py:318
  100.5 18.6 %collective-permute-start.2 = (f32[6,3,120,128]{3,2,1,0:T(8,128)}, f32[6,3,120,128]{3,2,1,0:T(8,128)S(1)}, u32[]{:S(2)}, u32[]{:S(2)}) collective-permute-start(f32[6,3,120,128]{3,2,1,0:T(8,128)} %get-tuple-element.21), channel_id=1, source_target_pairs={{0,8},{8,16},{16,24},{24,32},{32,40},{40,48},{48,56},{56,64},{64,7... | collective-permute-start | bytes 3317768 | tf_op jit(solution)/shard_map/ppermute | solution.py:381
  106.4 18.2 %collective-permute-start.3 = (f32[6,3,120,128]{3,2,1,0:T(8,128)}, f32[6,3,120,128]{3,2,1,0:T(8,128)S(1)}, u32[]{:S(2)}, u32[]{:S(2)}) collective-permute-start(f32[6,3,120,128]{3,2,1,0:T(8,128)} %get-tuple-element.20), channel_id=1, source_target_pairs={{8,0},{16,8},{24,16},{32,24},{40,32},{48,40},{56,48},{64,56},{72,6... | collective-permute-start | bytes 3317768 | tf_op jit(solution)/shard_map/ppermute | solution.py:382
  119.1 5.5 %copy-start.4 = (f32[6,3,120,128]{3,2,1,0:T(8,128)}, f32[6,3,120,128]{3,2,1,0:T(8,128)S(1)}, u32[]{:S(2)}) copy-start(f32[6,3,120,128]{3,2,1,0:T(8,128)S(1)} %collective-permute-done.2.up) | copy-start | bytes 3317764
  124.6 1.0 copy-start.5

commit v5 on v4

--- a/solution.py
+++ b/solution.py
@@ -12,11 +12,27 @@
 F32 = jnp.float32
 BF16 = jnp.bfloat16
 TAPS = 7
+GRANT = 48 << 20
 HALO = 6
 
 
-def call(body, out_shape, **kw):
-    return pl.pallas_call(body, out_shape=out_shape, interpret=INTERPRET, **kw)
+def near(array):
+    return array if INTERPRET else pltpu.with_memory_space_constraint(array, pltpu.VMEM)
+
+
+def far(array):
+    return array if INTERPRET else pltpu.with_memory_space_constraint(array, pltpu.HBM)
+
+
+def far_shape(shape):
+    return jax.ShapeDtypeStruct(shape, F32) if INTERPRET else pltpu.HBM(shape, F32)
+
+
+def call(body, out_shape, grant=None, **kw):
+    params = pltpu.CompilerParams(vmem_limit_bytes=grant)
+    return pl.pallas_call(
+        body, out_shape=out_shape, interpret=INTERPRET, compiler_params=params, **kw
+    )
 
 
 def pack_even(x, cf, own, up, down, speeds):
@@ -198,22 +214,37 @@
     return top, (value - top.astype(F32)).astype(BF16)
 
 
-def couple(x, matrix, *refs):
-    out, wide = refs[-2:]
+def couple(index, place, x, matrix, *refs):
+    out, wide, line, come, go = refs[-5:]
     species = matrix.shape[0]
-    x = x.reshape(species * 4, 128)
-    out = out.reshape(species * 4, 128)
-    for j in range(4):
-        wide[:, j * 128 : j * 128 + 128] = x[pl.ds(j, species, stride=4), :]
-    value = wide[...]
-    top, rest = halves(value)
+    rows, strips, width = x.shape[0], x.shape[2], x.shape[3]
+
+    def part(t, d):
+        return line.at[t, pl.ds(d * width, width)]
+
+    blocks = [(t, d) for t in range(strips) for d in range(rows)]
+    inward = {k: pltpu.make_async_copy(x.at[k[1], index, k[0]], part(*k), come.at[*k]) for k in blocks}
+    outward = {k: pltpu.make_async_copy(part(*k), out.at[k[1], place, k[0]], go.at[*k]) for k in blocks}
+    for k in blocks:
+        inward[k].start()
     high, low = halves(matrix[...])
-    total = jnp.dot(high, top, preferred_element_type=F32)
-    total += jnp.dot(high, rest, preferred_element_type=F32)
-    total += jnp.dot(low, top, preferred_element_type=F32)
-    wide[...] = value + total
-    for j in range(4):
-        out[pl.ds(j, species, stride=4), :] = wide[:, j * 128 : j * 128 + 128]
+    for t in range(strips):
+        for d in range(rows):
+            inward[t, d].wait()
+        for j in range(4):
+            wide[:, j * 128 : j * 128 + 128] = line.at[t][pl.ds(j, species, stride=4), :]
+        value = wide[...]
+        top, rest = halves(value)
+        total = jnp.dot(high, top, preferred_element_type=F32)
+        total += jnp.dot(high, rest, preferred_element_type=F32)
+        total += jnp.dot(low, top, preferred_element_type=F32)
+        wide[...] = value + total
+        for j in range(4):
+            line.at[t][pl.ds(j, species, stride=4), :] = wide[:, j * 128 : j * 128 + 128]
+        for d in range(rows):
+            outward[t, d].start()
+    for k in blocks:
+        outward[k].wait()
 
 
 def prepare(lm, pbl, land, rates, keep, weven, wodd):
@@ -240,6 +271,7 @@
 
 
 def finish(even, odd, keep, weven, wodd, pbl, lm, out, dep, flux):
+    t = pl.program_id(0)
     ny = even.shape[3]
     width = even.shape[2]
     sub = lax.broadcasted_iota(jnp.int32, (8, ny), 0)
@@ -250,7 +282,7 @@
         top = pbl[r : r + 1, :]
         for i in range(width // 8):
             at = slice(i * 8, i * 8 + 8)
-            a, b = even[r, 0, at, :], odd[r, 0, at, :]
+            a, b = even[r, t, at, :], odd[r, 0, at, :]
             total = weven[r] * a + wodd[r] * b
             total += jnp.where(first, pltpu.roll(total, 7, 0), pltpu.roll(total, 1, 0))
             total += jnp.where(low, pltpu.roll(total, 6, 0), pltpu.roll(total, 2, 0))
@@ -317,32 +349,36 @@
     def exchange(a):
         return lax.all_to_all(a, "spec", split_axis=0, concat_axis=0, tiled=True)
 
-    pair = sds((rows, 2, strips, width, 128), F32)
-
-    def half(index):
-        return pl.BlockSpec((rows, 1, 1, width, 128), lambda t: (0, index, t, 0, 0))
-
-    def coupled(a, index, shape, out_index, *into):
-        whole = pl.BlockSpec((species, species), lambda t: (0, 0))
+    pair = far_shape((rows, 2, strips, width, 128))
+
+    whole = pl.BlockSpec(memory_space=pltpu.VMEM)
+    anywhere = pl.BlockSpec(memory_space=pl.ANY)
+    far_spec = anywhere if INTERPRET else pl.BlockSpec(memory_space=pltpu.HBM)
+
+    def coupled(a, index, shape, place, *into):
         return call(
-            couple,
+            functools.partial(couple, index, place),
             shape,
-            grid=(strips,),
-            in_specs=[half(index), whole] + [pl.BlockSpec(memory_space=pl.ANY)] * len(into),
-            out_specs=half(out_index),
-            scratch_shapes=[pltpu.VMEM((species, 512), F32)],
+            in_specs=[anywhere, whole] + [far_spec] * len(into),
+            out_specs=far_spec,
+            scratch_shapes=[
+                pltpu.VMEM((species, 512), F32),
+                pltpu.VMEM((strips, species * 4, 128), F32),
+                pltpu.SemaphoreType.DMA((strips, rows)),
+                pltpu.SemaphoreType.DMA((strips, rows)),
+            ],
             input_output_aliases={2: 0} if into else {},
         )(a, coupling, *into)
 
     cup, cdown = up, down
 
     def transported(parity, a, index, shape, before, after):
-        anywhere = pl.BlockSpec(memory_space=pl.ANY)
         return call(
             functools.partial(transport, parity, index),
             shape,
+            grant=GRANT,
             in_specs=[anywhere] * 6 + [pl.BlockSpec(memory_space=pltpu.SMEM)],
-            out_specs=anywhere,
+            out_specs=far_spec,
             scratch_shapes=[
                 pltpu.VMEM((20, strips, width, 128), F32),
                 pltpu.VMEM((2, 16, 8, ny), F32),
@@ -353,7 +389,7 @@
                 pltpu.VMEM((rows, strips, width, 128), F32),
                 pltpu.SemaphoreType.DMA((15,)),
             ],
-        )(a, before, after, cup, cdown, speeds, valid)
+        )(far(a) if index == 0 else a, before, after, cup, cdown, far(speeds), valid)
 
     start = lax.axis_index("spec") * own_species
     mine = lax.dynamic_slice_in_dim(rates, start, own_species, 1).T
@@ -373,7 +409,7 @@
         out_specs=[columns(rows), strip(rows, 8), strip(rows, 8)],
     )(lm, pbl_top, land_type, mine)
 
-    single = sds((rows, 1, strips, width, 128), F32)
+    single = far_shape((rows, 1, strips, width, 128))
     odd = exchange(odd)
     both = transported(0, even[:, None], 0, pair, up, down)
     both = coupled(odd[:, None], 0, pair, 1, both)
@@ -388,10 +424,10 @@
         finish,
         (sds((tracers.size // ny, ny), F32), sds((own_species * rows, ny), F32)),
         grid=(strips,),
-        in_specs=[columns(rows)] * 3 + [strip(rows, 8)] * 2 + [strip(rows)] * 2,
+        in_specs=[whole] + [columns(rows)] * 2 + [strip(rows, 8)] * 2 + [strip(rows)] * 2,
         out_specs=[strip(tracers.size // ny), strip(own_species * rows)],
         scratch_shapes=[pltpu.VMEM((width, 128), F32)],
-    )(even, odd, keep, weven, wodd, pbl_top, lm)
+    )(near(even), odd, keep, weven, wodd, pbl_top, lm)
     return (updated.reshape(tracers.shape), deposited.reshape(own_species, rows, ny))
 
 

time: 145 us -> 146 us (level)
    unnamed x13 -> x3, local copies, waits for them, and re-layouts: 2.19 us -> 0.11 us
    squeeze x1, local copies, waits for them, and re-layouts: 1.52 us -> 3.15 us  [on_device(): down = lax.ppermute(both[:HALO, 1], 'space', down_pairs)]
  transfers between devices with their start and end apart: 6 -> 6, of which waited for: 4 -> 4; matrix products, arithmetic and copies ran while one was open for 2% -> 3% of each run, Pallas kernels for 24% -> 24%
where the time goes in v5:
time: 146 us; the launch traced here: 144 us
  Pallas kernels  53.1 us (36%)
  blocking collectives  39 us (27%)
  starting transfers between devices  28.5 us (20%)
  waiting for transfers between devices  19.1 us (13%)
  local copies, waits for them, and re-layouts  3.98 us (3%)
    all_to_all x1, blocking collectives, exchange(): return lax.all_to_all(a, 'spec', split_axis=0, concat_axis=0, tiled=True)  39 us
    pallas_call x2, Pallas kernels, transported(): call(functools.partial(transport, parity, index), shape, grant=GRANT, in_...  26.8 us
    all_to_all x2, starting transfers between devices, exchange(): return lax.all_to_all(a, 'spec', split_axis=0, concat_axis=0, tiled=True)  13.7 us
    pallas_call x2, Pallas kernels, coupled(): call(functools.partial(couple, index, place), shape, in_specs=[anywhere,...  8.64 us
    ppermute x1, waiting for transfers between devices, on_device(): down = lax.ppermute(send_down, 'space', down_pairs)  5.9 us
    pallas_call x1, Pallas kernels, on_device(): call(finish, (sds((tracers.size // ny, ny), F32), sds((own_species * rows...  5.65 us
    ppermute x1, waiting for transfers between devices, on_device(): down = lax.ppermute(both[:HALO, 1], 'space', down_pairs)  5.61 us
    ppermute x1, starting transfers between devices, on_device(): up = lax.ppermute(both[2:, 1], 'space', up_pairs)  5.58 us
  transfers between devices with their start and end apart: 6, of which 4 were waited for; matrix products, arithmetic and copies ran while one was open for 3% of the time, Pallas kernels for 24%

profile of v5, /device:TPU:101, one launch (start us, length us, event | category | flops | bytes accessed | tf_op | source)
XLA Modules:
  0.0 144.4 jit_solution(832274769708020857)
XLA Ops:
  0.6 0.0 copy-start
  0.6 3.9 %shard_map.87 = (f32[8,3,120,128]{3,2,1,0:T(8,128)}, f32[7,3,120,128]{3,2,1,0:T(8,128)}, f32[7,3,120,128]{3,2,1,0:T(8,128)}, f32[2,2,8,8,384]{4,3,2,1,0:T(8,128)}) custom-call(f32[30,4,2,8,384]{4,3,2,1,0:T(8,128)} %bitcast.23, f32[128,384]{1,0:T(8,128)} %bitcast.30), custom_call_target="tpu_custom_call" | custom-call | tf_op jit(solution)/shard_map/pallas_call | solution.py:327
  4.6 5.3 %collective-permute-start = (f32[7,3,120,128]{3,2,1,0:T(8,128)}, f32[7,3,120,128]{3,2,1,0:T(8,128)S(1)}, u32[]{:S(2)}, u32[]{:S(2)}) collective-permute-start(f32[7,3,120,128]{3,2,1,0:T(8,128)} %get-tuple-element.12), channel_id=1, source_target_pairs={{0,8},{8,16},{16,24},{24,32},{32,40},{40,48},{48,56},{56,64},{64,7... | collective-permute-start | bytes 3870728 | tf_op jit(solution)/shard_map/ppermute | solution.py:339
  9.9 1.9 %collective-permute-start.1 = (f32[7,3,120,128]{3,2,1,0:T(8,128)}, f32[7,3,120,128]{3,2,1,0:T(8,128)S(1)}, u32[]{:S(2)}, u32[]{:S(2)}) collective-permute-start(f32[7,3,120,128]{3,2,1,0:T(8,128)} %get-tuple-element.13), channel_id=1, source_target_pairs={{8,0},{16,8},{24,16},{32,24},{40,32},{48,40},{56,48},{64,56},{72,6... | collective-permute-start | bytes 3870728 | tf_op jit(solution)/shard_map/ppermute | solution.py:340
  11.8 3.5 %shard_map.86 = f32[8,3,120,128]{3,2,1,0:T(8,128)} custom-call(f32[30,4,2,8,384]{4,3,2,1,0:T(8,128)} %bitcast.24), custom_call_target="tpu_custom_call" | custom-call | tf_op jit(solution)/shard_map/pallas_call | solution.py:341
  15.3 6.9 %all-to-all-start = ((f32[8,3,120,128]{3,2,1,0:T(8,128)}), f32[8,3,120,128]{3,2,1,0:T(8,128)}, u32[]{:S(2)}, u32[]{:S(2)}) async-start(f32[8,3,120,128]{3,2,1,0:T(8,128)} %shard_map.86), calls=%async_computation | async-start | bytes 2949120 | tf_op jit(solution)/shard_map/all_to_all | solution.py:350
  22.2 2.4 %collective-permute-done.up.cup = f32[7,3,120,128]{3,2,1,0:T(8,128)S(1)} collective-permute-done((f32[7,3,120,128]{3,2,1,0:T(8,128)}, f32[7,3,120,128]{3,2,1,0:T(8,128)S(1)}, u32[]{:S(2)}, u32[]{:S(2)}) %collective-permute-start) | collective-permute-done | bytes 1290272 | tf_op jit(solution)/shard_map/ppermute | solution.py:339
  24.5 5.9 %collective-permute-done.1.down.cdown = f32[7,3,120,128]{3,2,1,0:T(8,128)S(1)} collective-permute-done((f32[7,3,120,128]{3,2,1,0:T(8,128)}, f32[7,3,120,128]{3,2,1,0:T(8,128)S(1)}, u32[]{:S(2)}, u32[]{:S(2)}) %collective-permute-start.1) | collective-permute-done | bytes 1290272 | tf_op jit(solution)/shard_map/ppermute | solution.py:340
  30.4 13.9 %shard_map.88.refs_0_ = f32[8,2,3,120,128]{4,3,2,1,0:T(8,128)} custom-call(f32[8,1,3,120,128]{4,3,2,1,0:T(8,128)} %bitcast.26, f32[7,3,120,128]{3,2,1,0:T(8,128)S(1)} %collective-permute-done.up.cup, f32[7,3,120,128]{3,2,1,0:T(8,128)S(1)} %collective-permute-done.1.down.cdown, f32[7,3,120,128]{3,2,1,0:T(8,128)S(1)} %collective-permute-done.up.cup, ...), custom_call_target="tpu_custom_call" | custom-call | tf_op jit(solution)/shard_map/pallas_call | solution.py:376
  44.3 0.0 all-to-all-done
  44.3 4.3 %shard_map.89 = f32[8,2,3,120,128]{4,3,2,1,0:T(8,128)} custom-call(f32[8,1,3,120,128]{4,3,2,1,0:T(8,128)} %bitcast.1.x, f32[240,240]{1,0:T(8,128)} %matrix.3, f32[8,2,3,120,128]{4,3,2,1,0:T(8,128)} %shard_map.88.refs_0_), custom_call_target="tpu_custom_call", output_to_operand_aliasing={{}: (2, {})} | custom-call | tf_op jit(solution)/shard_map/pallas_call | solution.py:359
  48.6 39.0 %all_to_all.15.x.own = f32[8,2,3,120,128]{4,3,2,1,0:T(8,128)} all-to-all(f32[8,2,3,120,128]{4,3,2,1,0:T(8,128)} %shard_map.89), channel_id=1, replica_groups=mesh['space'=32,'spec'=8] {'spec'}, dimensions={0} | all-to-all | bytes 5898240 | tf_op jit(solution)/shard_map/all_to_all | solution.py:350
  87.6 4.3 %shard_map.90 = f32[8,1,3,120,128]{4,3,2,1,0:T(8,128)} custom-call(f32[8,2,3,120,128]{4,3,2,1,0:T(8,128)} %all_to_all.15.x.own, f32[240,240]{1,0:T(8,128)} %matrix.3), custom_call_target="tpu_custom_call" | custom-call | tf_op jit(solution)/shard_map/pallas_call | solution.py:359
  91.9 6.9 %all-to-all-start.2 = ((f32[8,1,3,120,128]{4,3,2,1,0:T(8,128)}), f32[8,1,3,120,128]{4,3,2,1,0:T(8,128)}, u32[]{:S(2)}, u32[]{:S(2)}) async-start(f32[8,1,3,120,128]{4,3,2,1,0:T(8,128)} %shard_map.90), calls=%async_computation.2 | async-start | bytes 2949120 | tf_op jit(solution)/shard_map/all_to_all | solution.py:350
  98.8 3.2 %slice_bitcast_fusion = (f32[6,3,120,128]{3,2,1,0:T(8,128)}, f32[6,3,120,128]{3,2,1,0:T(8,128)}) fusion(f32[8,2,3,120,128]{4,3,2,1,0:T(8,128)} %all_to_all.15.x.own), kind=kLoop, calls=%fused_computation | loop fusion | bytes 4423680 | tf_op jit(solution)/shard_map/squeeze | solution.py:418
  102.0 5.6 %collective-permute-start.2 = (f32[6,3,120,128]{3,2,1,0:T(8,128)}, f32[6,3,120,128]{3,2,1,0:T(8,128)}, u32[]{:S(2)}, u32[]{:S(2)}) collective-permute-start(f32[6,3,120,128]{3,2,1,0:T(8,128)} %get-tuple-element.21), channel_id=1, source_target_pairs={{0,8},{8,16},{16,24},{24,32},{32,40},{40,48},{48,56},{56,64},{64,7... | collective-permute-start | bytes 3317768 | tf_op jit(solution)/shard_map/ppermute | solution.py:417
  107.5 1.9 %collective-permute-start.3 = (f32[6,3,120,128]{3,2,1,0:T(8,128)}, f32[6,3,120,128]{3,2,1,0:T(8,128)}, u32[]{:S(2)}, u32[]{:S(2)}) collective-permute-start(f32[6,3,120,128]{3,2,1,0:T(8,128)} %get-tuple-element.20), channel_id=1, source_target_pairs={{8,0},{16,8},{24,16},{32,24},{40,32},{48,40},{56,48},{64,56},{72,6... | collective-permute-start | bytes 3317768 | tf_op jit(solution)/shard_map/ppermute | solution.py:418
  109.5 0.0 copy-done
  109.5 0.1 dynamic-slice_bitcast_fusion
  109.6 0.1 copy.20
  109.7 0.6 pad.4.clone
  110.3 4.6 %shard_map.92 = (f32[8,3,120,128]{3,2,1,0:T(8,128)}, f32[8,8,384]{2,1,0:T(8,128)}, f32[8,8,384]{2,1,0:T(8,128)}) custom-call(f32[64,384]{1,0:T(8,128)} %bitcast.27, s32[8,384]{1,0:T(8,128)} %pbl.3, s32[8,384]{1,0:T(8,128)} %land.1, f32[120,16]{1,0:T(8,128)} %bitcast.29), custom_call_target="tpu_custom_call" | custom-call | tf_op jit(solution)/shard_map/pallas_call | solution.py:399
  114.9 5.2 %collective-permute-done.2.up = f32[6,3,120,128]{3,2,1,0:T(8,128)} collective-permute-done((f32[6,3,120,128]{3,2,1,0:T(8,128)}, f32[6,3,120,128]{3,2,1,0:T(8,128)}, u32[]{:S(2)}, u32[]{:S(2)}) %collective-permute-start.2) | collective-permute-done | bytes 1105952 | tf_op jit(solution)/shard_map/ppermute | solution.py:417
  120.2 5.6 %collective-permute-done.3.down = f32[6,3,120,128]{3,2,1,0:T(8,128)} collective-permute-done((f32[6,3,120,128]{3,2,1,0:T(8,128)}, f32[6,3,120,128]{3,2,1,0:T(8,128)}, u32[]{:S(2)}, u32[]{:S(2)}) %collective-permute-start.3) | collective-permute-done | bytes 1105952 | tf_op jit(solution)/shard_map/ppermute | solution.py:418
  125.8 12.9 %shard_map.91 = f32[8,1,3,120,128]{4,3,2,1,0:T(8,128)} custom-call(f32[8,2,3,120,128]{4,3,2,1,0:T(8,128)} %all_to_all.15.x.own, f32[6,3,120,128]{3,2,1,0:T(8,128)} %collective-permute-done.2.up, f32[6,3,120,128]{3,2,1,0:T(8,128)} %collective-permute-done.3.down, f32[7,3,120,128]{3,2,1,0:T(8,128)S(1)} %collective-permute-done.up.cup, ...), custom_call_target="tpu_custom_call" | custom-call | tf_op jit(solution)/shard_map/pallas_call | solution.py:376
  138.7 0.0 all-to-all-done.2
  138.7 5.7 %shard_map.93 = (f32[1920,384]{1,0:T(8,128)}, f32[240,384]{1,0:T(8,128)}) custom-call(f32[8,3,120,128]{3,2,1,0:T(8,128)} %bitcast.5.even, f32[8,3,120,128]{3,2,1,0:T(8,128)} %bitcast.25, f32[8,3,120,128]{3,2,1,0:T(8,128)} %get-tuple-element.15.keep, f32[8,8,384]{2,1,0:T(8,128)} %get-tuple-element.16.weven, f32[8,8,384]{2,1,0:T(8,128)} %get-tuple-element.17.wodd, ...), custom_call_target="tpu_custom_call" | custom-call | tf_op jit(solution)/shard_map/pallas_call | solution.py:423
Async XLA Ops:
  0.6 108.8 %copy-start = (f32[11,240]{1,0:T(8,128)S(1)}, f32[11,240]{1,0:T(8,128)}, u32[]{:S(2)}) copy-start(f32[11,240]{1,0:T(8,128)} %param.12) | copy-start | bytes 31684
  4.6 19.9 %collective-permute-start = (f32[7,3,120,128]{3,2,1,0:T(8,128)}, f32[7,3,120,128]{3,2,1,0:T(8,128)S(1)}, u32[]{:S(2)}, u32[]{:S(2)}) collective-permute-start(f32[7,3,120,128]{3,2,1,0:T(8,128)} %get-tuple-element.12), channel_id=1, source_target_pairs={{0,8},{8,16},{16,24},{24,32},{32,40},{40,48},{48,56},{56,64},{64,7... | collective-permute-start | bytes 3870728 | tf_op jit(solution)/shard_map/ppermute | solution.py:339
  9.9 20.5 %collective-permute-start.1 = (f32[7,3,120,128]{3,2,1,0:T(8,128)}, f32[7,3,120,128]{3,2,1,0:T(8,128)S(1)}, u32[]{:S(2)}, u32[]{:S(2)}) collective-permute-start(f32[7,3,120,128]{3,2,1,0:T(8,128)} %get-tuple-element.13), channel_id=1, source_target_pairs={{8,0},{16,8},{24,16},{32,24},{40,32},{48,40},{56,48},{64,56},{72,6... | collective-permute-start | bytes 3870728 | tf_op jit(solution)/shard_map/ppermute | solution.py:340
  15.3 29.0 %all-to-all-start = ((f32[8,3,120,128]{3,2,1,0:T(8,128)}), f32[8,3,120,128]{3,2,1,0:T(8,128)}, u32[]{:S(2)}, u32[]{:S(2)}) async-start(f32[8,3,120,128]{3,2,1,0:T(8,128)} %shard_map.86), calls=%async_computation | async-start | bytes 2949120 | tf_op jit(solution)/shard_map/all_to_all | solution.py:350
  91.9 46.8 %all-to-all-start.2 = ((f32[8,1,3,120,128]{4,3,2,1,0:T(8,128)}), f32[8,1,3,120,128]{4,3,2,1,0:T(8,128)}, u32[]{:S(2)}, u32[]{:S(2)}) async-start(f32[8,1,3,120,128]{4,3,2,1,0:T(8,128)} %shard_map.90), calls=%async_computation.2 | async-start | bytes 2949120 | tf_op jit(solution)/shard_map/all_to_all | solution.py:350
  102.0 18.2 %collective-permute-start.2 = (f32[6,3,120,128]{3,2,1,0:T(8,128)}, f32[6,3,120,128]{3,2,1,0:T(8,128)}, u32[]{:S(2)}, u32[]{:S(2)}) collective-permute-start(f32[6,3,120,128]{3,2,1,0:T(8,128)} %get-tuple-element.21), channel_id=1, source_target_pairs={{0,8},{8,16},{16,24},{24,32},{32,40},{40,48},{48,56},{56,64},{64,7... | collective-permute-start | bytes 3317768 | tf_op jit(solution)/shard_map/ppermute | solution.py:417
  107.5 18.3 %collective-permute-start.3 = (f32[6,3,120,128]{3,2,1,0:T(8,128)}, f32[6,3,120,128]{3,2,1,0:T(8,128)}, u32[]{:S(2)}, u32[]{:S(2)}) collective-permute-start(f32[6,3,120,128]{3,2,1,0:T(8,128)} %get-tuple-element.20), channel_id=1, source_target_pairs={{8,0},{16,8},{24,16},{32,24},{40,32},{48,40},{56,48},{64,56},{72,6... | collective-permute-start | bytes 3317768 | tf_op jit(solution)/shard_map/ppermute | solution.py:418

commit v6 on v5

--- a/solution.py
+++ b/solution.py
@@ -44,18 +44,20 @@
             rows = slice(i * 8, i * 8 + 8)
             own[r, 0, rows, :] = value
             if r >= 2:
-                up[r - 2, 0, rows, :] = value
+                at = (r - 2) * width + i * 8
+                up[0, at : at + 8, :] = value
             if r < 6:
-                down[r, 0, rows, :] = value
+                at = r * width + i * 8
+                down[0, at : at + 8, :] = value
     for d in range(2):
         for parity in range(2):
             for row in range(4):
-                at = ((d * 2 + parity) * 4 + row) * 4
+                at = HALO * width + ((d * 2 + parity) * 4 + row) * 4
                 start = d * 64 + parity * 8 + row
                 before = cf[pl.ds(start, 4, stride=16), :]
                 after = cf[pl.ds(start + 4, 4, stride=16), :]
-                down[HALO, 0, at : at + 4, :] = before
-                up[HALO, 0, at : at + 4, :] = after
+                down[0, at : at + 4, :] = before
+                up[0, at : at + 4, :] = after
                 for half in (slice(0, 4), slice(4, 8)):
                     speeds[parity, d, row, half, :] = before
                     speeds[parity, d, row + 4, half, :] = after
@@ -108,15 +110,20 @@
     width = own.shape[3]
     strips = own.shape[2]
     ny = strips * 128
-    group = 8
+    group = 24
+    tail = pl.ds(HALO * width, 64)
     moves = [
         pltpu.make_async_copy(cf.at[parity], c.at[:, pl.ds(4, 8)], sems.at[0]),
-        pltpu.make_async_copy(cup.at[HALO, :, pl.ds(0, 64)], ends.at[0], sems.at[1]),
-        pltpu.make_async_copy(cdown.at[HALO, :, pl.ds(0, 64)], ends.at[1], sems.at[2]),
-        pltpu.make_async_copy(up.at[pl.ds(0, HALO)], q.at[pl.ds(0, HALO)], sems.at[3]),
-        pltpu.make_async_copy(own.at[:, index], q.at[pl.ds(HALO, 8)], sems.at[4]),
-        pltpu.make_async_copy(down.at[pl.ds(0, HALO)], q.at[pl.ds(HALO + 8, HALO)], sems.at[5]),
+        pltpu.make_async_copy(cup.at[:, tail], ends.at[0], sems.at[1]),
+        pltpu.make_async_copy(cdown.at[:, tail], ends.at[1], sems.at[2]),
+        pltpu.make_async_copy(own.at[:, index], q.at[pl.ds(HALO, 8)], sems.at[3]),
     ]
+    for row in range(HALO):
+        span = pl.ds(row * width, width)
+        before = up.at[:, span] if index == 0 else up.at[row]
+        after = down.at[:, span] if index == 0 else down.at[row]
+        moves.append(pltpu.make_async_copy(before, q.at[row], sems.at[4 + row]))
+        moves.append(pltpu.make_async_copy(after, q.at[HALO + 8 + row], sems.at[10 + row]))
     for move in moves:
         move.start()
     for move in moves[:3]:
@@ -143,10 +150,6 @@
         for k, w in enumerate(cell_taps(low, high)):
             shift = k - 3
             w = jnp.where((lane + shift >= 0) & (lane + shift < ny), w, 0.0)
-            if shift >= 2:
-                w = pltpu.roll(w, 3, 1)
-            if shift <= -2:
-                w = pltpu.roll(w, ny - 3, 1)
             wy[row, k] = w
         return carry
 
@@ -156,15 +159,13 @@
     parts = range(group // 8)
 
     def across(values, row):
-        after = [pltpu.roll(v, ny - 1, 1) for v in values]
-        before = [pltpu.roll(v, 1, 1) for v in values]
-        w = [wy[row, k] for k in range(TAPS)]
-        totals = []
-        for v, p, m in zip(values, after, before):
-            total = w[3] * v + w[4] * p + w[2] * m
-            total += pltpu.roll(w[5] * m + w[6] * v, ny - 3, 1)
-            total += pltpu.roll(w[1] * p + w[0] * v, 3, 1)
-            totals.append(total)
+        w = wy[row, 3]
+        totals = [w * v for v in values]
+        for shift in (1, 2, 3):
+            w = wy[row, 3 + shift]
+            totals = [t + w * pltpu.roll(v, ny - shift, 1) for t, v in zip(totals, values)]
+            w = wy[row, 3 - shift]
+            totals = [t + w * pltpu.roll(v, shift, 1) for t, v in zip(totals, values)]
         return totals
 
     def along(read, row, base):
@@ -196,11 +197,10 @@
         for row in range(14):
             for u, v in enumerate(across(along(first, row, row), row)):
                 mid[row, u] = v
-            late = row - 6
-            if late >= 0:
-                for u, v in enumerate(across(along(second, late + 3, late), late + 3)):
-                    for t in range(strips):
-                        new[late, t, pl.ds(places[u], 8), :] = v[:, t * 128 : t * 128 + 128]
+        for row in range(8):
+            for u, v in enumerate(across(along(second, row + 3, row), row + 3)):
+                for t in range(strips):
+                    new[row, t, pl.ds(places[u], 8), :] = v[:, t * 128 : t * 128 + 128]
         back(i).start()
         return carry
 
@@ -311,7 +311,7 @@
 
     strips = ny // 128
     group = sds((rows, strips, width, 128), F32)
-    edge = sds((HALO + 1, strips, width, 128), F32)
+    edge = sds((strips, HALO * width + 64, 128), F32)
     speeds = sds((2, 2, rows, 8, ny), F32)
 
     def strip(*shape):
@@ -319,6 +319,8 @@
 
     def columns(count):
         return pl.BlockSpec((count, 1, width, 128), lambda t: (0, t, 0, 0))
+
+    ends = pl.BlockSpec((1, HALO * width + 64, 128), lambda t: (t, 0, 0))
 
     def level_group(parity):
         shape = (own_species, 4, 1, rows, 128)
@@ -331,8 +333,8 @@
         in_specs=[level_group(0), strip(cf.shape[0])],
         out_specs=[
             columns(rows),
-            columns(HALO + 1),
-            columns(HALO + 1),
+            ends,
+            ends,
             strip(2, 2, rows, 8),
         ],
     )(split, cf)
@@ -359,6 +361,7 @@
         return call(
             functools.partial(couple, index, place),
             shape,
+            grant=GRANT,
             in_specs=[anywhere, whole] + [far_spec] * len(into),
             out_specs=far_spec,
             scratch_shapes=[
@@ -385,9 +388,9 @@
                 pltpu.VMEM((2, strips, 64, 128), F32),
                 pltpu.VMEM((14, TAPS, 8, ny), F32),
                 pltpu.VMEM((14, TAPS, 8, ny), F32),
-                pltpu.VMEM((14, 1, 8, ny), F32),
+                pltpu.VMEM((14, 3, 8, ny), F32),
                 pltpu.VMEM((rows, strips, width, 128), F32),
-                pltpu.SemaphoreType.DMA((15,)),
+                pltpu.SemaphoreType.DMA((16,)),
             ],
         )(far(a) if index == 0 else a, before, after, cup, cdown, far(speeds), valid)
 
@@ -410,6 +413,7 @@
     )(lm, pbl_top, land_type, mine)
 
     single = far_shape((rows, 1, strips, width, 128))
+
     odd = exchange(odd)
     both = transported(0, even[:, None], 0, pair, up, down)
     both = coupled(odd[:, None], 0, pair, 1, both)

time: 146 us -> 151 us (1.034)
  waiting for transfers between devices: 19.1 us -> 28.1 us
  Pallas kernels: 53.1 us -> 48.4 us
    ppermute x1, waiting for transfers between devices: 2.36 us -> 11.8 us  [on_device(): up = lax.ppermute(send_up, 'space', up_pairs)]
    pallas_call x2, Pallas kernels: 26.8 us -> 23.1 us  [transported(): call(functools.partial(transport, parity, index), shape, grant=GRANT, in_...]
    unnamed x3 -> x15, local copies, waits for them, and re-layouts: 0.11 us -> 2.68 us
    squeeze x1, local copies, waits for them, and re-layouts: 3.15 us -> 1.55 us  [on_device(): down = lax.ppermute(both[:HALO, 1], 'space', down_pairs)]
  transfers between devices with their start and end apart: 6 -> 6, of which waited for: 4 -> 4; matrix products, arithmetic and copies ran while one was open for 3% -> 2% of each run, Pallas kernels for 24% -> 21%
where the time goes in v6:
time: 151 us; the launch traced here: 150 us
  Pallas kernels  48.4 us (32%)
  blocking collectives  38.7 us (26%)
  starting transfers between devices  29 us (19%)
  waiting for transfers between devices  28.1 us (19%)
  local copies, waits for them, and re-layouts  4.94 us (3%)
    all_to_all x1, blocking collectives, exchange(): return lax.all_to_all(a, 'spec', split_axis=0, concat_axis=0, tiled=True)  38.7 us
    pallas_call x2, Pallas kernels, transported(): call(functools.partial(transport, parity, index), shape, grant=GRANT, in_...  23.1 us
    all_to_all x2, starting transfers between devices, exchange(): return lax.all_to_all(a, 'spec', split_axis=0, concat_axis=0, tiled=True)  13.8 us
    ppermute x1, waiting for transfers between devices, on_device(): up = lax.ppermute(send_up, 'space', up_pairs)  11.8 us
    pallas_call x2, Pallas kernels, coupled(): call(functools.partial(couple, index, place), shape, grant=GRANT, in_spec...  7.71 us
    ppermute x1, starting transfers between devices, on_device(): up = lax.ppermute(send_up, 'space', up_pairs)  5.86 us
    pallas_call x1, Pallas kernels, on_device(): call(finish, (sds((tracers.size // ny, ny), F32), sds((own_species * rows...  5.65 us
    ppermute x1, starting transfers between devices, on_device(): up = lax.ppermute(both[2:, 1], 'space', up_pairs)  5.54 us
  transfers between devices with their start and end apart: 6, of which 4 were waited for; matrix products, arithmetic and copies ran while one was open for 2% of the time, Pallas kernels for 21%

profile of v6, /device:TPU:101, one launch (start us, length us, event | category | flops | bytes accessed | tf_op | source)
XLA Modules:
  0.0 149.8 jit_solution(8427703658734511761)
XLA Ops:
  0.6 0.0 copy-start
  0.6 3.4 %shard_map.86 = f32[8,3,120,128]{3,2,1,0:T(8,128)} custom-call(f32[30,4,2,8,384]{4,3,2,1,0:T(8,128)} %bitcast.23), custom_call_target="tpu_custom_call" | custom-call | tf_op jit(solution)/shard_map/pallas_call | solution.py:343
  4.1 6.9 %all-to-all-start = ((f32[8,3,120,128]{3,2,1,0:T(8,128)}), f32[8,3,120,128]{3,2,1,0:T(8,128)}, u32[]{:S(2)}, u32[]{:S(2)}) async-start(f32[8,3,120,128]{3,2,1,0:T(8,128)} %shard_map.86), calls=%async_computation | async-start | bytes 2949120 | tf_op jit(solution)/shard_map/all_to_all | solution.py:352
  11.0 3.9 %shard_map.87 = (f32[8,3,120,128]{3,2,1,0:T(8,128)}, f32[3,784,128]{2,1,0:T(8,128)}, f32[3,784,128]{2,1,0:T(8,128)}, f32[2,2,8,8,384]{4,3,2,1,0:T(8,128)}) custom-call(f32[30,4,2,8,384]{4,3,2,1,0:T(8,128)} %bitcast.24, f32[128,384]{1,0:T(8,128)} %bitcast.30), custom_call_target="tpu_custom_call" | custom-call | tf_op jit(solution)/shard_map/pallas_call | solution.py:329
  14.9 5.9 %collective-permute-start = (f32[3,784,128]{2,1,0:T(8,128)}, f32[3,784,128]{2,1,0:T(8,128)S(1)}, u32[]{:S(2)}, u32[]{:S(2)}) collective-permute-start(f32[3,784,128]{2,1,0:T(8,128)} %get-tuple-element.12), channel_id=1, source_target_pairs={{0,8},{8,16},{16,24},{24,32},{32,40},{40,48},{48,56},{56,64},{64,7... | collective-permute-start | bytes 3612680 | tf_op jit(solution)/shard_map/ppermute | solution.py:341
  20.7 1.9 %collective-permute-start.1 = (f32[3,784,128]{2,1,0:T(8,128)}, f32[3,784,128]{2,1,0:T(8,128)S(1)}, u32[]{:S(2)}, u32[]{:S(2)}) collective-permute-start(f32[3,784,128]{2,1,0:T(8,128)} %get-tuple-element.13), channel_id=1, source_target_pairs={{8,0},{16,8},{24,16},{32,24},{40,32},{48,40},{56,48},{64,56},{72,6... | collective-permute-start | bytes 3612680 | tf_op jit(solution)/shard_map/ppermute | solution.py:342
  22.7 11.8 %collective-permute-done.up.cup = f32[3,784,128]{2,1,0:T(8,128)S(1)} collective-permute-done((f32[3,784,128]{2,1,0:T(8,128)}, f32[3,784,128]{2,1,0:T(8,128)S(1)}, u32[]{:S(2)}, u32[]{:S(2)}) %collective-permute-start) | collective-permute-done | bytes 1204256 | tf_op jit(solution)/shard_map/ppermute | solution.py:341
  34.4 0.0 copy-start.2
  34.4 5.5 %collective-permute-done.1.down.cdown = f32[3,784,128]{2,1,0:T(8,128)S(1)} collective-permute-done((f32[3,784,128]{2,1,0:T(8,128)}, f32[3,784,128]{2,1,0:T(8,128)S(1)}, u32[]{:S(2)}, u32[]{:S(2)}) %collective-permute-start.1) | collective-permute-done | bytes 1204256 | tf_op jit(solution)/shard_map/ppermute | solution.py:342
  39.9 0.0 copy-start.4
  39.9 0.0 copy-start.6
  39.9 10.7 %shard_map.88.refs_0_ = f32[8,2,3,120,128]{4,3,2,1,0:T(8,128)} custom-call(f32[8,1,3,120,128]{4,3,2,1,0:T(8,128)} %bitcast.26, f32[3,784,128]{2,1,0:T(8,128)S(1)} %collective-permute-done.up.cup, f32[3,784,128]{2,1,0:T(8,128)S(1)} %collective-permute-done.1.down.cdown, f32[3,784,128]{2,1,0:T(8,128)S(1)} %collective-permute-done.up.cup, ...), custom_call_target="tpu_custom_call" | custom-call | tf_op jit(solution)/shard_map/pallas_call | solution.py:379
  50.6 0.0 copy-done.2
  50.6 0.0 copy-done.4
  50.6 0.0 all-to-all-done
  50.6 0.0 copy-done.6
  50.7 3.4 %shard_map.89 = f32[8,2,3,120,128]{4,3,2,1,0:T(8,128)} custom-call(f32[8,1,3,120,128]{4,3,2,1,0:T(8,128)} %bitcast.1.x, f32[240,240]{1,0:T(8,128)S(1)} %copy-done.6, f32[8,2,3,120,128]{4,3,2,1,0:T(8,128)} %shard_map.88.refs_0_), custom_call_target="tpu_custom_call", output_to_operand_aliasing={{}: (2, {})} | custom-call | tf_op jit(solution)/shard_map/pallas_call | solution.py:361
  54.0 38.7 %all_to_all.15.x.own = f32[8,2,3,120,128]{4,3,2,1,0:T(8,128)S(1)} all-to-all(f32[8,2,3,120,128]{4,3,2,1,0:T(8,128)} %shard_map.89), channel_id=1, replica_groups=mesh['space'=32,'spec'=8] {'spec'}, dimensions={0} | all-to-all | bytes 5898240 | tf_op jit(solution)/shard_map/all_to_all | solution.py:352
  92.7 0.0 copy-start.1
  92.7 4.3 %shard_map.90 = f32[8,1,3,120,128]{4,3,2,1,0:T(8,128)} custom-call(f32[8,2,3,120,128]{4,3,2,1,0:T(8,128)S(1)} %all_to_all.15.x.own, f32[240,240]{1,0:T(8,128)S(1)} %copy-done.6), custom_call_target="tpu_custom_call" | custom-call | tf_op jit(solution)/shard_map/pallas_call | solution.py:361
  97.0 6.9 %all-to-all-start.2 = ((f32[8,1,3,120,128]{4,3,2,1,0:T(8,128)}), f32[8,1,3,120,128]{4,3,2,1,0:T(8,128)}, u32[]{:S(2)}, u32[]{:S(2)}) async-start(f32[8,1,3,120,128]{4,3,2,1,0:T(8,128)} %shard_map.90), calls=%async_computation.2 | async-start | bytes 2949120 | tf_op jit(solution)/shard_map/all_to_all | solution.py:352
  103.9 0.0 copy-done.1
  103.9 1.5 %slice_bitcast_fusion = (f32[6,3,120,128]{3,2,1,0:T(8,128)}, f32[6,3,120,128]{3,2,1,0:T(8,128)}) fusion(f32[8,2,3,120,128]{4,3,2,1,0:T(8,128)S(1)} %all_to_all.15.x.own), kind=kLoop, calls=%fused_computation | loop fusion | bytes 4423680 | tf_op jit(solution)/shard_map/squeeze | solution.py:422
  105.5 5.5 %collective-permute-start.2 = (f32[6,3,120,128]{3,2,1,0:T(8,128)}, f32[6,3,120,128]{3,2,1,0:T(8,128)S(1)}, u32[]{:S(2)}, u32[]{:S(2)}) collective-permute-start(f32[6,3,120,128]{3,2,1,0:T(8,128)} %get-tuple-element.21), channel_id=1, source_target_pairs={{0,8},{8,16},{16,24},{24,32},{32,40},{40,48},{48,56},{56,64},{64,7... | collective-permute-start | bytes 3317768 | tf_op jit(solution)/shard_map/ppermute | solution.py:421
  111.0 1.9 %collective-permute-start.3 = (f32[6,3,120,128]{3,2,1,0:T(8,128)}, f32[6,3,120,128]{3,2,1,0:T(8,128)S(1)}, u32[]{:S(2)}, u32[]{:S(2)}) collective-permute-start(f32[6,3,120,128]{3,2,1,0:T(8,128)} %get-tuple-element.20), channel_id=1, source_target_pairs={{8,0},{16,8},{24,16},{32,24},{40,32},{48,40},{56,48},{64,56},{72,6... | collective-permute-start | bytes 3317768 | tf_op jit(solution)/shard_map/ppermute | solution.py:422
  113.0 0.0 copy-done
  113.0 0.1 dynamic-slice_bitcast_fusion
  113.1 0.1 copy.20
  113.2 0.6 pad.4.clone
  113.8 4.6 %shard_map.92 = (f32[8,3,120,128]{3,2,1,0:T(8,128)}, f32[8,8,384]{2,1,0:T(8,128)}, f32[8,8,384]{2,1,0:T(8,128)}) custom-call(f32[64,384]{1,0:T(8,128)} %bitcast.27, s32[8,384]{1,0:T(8,128)} %pbl.3, s32[8,384]{1,0:T(8,128)} %land.1, f32[120,16]{1,0:T(8,128)} %bitcast.29), custom_call_target="tpu_custom_call" | custom-call | tf_op jit(solution)/shard_map/pallas_call | solution.py:402
  118.4 5.3 %collective-permute-done.2.up = f32[6,3,120,128]{3,2,1,0:T(8,128)S(1)} collective-permute-done((f32[6,3,120,128]{3,2,1,0:T(8,128)}, f32[6,3,120,128]{3,2,1,0:T(8,128)S(1)}, u32[]{:S(2)}, u32[]{:S(2)}) %collective-permute-start.2) | collective-permute-done | bytes 1105952 | tf_op jit(solution)/shard_map/ppermute | solution.py:421
  123.7 5.5 %collective-permute-done.3.down = f32[6,3,120,128]{3,2,1,0:T(8,128)S(1)} collective-permute-done((f32[6,3,120,128]{3,2,1,0:T(8,128)}, f32[6,3,120,128]{3,2,1,0:T(8,128)S(1)}, u32[]{:S(2)}, u32[]{:S(2)}) %collective-permute-start.3) | collective-permute-done | bytes 1105952 | tf_op jit(solution)/shard_map/ppermute | solution.py:422
  129.2 0.0 copy-start.3
  129.2 1.3 copy-done.3
  130.5 0.0 copy-start.5
  130.5 1.3 copy-done.5
  131.7 12.4 %shard_map.91 = f32[8,1,3,120,128]{4,3,2,1,0:T(8,128)} custom-call(f32[8,2,3,120,128]{4,3,2,1,0:T(8,128)} %copy-done.1, f32[6,3,120,128]{3,2,1,0:T(8,128)S(1)} %collective-permute-done.2.up, f32[6,3,120,128]{3,2,1,0:T(8,128)S(1)} %collective-permute-done.3.down, f32[3,784,128]{2,1,0:T(8,128)S(1)} %copy-done.3, f32[3,784,128]{2,1,0:T(8,128)S(1)} %copy-done.5, ...), custom_call_target="tpu_custom_call" | custom-call | tf_op jit(solution)/shard_map/pallas_call | solution.py:379
  144.2 0.0 all-to-all-done.2
  144.2 5.7 %shard_map.93 = (f32[1920,384]{1,0:T(8,128)}, f32[240,384]{1,0:T(8,128)}) custom-call(f32[8,3,120,128]{3,2,1,0:T(8,128)} %bitcast.5.even, f32[8,3,120,128]{3,2,1,0:T(8,128)} %bitcast.25, f32[8,3,120,128]{3,2,1,0:T(8,128)} %get-tuple-element.15.keep, f32[8,8,384]{2,1,0:T(8,128)} %get-tuple-element.16.weven, f32[8,8,384]{2,1,0:T(8,128)} %get-tuple-element.17.wodd, ...), custom_call_target="tpu_custom_call" | custom-call | tf_op jit(solution)/shard_map/pallas_call | solution.py:427
Async XLA Ops:
  0.6 112.3 %copy-start = (f32[11,240]{1,0:T(8,128)S(1)}, f32[11,240]{1,0:T(8,128)}, u32[]{:S(2)}) copy-start(f32[11,240]{1,0:T(8,128)} %param.12) | copy-start | bytes 31684
  4.1 46.5 %all-to-all-start = ((f32[8,3,120,128]{3,2,1,0:T(8,128)}), f32[8,3,120,128]{3,2,1,0:T(8,128)}, u32[]{:S(2)}, u32[]{:S(2)}) async-start(f32[8,3,120,128]{3,2,1,0:T(8,128)} %shard_map.86), calls=%async_computation | async-start | bytes 2949120 | tf_op jit(solution)/shard_map/all_to_all | solution.py:352
  14.9 19.6 %collective-permute-start = (f32[3,784,128]{2,1,0:T(8,128)}, f32[3,784,128]{2,1,0:T(8,128)S(1)}, u32[]{:S(2)}, u32[]{:S(2)}) collective-permute-start(f32[3,784,128]{2,1,0:T(8,128)} %get-tuple-element.12), channel_id=1, source_target_pairs={{0,8},{8,16},{16,24},{24,32},{32,40},{40,48},{48,56},{56,64},{64,7... | collective-permute-start | bytes 3612680 | tf_op jit(solution)/shard_map/ppermute | solution.py:341
  20.7 19.2 %collective-permute-start.1 = (f32[3,784,128]{2,1,0:T(8,128)}, f32[3,784,128]{2,1,0:T(8,128)S(1)}, u32[]{:S(2)}, u32[]{:S(2)}) collective-permute-start(f32[3,784,128]{2,1,0:T(8,128)} %get-tuple-element.13), channel_id=1, source_target_pairs={{8,0},{16,8},{24,16},{32,24},{40,32},{48,40},{56,48},{64,56},{72,6... | collective-permute-start | bytes 3612680 | tf_op jit(solution)/shard_map/ppermute | solution.py:342
  34.4 16.2 %copy-start.2 = (f32[3,784,128]{2,1,0:T(8,128)}, f32[3,784,128]{2,1,0:T(8,128)S(1)}, u32[]{:S(2)}) copy-start(f32[3,784,128]{2,1,0:T(8,128)S(1)} %collective-permute-done.up.cup) | copy-start | bytes 3612676
  39.9 10.7 %copy-start.4 = (f32[3,784,128]{2,1,0:T(8,128)}, f32[3,784,128]{2,1,0:T(8,128)S(1)}, u32[]{:S(2)}) copy-start(f32[3,784,128]{2,1,0:T(8,128)S(1)} %collective-permute-done.1.down.cdown) | copy-start | bytes 3612676
  39.9 10.7 %copy-start.6 = (f32[240,240]{1,0:T(8,128)S(1)}, f32[240,240]{1,0:T(8,128)}, u32[]{:S(2)}) copy-start(f32[240,240]{1,0:T(8,128)} %matrix.3) | copy-start | bytes 691204
  92.7 11.2 %copy-start.1 = (f32[8,2,3,120,128]{4,3,2,1,0:T(8,128)}, f32[8,2,3,120,128]{4,3,2,1,0:T(8,128)S(1)}, u32[]{:S(2)}) copy-start(f32[8,2,3,120,128]{4,3,2,1,0:T(8,128)S(1)} %all_to_all.15.x.own) | copy-start | bytes 8847364
  97.0 47.1 %all-to-all-start.2 = ((f32[8,1,3,120,128]{4,3,2,1,0:T(8,128)}), f32[8,1,3,120,128]{4,3,2,1,0:T(8,128)}, u32[]{:S(2)}, u32[]{:S(2)}) async-start(f32[8,1,3,120,128]{4,3,2,1,0:T(8,128)} %shard_map.90), calls=%async_computation.2 | async-start | bytes 2949120 | tf_op jit(solution)/shard_map/all_to_all | solution.py:352
  105.5 18.2 %collective-permute-start.2 = (f32[6,3,120,128]{3,2,1,0:T(8,128)}, f32[6,3,120,128]{3,2,1,0:T(8,128)S(1)}, u32[]{:S(2)}, u32[]{:S(2)}) collective-permute-start(f32[6,3,120,128]{3,2,1,0:T(8,128)} %get-tuple-element.21), channel_id=1, source_target_pairs={{0,8},{8,16},{16,24},{24,32},{32,40},{40,48},{48,56},{56,64},{64,7... | collective-permute-start | bytes 3317768 | tf_op jit(solution)/shard_map/ppermute | solution.py:421
  111.0 18.2 %collective-permute-start.3 = (f32[6,3,120,128]{3,2,1,0:T(8,128)}, f32[6,3,120,128]{3,2,1,0:T(8,128)S(1)}, u32[]{:S(2)}, u32[]{:S(2)}) collective-permute-start(f32[6,3,120,128]{3,2,1,0:T(8,128)} %get-tuple-element.20), channel_id=1, source_target_pairs={{8,0},{16,8},{24,16},{32,24},{40,32},{48,40},{56,48},{64,56},{72,6... | collective-permute-start | bytes 3317768 | tf_op jit(solution)/shard_map/ppermute | solution.py:422
  129.2 1.3 copy-start.3
  130.5 1.3 copy-start.5

commit v7 on v6

--- a/solution.py
+++ b/solution.py
@@ -35,20 +35,20 @@
     )
 
 
-def pack_even(x, cf, own, up, down, speeds):
-    width = own.shape[2]
+def pack(x, y, cf, up, down, speeds, odd):
+    width = odd.shape[2]
     x = x.reshape(width * 8, 128)
+    y = y.reshape(width * 8, 128)
     for r in range(8):
         for i in range(width // 8):
             value = x[pl.ds(i * 64 + r, 8, stride=8), :]
-            rows = slice(i * 8, i * 8 + 8)
-            own[r, 0, rows, :] = value
             if r >= 2:
                 at = (r - 2) * width + i * 8
                 up[0, at : at + 8, :] = value
             if r < 6:
                 at = r * width + i * 8
                 down[0, at : at + 8, :] = value
+            odd[r, 0, i * 8 : i * 8 + 8, :] = y[pl.ds(i * 64 + r, 8, stride=8), :]
     for d in range(2):
         for parity in range(2):
             for row in range(4):
@@ -61,13 +61,6 @@
                 for half in (slice(0, 4), slice(4, 8)):
                     speeds[parity, d, row, half, :] = before
                     speeds[parity, d, row + 4, half, :] = after
-
-
-def pack_odd(x, own):
-    x = x.reshape(own.shape[2] * 8, 128)
-    for r in range(8):
-        for i in range(own.shape[2] // 8):
-            own[r, 0, i * 8 : i * 8 + 8, :] = x[pl.ds(i * 64 + r, 8, stride=8), :]
 
 
 def flux_taps(c):
@@ -105,25 +98,32 @@
 
 
 def transport(
-    parity, index, own, up, down, cup, cdown, cf, valid, out, q, c, ends, wx, wy, mid, new, sems
+    parity, own, extra, up, down, cup, cdown, cf, valid, out, q, c, ends, wx, wy, mid, new, sems
 ):
-    width = own.shape[3]
-    strips = own.shape[2]
+    strips, width = out.shape[2], out.shape[3]
     ny = strips * 128
     group = 24
+    packed = parity == 0
     tail = pl.ds(HALO * width, 64)
     moves = [
         pltpu.make_async_copy(cf.at[parity], c.at[:, pl.ds(4, 8)], sems.at[0]),
         pltpu.make_async_copy(cup.at[:, tail], ends.at[0], sems.at[1]),
         pltpu.make_async_copy(cdown.at[:, tail], ends.at[1], sems.at[2]),
-        pltpu.make_async_copy(own.at[:, index], q.at[pl.ds(HALO, 8)], sems.at[3]),
     ]
+    if packed:
+        for row in range(8):
+            at = row if row < HALO else row - 2
+            source = own if row < HALO else extra
+            move = source.at[:, pl.ds(at * width, width)], q.at[HALO + row], sems.at[15 + row]
+            moves.append(pltpu.make_async_copy(*move))
+    else:
+        moves.append(pltpu.make_async_copy(own.at[:, 1], q.at[pl.ds(HALO, 8)], sems.at[15]))
     for row in range(HALO):
         span = pl.ds(row * width, width)
-        before = up.at[:, span] if index == 0 else up.at[row]
-        after = down.at[:, span] if index == 0 else down.at[row]
-        moves.append(pltpu.make_async_copy(before, q.at[row], sems.at[4 + row]))
-        moves.append(pltpu.make_async_copy(after, q.at[HALO + 8 + row], sems.at[10 + row]))
+        before = up.at[:, span] if packed else up.at[row]
+        after = down.at[:, span] if packed else down.at[row]
+        moves.append(pltpu.make_async_copy(before, q.at[row], sems.at[3 + row]))
+        moves.append(pltpu.make_async_copy(after, q.at[HALO + 8 + row], sems.at[9 + row]))
     for move in moves:
         move.start()
     for move in moves[:3]:
@@ -326,27 +326,15 @@
         shape = (own_species, 4, 1, rows, 128)
         return pl.BlockSpec(shape, lambda t: (0, 0, parity, 0, t))
 
-    even, send_up, send_down, speeds = call(
-        pack_even,
-        (group, edge, edge, speeds),
+    send_up, send_down, speeds, odd = call(
+        pack,
+        (edge, edge, speeds, group),
         grid=(strips,),
-        in_specs=[level_group(0), strip(cf.shape[0])],
-        out_specs=[
-            columns(rows),
-            ends,
-            ends,
-            strip(2, 2, rows, 8),
-        ],
-    )(split, cf)
+        in_specs=[level_group(0), level_group(1), strip(cf.shape[0])],
+        out_specs=[ends, ends, strip(2, 2, rows, 8), columns(rows)],
+    )(split, split, cf)
     up = lax.ppermute(send_up, "space", up_pairs)
     down = lax.ppermute(send_down, "space", down_pairs)
-    odd = call(
-        pack_odd,
-        group,
-        grid=(strips,),
-        in_specs=[level_group(1)],
-        out_specs=columns(rows),
-    )(split)
 
     def exchange(a):
         return lax.all_to_all(a, "spec", split_axis=0, concat_axis=0, tiled=True)
@@ -375,12 +363,12 @@
 
     cup, cdown = up, down
 
-    def transported(parity, a, index, shape, before, after):
+    def transported(parity, a, extra, shape, before, after):
         return call(
-            functools.partial(transport, parity, index),
+            functools.partial(transport, parity),
             shape,
             grant=GRANT,
-            in_specs=[anywhere] * 6 + [pl.BlockSpec(memory_space=pltpu.SMEM)],
+            in_specs=[anywhere] * 7 + [pl.BlockSpec(memory_space=pltpu.SMEM)],
             out_specs=far_spec,
             scratch_shapes=[
                 pltpu.VMEM((20, strips, width, 128), F32),
@@ -390,9 +378,9 @@
                 pltpu.VMEM((14, TAPS, 8, ny), F32),
                 pltpu.VMEM((14, 3, 8, ny), F32),
                 pltpu.VMEM((rows, strips, width, 128), F32),
-                pltpu.SemaphoreType.DMA((16,)),
+                pltpu.SemaphoreType.DMA((23,)),
             ],
-        )(far(a) if index == 0 else a, before, after, cup, cdown, far(speeds), valid)
+        )(a, extra, before, after, cup, cdown, far(speeds), valid)
 
     start = lax.axis_index("spec") * own_species
     mine = lax.dynamic_slice_in_dim(rates, start, own_species, 1).T
@@ -415,14 +403,14 @@
     single = far_shape((rows, 1, strips, width, 128))
 
     odd = exchange(odd)
-    both = transported(0, even[:, None], 0, pair, up, down)
+    both = transported(0, far(send_down), far(send_up), pair, up, down)
     both = coupled(odd[:, None], 0, pair, 1, both)
     both = exchange(both)
     up = lax.ppermute(both[2:, 1], "space", up_pairs)
     down = lax.ppermute(both[:HALO, 1], "space", down_pairs)
     even = coupled(both, 0, single, 0)
     even = exchange(even)[:, 0]
-    odd = transported(1, both, 1, single, up, down)[:, 0]
+    odd = transported(1, both, valid, single, up, down)[:, 0]
 
     updated, deposited = call(
         finish,

time: 151 us -> 148 us (0.980)
  Pallas kernels: 48.4 us -> 45.9 us
    pallas_call x4 -> x3, Pallas kernels: 30.4 us -> 27.9 us  [the longest x2 23.2 us: transported(): call(functools.partial(transport, parity), shape, grant=GRANT, in_specs=[...]
  transfers between devices with their start and end apart: 6 -> 6, of which waited for: 4 -> 4; matrix products, arithmetic and copies ran while one was open for 2% -> 2% of each run, Pallas kernels for 21% -> 19%
where the time goes in v7:
time: 148 us; the launch traced here: 147 us
  Pallas kernels  45.9 us (31%)
  blocking collectives  38.7 us (26%)
  starting transfers between devices  29 us (20%)
  waiting for transfers between devices  28.1 us (19%)
  local copies, waits for them, and re-layouts  4.94 us (3%)
    all_to_all x1, blocking collectives, exchange(): return lax.all_to_all(a, 'spec', split_axis=0, concat_axis=0, tiled=True)  38.7 us
    pallas_call x2, Pallas kernels, transported(): call(functools.partial(transport, parity), shape, grant=GRANT, in_specs=[...  23.2 us
    all_to_all x2, starting transfers between devices, exchange(): return lax.all_to_all(a, 'spec', split_axis=0, concat_axis=0, tiled=True)  13.8 us
    ppermute x1, waiting for transfers between devices, on_device(): up = lax.ppermute(send_up, 'space', up_pairs)  11.8 us
    pallas_call x2, Pallas kernels, coupled(): call(functools.partial(couple, index, place), shape, grant=GRANT, in_spec...  7.71 us
    ppermute x1, starting transfers between devices, on_device(): up = lax.ppermute(send_up, 'space', up_pairs)  5.86 us
    pallas_call x1, Pallas kernels, on_device(): call(finish, (sds((tracers.size // ny, ny), F32), sds((own_species * rows...  5.65 us
    ppermute x1, starting transfers between devices, on_device(): up = lax.ppermute(both[2:, 1], 'space', up_pairs)  5.54 us
  transfers between devices with their start and end apart: 6, of which 4 were waited for; matrix products, arithmetic and copies ran while one was open for 2% of the time, Pallas kernels for 19%

profile of v7, /device:TPU:101, one launch (start us, length us, event | category | flops | bytes accessed | tf_op | source)
XLA Modules:
  0.0 147.3 jit_solution(1318201769434760003)
XLA Ops:
  0.6 0.0 copy-start
  0.6 4.7 %shard_map.86 = (f32[3,784,128]{2,1,0:T(8,128)}, f32[3,784,128]{2,1,0:T(8,128)}, f32[2,2,8,8,384]{4,3,2,1,0:T(8,128)}, f32[8,3,120,128]{3,2,1,0:T(8,128)}) custom-call(f32[30,4,2,8,384]{4,3,2,1,0:T(8,128)} %bitcast.22, f32[30,4,2,8,384]{4,3,2,1,0:T(8,128)} %bitcast.23, f32[128,384]{1,0:T(8,128)} %bitcast.28), custom_call_target="tpu_custom_call" | custom-call | tf_op jit(solution)/shard_map/pallas_call | solution.py:329
  5.4 6.9 %all-to-all-start = ((f32[8,3,120,128]{3,2,1,0:T(8,128)}), f32[8,3,120,128]{3,2,1,0:T(8,128)}, u32[]{:S(2)}, u32[]{:S(2)}) async-start(f32[8,3,120,128]{3,2,1,0:T(8,128)} %get-tuple-element.11), calls=%async_computation | async-start | bytes 2949120 | tf_op jit(solution)/shard_map/all_to_all | solution.py:340
  12.2 5.9 %collective-permute-start = (f32[3,784,128]{2,1,0:T(8,128)}, f32[3,784,128]{2,1,0:T(8,128)S(1)}, u32[]{:S(2)}, u32[]{:S(2)}) collective-permute-start(f32[3,784,128]{2,1,0:T(8,128)} %get-tuple-element.13.extra), channel_id=1, source_target_pairs={{0,8},{8,16},{16,24},{24,32},{32,40},{40,48},{48,56},{56,64},{64,7... | collective-permute-start | bytes 3612680 | tf_op jit(solution)/shard_map/ppermute | solution.py:336
  18.1 1.9 %collective-permute-start.1 = (f32[3,784,128]{2,1,0:T(8,128)}, f32[3,784,128]{2,1,0:T(8,128)S(1)}, u32[]{:S(2)}, u32[]{:S(2)}) collective-permute-start(f32[3,784,128]{2,1,0:T(8,128)} %get-tuple-element.12.own), channel_id=1, source_target_pairs={{8,0},{16,8},{24,16},{32,24},{40,32},{48,40},{56,48},{64,56},{72,6... | collective-permute-start | bytes 3612680 | tf_op jit(solution)/shard_map/ppermute | solution.py:337
  20.0 11.8 %collective-permute-done.up.cup = f32[3,784,128]{2,1,0:T(8,128)S(1)} collective-permute-done((f32[3,784,128]{2,1,0:T(8,128)}, f32[3,784,128]{2,1,0:T(8,128)S(1)}, u32[]{:S(2)}, u32[]{:S(2)}) %collective-permute-start) | collective-permute-done | bytes 1204256 | tf_op jit(solution)/shard_map/ppermute | solution.py:336
  31.8 0.0 copy-start.2
  31.8 5.5 %collective-permute-done.1.down.cdown = f32[3,784,128]{2,1,0:T(8,128)S(1)} collective-permute-done((f32[3,784,128]{2,1,0:T(8,128)}, f32[3,784,128]{2,1,0:T(8,128)S(1)}, u32[]{:S(2)}, u32[]{:S(2)}) %collective-permute-start.1) | collective-permute-done | bytes 1204256 | tf_op jit(solution)/shard_map/ppermute | solution.py:337
  37.3 0.0 copy-start.4
  37.3 0.0 copy-start.6
  37.3 10.7 %shard_map.87.refs_0_ = f32[8,2,3,120,128]{4,3,2,1,0:T(8,128)} custom-call(f32[3,784,128]{2,1,0:T(8,128)} %get-tuple-element.12.own, f32[3,784,128]{2,1,0:T(8,128)} %get-tuple-element.13.extra, f32[3,784,128]{2,1,0:T(8,128)S(1)} %collective-permute-done.up.cup, f32[3,784,128]{2,1,0:T(8,128)S(1)} %collective-permute-done.1.down.cdown, ...), custom_call_target="tpu_custom_call" | custom-call | tf_op jit(solution)/shard_map/pallas_call | solution.py:367
  48.1 0.0 copy-done.2
  48.1 0.0 copy-done.4
  48.1 0.0 all-to-all-done
  48.1 0.0 copy-done.6
  48.1 3.4 %shard_map.88 = f32[8,2,3,120,128]{4,3,2,1,0:T(8,128)} custom-call(f32[8,1,3,120,128]{4,3,2,1,0:T(8,128)} %bitcast.2.x, f32[240,240]{1,0:T(8,128)S(1)} %copy-done.6, f32[8,2,3,120,128]{4,3,2,1,0:T(8,128)} %shard_map.87.refs_0_), custom_call_target="tpu_custom_call", output_to_operand_aliasing={{}: (2, {})} | custom-call | tf_op jit(solution)/shard_map/pallas_call | solution.py:349
  51.5 38.7 %all_to_all.15.x.own = f32[8,2,3,120,128]{4,3,2,1,0:T(8,128)S(1)} all-to-all(f32[8,2,3,120,128]{4,3,2,1,0:T(8,128)} %shard_map.88), channel_id=1, replica_groups=mesh['space'=32,'spec'=8] {'spec'}, dimensions={0} | all-to-all | bytes 5898240 | tf_op jit(solution)/shard_map/all_to_all | solution.py:340
  90.2 0.0 copy-start.1
  90.2 4.3 %shard_map.89 = f32[8,1,3,120,128]{4,3,2,1,0:T(8,128)} custom-call(f32[8,2,3,120,128]{4,3,2,1,0:T(8,128)S(1)} %all_to_all.15.x.own, f32[240,240]{1,0:T(8,128)S(1)} %copy-done.6), custom_call_target="tpu_custom_call" | custom-call | tf_op jit(solution)/shard_map/pallas_call | solution.py:349
  94.5 6.9 %all-to-all-start.2 = ((f32[8,1,3,120,128]{4,3,2,1,0:T(8,128)}), f32[8,1,3,120,128]{4,3,2,1,0:T(8,128)}, u32[]{:S(2)}, u32[]{:S(2)}) async-start(f32[8,1,3,120,128]{4,3,2,1,0:T(8,128)} %shard_map.89), calls=%async_computation.2 | async-start | bytes 2949120 | tf_op jit(solution)/shard_map/all_to_all | solution.py:340
  101.4 0.0 copy-done.1
  101.4 1.5 %slice_bitcast_fusion = (f32[6,3,120,128]{3,2,1,0:T(8,128)}, f32[6,3,120,128]{3,2,1,0:T(8,128)}) fusion(f32[8,2,3,120,128]{4,3,2,1,0:T(8,128)S(1)} %all_to_all.15.x.own), kind=kLoop, calls=%fused_computation | loop fusion | bytes 4423680 | tf_op jit(solution)/shard_map/squeeze | solution.py:410
  102.9 5.5 %collective-permute-start.2 = (f32[6,3,120,128]{3,2,1,0:T(8,128)}, f32[6,3,120,128]{3,2,1,0:T(8,128)S(1)}, u32[]{:S(2)}, u32[]{:S(2)}) collective-permute-start(f32[6,3,120,128]{3,2,1,0:T(8,128)} %get-tuple-element.21), channel_id=1, source_target_pairs={{0,8},{8,16},{16,24},{24,32},{32,40},{40,48},{48,56},{56,64},{64,7... | collective-permute-start | bytes 3317768 | tf_op jit(solution)/shard_map/ppermute | solution.py:409
  108.5 1.9 %collective-permute-start.3 = (f32[6,3,120,128]{3,2,1,0:T(8,128)}, f32[6,3,120,128]{3,2,1,0:T(8,128)S(1)}, u32[]{:S(2)}, u32[]{:S(2)}) collective-permute-start(f32[6,3,120,128]{3,2,1,0:T(8,128)} %get-tuple-element.20), channel_id=1, source_target_pairs={{8,0},{16,8},{24,16},{32,24},{40,32},{48,40},{56,48},{64,56},{72,6... | collective-permute-start | bytes 3317768 | tf_op jit(solution)/shard_map/ppermute | solution.py:410
  110.4 0.0 copy-done
  110.4 0.1 dynamic-slice_bitcast_fusion
  110.5 0.1 copy.20
  110.6 0.6 pad.4.clone
  111.2 4.6 %shard_map.91 = (f32[8,3,120,128]{3,2,1,0:T(8,128)}, f32[8,8,384]{2,1,0:T(8,128)}, f32[8,8,384]{2,1,0:T(8,128)}) custom-call(f32[64,384]{1,0:T(8,128)} %bitcast.25, s32[8,384]{1,0:T(8,128)} %pbl.3, s32[8,384]{1,0:T(8,128)} %land.1, f32[120,16]{1,0:T(8,128)} %bitcast.27), custom_call_target="tpu_custom_call" | custom-call | tf_op jit(solution)/shard_map/pallas_call | solution.py:390
  115.8 5.3 %collective-permute-done.2.up = f32[6,3,120,128]{3,2,1,0:T(8,128)S(1)} collective-permute-done((f32[6,3,120,128]{3,2,1,0:T(8,128)}, f32[6,3,120,128]{3,2,1,0:T(8,128)S(1)}, u32[]{:S(2)}, u32[]{:S(2)}) %collective-permute-start.2) | collective-permute-done | bytes 1105952 | tf_op jit(solution)/shard_map/ppermute | solution.py:409
  121.1 5.5 %collective-permute-done.3.down = f32[6,3,120,128]{3,2,1,0:T(8,128)S(1)} collective-permute-done((f32[6,3,120,128]{3,2,1,0:T(8,128)}, f32[6,3,120,128]{3,2,1,0:T(8,128)S(1)}, u32[]{:S(2)}, u32[]{:S(2)}) %collective-permute-start.3) | collective-permute-done | bytes 1105952 | tf_op jit(solution)/shard_map/ppermute | solution.py:410
  126.6 0.0 copy-start.3
  126.6 1.3 copy-done.3
  127.9 0.0 copy-start.5
  127.9 1.3 copy-done.5
  129.2 12.5 %shard_map.90 = f32[8,1,3,120,128]{4,3,2,1,0:T(8,128)} custom-call(f32[8,2,3,120,128]{4,3,2,1,0:T(8,128)} %copy-done.1, f32[1,1]{1,0:T(1,128)} %bitcast.3.valid.extra, f32[6,3,120,128]{3,2,1,0:T(8,128)S(1)} %collective-permute-done.2.up, f32[6,3,120,128]{3,2,1,0:T(8,128)S(1)} %collective-permute-done.3.down, f32[3,784,128]{2,1,0:T(8,128)S(1)} %copy-done.3, ...), custom_call_target="tpu_custom_call" | custom-call | tf_op jit(solution)/shard_map/pallas_call | solution.py:367
  141.7 0.0 all-to-all-done.2
  141.7 5.7 %shard_map.92 = (f32[1920,384]{1,0:T(8,128)}, f32[240,384]{1,0:T(8,128)}) custom-call(f32[8,3,120,128]{3,2,1,0:T(8,128)} %bitcast.4.even, f32[8,3,120,128]{3,2,1,0:T(8,128)} %bitcast.24, f32[8,3,120,128]{3,2,1,0:T(8,128)} %get-tuple-element.15.keep, f32[8,8,384]{2,1,0:T(8,128)} %get-tuple-element.16.weven, f32[8,8,384]{2,1,0:T(8,128)} %get-tuple-element.17.wodd, ...), custom_call_target="tpu_custom_call" | custom-call | tf_op jit(solution)/shard_map/pallas_call | solution.py:415
Async XLA Ops:
  0.6 109.8 %copy-start = (f32[11,240]{1,0:T(8,128)S(1)}, f32[11,240]{1,0:T(8,128)}, u32[]{:S(2)}) copy-start(f32[11,240]{1,0:T(8,128)} %param.12) | copy-start | bytes 31684
  5.4 42.7 %all-to-all-start = ((f32[8,3,120,128]{3,2,1,0:T(8,128)}), f32[8,3,120,128]{3,2,1,0:T(8,128)}, u32[]{:S(2)}, u32[]{:S(2)}) async-start(f32[8,3,120,128]{3,2,1,0:T(8,128)} %get-tuple-element.11), calls=%async_computation | async-start | bytes 2949120 | tf_op jit(solution)/shard_map/all_to_all | solution.py:340
  12.2 19.6 %collective-permute-start = (f32[3,784,128]{2,1,0:T(8,128)}, f32[3,784,128]{2,1,0:T(8,128)S(1)}, u32[]{:S(2)}, u32[]{:S(2)}) collective-permute-start(f32[3,784,128]{2,1,0:T(8,128)} %get-tuple-element.13.extra), channel_id=1, source_target_pairs={{0,8},{8,16},{16,24},{24,32},{32,40},{40,48},{48,56},{56,64},{64,7... | collective-permute-start | bytes 3612680 | tf_op jit(solution)/shard_map/ppermute | solution.py:336
  18.1 19.2 %collective-permute-start.1 = (f32[3,784,128]{2,1,0:T(8,128)}, f32[3,784,128]{2,1,0:T(8,128)S(1)}, u32[]{:S(2)}, u32[]{:S(2)}) collective-permute-start(f32[3,784,128]{2,1,0:T(8,128)} %get-tuple-element.12.own), channel_id=1, source_target_pairs={{8,0},{16,8},{24,16},{32,24},{40,32},{48,40},{56,48},{64,56},{72,6... | collective-permute-start | bytes 3612680 | tf_op jit(solution)/shard_map/ppermute | solution.py:337
  31.8 16.3 %copy-start.2 = (f32[3,784,128]{2,1,0:T(8,128)}, f32[3,784,128]{2,1,0:T(8,128)S(1)}, u32[]{:S(2)}) copy-start(f32[3,784,128]{2,1,0:T(8,128)S(1)} %collective-permute-done.up.cup) | copy-start | bytes 3612676
  37.3 10.8 %copy-start.4 = (f32[3,784,128]{2,1,0:T(8,128)}, f32[3,784,128]{2,1,0:T(8,128)S(1)}, u32[]{:S(2)}) copy-start(f32[3,784,128]{2,1,0:T(8,128)S(1)} %collective-permute-done.1.down.cdown) | copy-start | bytes 3612676
  37.3 10.8 %copy-start.6 = (f32[240,240]{1,0:T(8,128)S(1)}, f32[240,240]{1,0:T(8,128)}, u32[]{:S(2)}) copy-start(f32[240,240]{1,0:T(8,128)} %matrix.3) | copy-start | bytes 691204
  90.2 11.2 %copy-start.1 = (f32[8,2,3,120,128]{4,3,2,1,0:T(8,128)}, f32[8,2,3,120,128]{4,3,2,1,0:T(8,128)S(1)}, u32[]{:S(2)}) copy-start(f32[8,2,3,120,128]{4,3,2,1,0:T(8,128)S(1)} %all_to_all.15.x.own) | copy-start | bytes 8847364
  94.5 47.2 %all-to-all-start.2 = ((f32[8,1,3,120,128]{4,3,2,1,0:T(8,128)}), f32[8,1,3,120,128]{4,3,2,1,0:T(8,128)}, u32[]{:S(2)}, u32[]{:S(2)}) async-start(f32[8,1,3,120,128]{4,3,2,1,0:T(8,128)} %shard_map.89), calls=%async_computation.2 | async-start | bytes 2949120 | tf_op jit(solution)/shard_map/all_to_all | solution.py:340
  102.9 18.2 %collective-permute-start.2 = (f32[6,3,120,128]{3,2,1,0:T(8,128)}, f32[6,3,120,128]{3,2,1,0:T(8,128)S(1)}, u32[]{:S(2)}, u32[]{:S(2)}) collective-permute-start(f32[6,3,120,128]{3,2,1,0:T(8,128)} %get-tuple-element.21), channel_id=1, source_target_pairs={{0,8},{8,16},{16,24},{24,32},{32,40},{40,48},{48,56},{56,64},{64,7... | collective-permute-start | bytes 3317768 | tf_op jit(solution)/shard_map/ppermute | solution.py:409
  108.5 18.2 %collective-permute-start.3 = (f32[6,3,120,128]{3,2,1,0:T(8,128)}, f32[6,3,120,128]{3,2,1,0:T(8,128)S(1)}, u32[]{:S(2)}, u32[]{:S(2)}) collective-permute-start(f32[6,3,120,128]{3,2,1,0:T(8,128)} %get-tuple-element.20), channel_id=1, source_target_pairs={{8,0},{16,8},{24,16},{32,24},{40,32},{48,40},{56,48},{64,56},{72,6... | collective-permute-start | bytes 3317768 | tf_op jit(solution)/shard_map/ppermute | solution.py:410
  126.6 1.3 copy-start.3
  127.9 1.3 copy-start.5

commit v8 on v7

--- a/solution.py
+++ b/solution.py
@@ -35,10 +35,9 @@
     )
 
 
-def pack(x, y, cf, up, down, speeds, odd):
-    width = odd.shape[2]
+def pack_even(x, cf, up, down, speeds):
+    width = x.shape[0] * 4
     x = x.reshape(width * 8, 128)
-    y = y.reshape(width * 8, 128)
     for r in range(8):
         for i in range(width // 8):
             value = x[pl.ds(i * 64 + r, 8, stride=8), :]
@@ -48,7 +47,6 @@
             if r < 6:
                 at = r * width + i * 8
                 down[0, at : at + 8, :] = value
-            odd[r, 0, i * 8 : i * 8 + 8, :] = y[pl.ds(i * 64 + r, 8, stride=8), :]
     for d in range(2):
         for parity in range(2):
             for row in range(4):
@@ -61,6 +59,13 @@
                 for half in (slice(0, 4), slice(4, 8)):
                     speeds[parity, d, row, half, :] = before
                     speeds[parity, d, row + 4, half, :] = after
+
+
+def pack_odd(x, own):
+    x = x.reshape(own.shape[2] * 8, 128)
+    for r in range(8):
+        for i in range(own.shape[2] // 8):
+            own[r, 0, i * 8 : i * 8 + 8, :] = x[pl.ds(i * 64 + r, 8, stride=8), :]
 
 
 def flux_taps(c):
@@ -326,15 +331,22 @@
         shape = (own_species, 4, 1, rows, 128)
         return pl.BlockSpec(shape, lambda t: (0, 0, parity, 0, t))
 
-    send_up, send_down, speeds, odd = call(
-        pack,
-        (edge, edge, speeds, group),
+    send_up, send_down, speeds = call(
+        pack_even,
+        (edge, edge, speeds),
         grid=(strips,),
-        in_specs=[level_group(0), level_group(1), strip(cf.shape[0])],
-        out_specs=[ends, ends, strip(2, 2, rows, 8), columns(rows)],
-    )(split, split, cf)
+        in_specs=[level_group(0), strip(cf.shape[0])],
+        out_specs=[ends, ends, strip(2, 2, rows, 8)],
+    )(split, cf)
     up = lax.ppermute(send_up, "space", up_pairs)
     down = lax.ppermute(send_down, "space", down_pairs)
+    odd = call(
+        pack_odd,
+        group,
+        grid=(strips,),
+        in_specs=[level_group(1)],
+        out_specs=columns(rows),
+    )(split)
 
     def exchange(a):
         return lax.all_to_all(a, "spec", split_axis=0, concat_axis=0, tiled=True)

time: 148 us -> 151 us (1.020)
  Pallas kernels: 45.9 us -> 48.3 us
    pallas_call x1 -> x2, Pallas kernels: 4.71 us -> 7.14 us  [the longest x1 3.7 us: on_device(): call(pack_even, (edge, edge, speeds), grid=(strips,), in_specs=[level_gro...]
  transfers between devices with their start and end apart: 6 -> 6, of which waited for: 4 -> 4; matrix products, arithmetic and copies ran while one was open for 2% -> 2% of each run, Pallas kernels for 19% -> 21%
where the time goes in v8:
time: 151 us; the launch traced here: 150 us
  Pallas kernels  48.3 us (32%)
  blocking collectives  38.7 us (26%)
  starting transfers between devices  29 us (19%)
  waiting for transfers between devices  28.1 us (19%)
  local copies, waits for them, and re-layouts  4.94 us (3%)
    all_to_all x1, blocking collectives, exchange(): return lax.all_to_all(a, 'spec', split_axis=0, concat_axis=0, tiled=True)  38.7 us
    pallas_call x2, Pallas kernels, transported(): call(functools.partial(transport, parity), shape, grant=GRANT, in_specs=[...  23.2 us
    all_to_all x2, starting transfers between devices, exchange(): return lax.all_to_all(a, 'spec', split_axis=0, concat_axis=0, tiled=True)  13.8 us
    ppermute x1, waiting for transfers between devices, on_device(): up = lax.ppermute(send_up, 'space', up_pairs)  11.8 us
    pallas_call x2, Pallas kernels, coupled(): call(functools.partial(couple, index, place), shape, grant=GRANT, in_spec...  7.71 us
    ppermute x1, starting transfers between devices, on_device(): up = lax.ppermute(send_up, 'space', up_pairs)  5.86 us
    pallas_call x1, Pallas kernels, on_device(): call(finish, (sds((tracers.size // ny, ny), F32), sds((own_species * rows...  5.65 us
    ppermute x1, starting transfers between devices, on_device(): up = lax.ppermute(both[2:, 1], 'space', up_pairs)  5.54 us
  transfers between devices with their start and end apart: 6, of which 4 were waited for; matrix products, arithmetic and copies ran while one was open for 2% of the time, Pallas kernels for 21%

profile of v8, /device:TPU:101, one launch (start us, length us, event | category | flops | bytes accessed | tf_op | source)
XLA Modules:
  0.0 149.8 jit_solution(14827414078124735411)
XLA Ops:
  0.6 0.0 copy-start
  0.6 3.4 %shard_map.86 = f32[8,3,120,128]{3,2,1,0:T(8,128)} custom-call(f32[30,4,2,8,384]{4,3,2,1,0:T(8,128)} %bitcast.22), custom_call_target="tpu_custom_call" | custom-call | tf_op jit(solution)/shard_map/pallas_call | solution.py:343
  4.1 6.9 %all-to-all-start = ((f32[8,3,120,128]{3,2,1,0:T(8,128)}), f32[8,3,120,128]{3,2,1,0:T(8,128)}, u32[]{:S(2)}, u32[]{:S(2)}) async-start(f32[8,3,120,128]{3,2,1,0:T(8,128)} %shard_map.86), calls=%async_computation | async-start | bytes 2949120 | tf_op jit(solution)/shard_map/all_to_all | solution.py:352
  11.0 3.7 %shard_map.87 = (f32[3,784,128]{2,1,0:T(8,128)}, f32[3,784,128]{2,1,0:T(8,128)}, f32[2,2,8,8,384]{4,3,2,1,0:T(8,128)}) custom-call(f32[30,4,2,8,384]{4,3,2,1,0:T(8,128)} %bitcast.23, f32[128,384]{1,0:T(8,128)} %bitcast.28), custom_call_target="tpu_custom_call" | custom-call | tf_op jit(solution)/shard_map/pallas_call | solution.py:334
  14.7 5.9 %collective-permute-start = (f32[3,784,128]{2,1,0:T(8,128)}, f32[3,784,128]{2,1,0:T(8,128)S(1)}, u32[]{:S(2)}, u32[]{:S(2)}) collective-permute-start(f32[3,784,128]{2,1,0:T(8,128)} %get-tuple-element.11.extra), channel_id=1, source_target_pairs={{0,8},{8,16},{16,24},{24,32},{32,40},{40,48},{48,56},{56,64},{64,7... | collective-permute-start | bytes 3612680 | tf_op jit(solution)/shard_map/ppermute | solution.py:341
  20.5 1.9 %collective-permute-start.1 = (f32[3,784,128]{2,1,0:T(8,128)}, f32[3,784,128]{2,1,0:T(8,128)S(1)}, u32[]{:S(2)}, u32[]{:S(2)}) collective-permute-start(f32[3,784,128]{2,1,0:T(8,128)} %get-tuple-element.10.own), channel_id=1, source_target_pairs={{8,0},{16,8},{24,16},{32,24},{40,32},{48,40},{56,48},{64,56},{72,6... | collective-permute-start | bytes 3612680 | tf_op jit(solution)/shard_map/ppermute | solution.py:342
  22.5 11.8 %collective-permute-done.up.cup = f32[3,784,128]{2,1,0:T(8,128)S(1)} collective-permute-done((f32[3,784,128]{2,1,0:T(8,128)}, f32[3,784,128]{2,1,0:T(8,128)S(1)}, u32[]{:S(2)}, u32[]{:S(2)}) %collective-permute-start) | collective-permute-done | bytes 1204256 | tf_op jit(solution)/shard_map/ppermute | solution.py:341
  34.2 0.0 copy-start.2
  34.2 5.5 %collective-permute-done.1.down.cdown = f32[3,784,128]{2,1,0:T(8,128)S(1)} collective-permute-done((f32[3,784,128]{2,1,0:T(8,128)}, f32[3,784,128]{2,1,0:T(8,128)S(1)}, u32[]{:S(2)}, u32[]{:S(2)}) %collective-permute-start.1) | collective-permute-done | bytes 1204256 | tf_op jit(solution)/shard_map/ppermute | solution.py:342
  39.7 0.0 copy-start.4
  39.7 0.0 copy-start.6
  39.7 10.7 %shard_map.88.refs_0_ = f32[8,2,3,120,128]{4,3,2,1,0:T(8,128)} custom-call(f32[3,784,128]{2,1,0:T(8,128)} %get-tuple-element.10.own, f32[3,784,128]{2,1,0:T(8,128)} %get-tuple-element.11.extra, f32[3,784,128]{2,1,0:T(8,128)S(1)} %collective-permute-done.up.cup, f32[3,784,128]{2,1,0:T(8,128)S(1)} %collective-permute-done.1.down.cdown, ...), custom_call_target="tpu_custom_call" | custom-call | tf_op jit(solution)/shard_map/pallas_call | solution.py:379
  50.5 0.0 copy-done.2
  50.5 0.0 copy-done.4
  50.5 0.0 all-to-all-done
  50.5 0.0 copy-done.6
  50.5 3.4 %shard_map.89 = f32[8,2,3,120,128]{4,3,2,1,0:T(8,128)} custom-call(f32[8,1,3,120,128]{4,3,2,1,0:T(8,128)} %bitcast.1.x, f32[240,240]{1,0:T(8,128)S(1)} %copy-done.6, f32[8,2,3,120,128]{4,3,2,1,0:T(8,128)} %shard_map.88.refs_0_), custom_call_target="tpu_custom_call", output_to_operand_aliasing={{}: (2, {})} | custom-call | tf_op jit(solution)/shard_map/pallas_call | solution.py:361
  53.9 38.7 %all_to_all.15.x.own = f32[8,2,3,120,128]{4,3,2,1,0:T(8,128)S(1)} all-to-all(f32[8,2,3,120,128]{4,3,2,1,0:T(8,128)} %shard_map.89), channel_id=1, replica_groups=mesh['space'=32,'spec'=8] {'spec'}, dimensions={0} | all-to-all | bytes 5898240 | tf_op jit(solution)/shard_map/all_to_all | solution.py:352
  92.6 0.0 copy-start.1
  92.6 4.3 %shard_map.90 = f32[8,1,3,120,128]{4,3,2,1,0:T(8,128)} custom-call(f32[8,2,3,120,128]{4,3,2,1,0:T(8,128)S(1)} %all_to_all.15.x.own, f32[240,240]{1,0:T(8,128)S(1)} %copy-done.6), custom_call_target="tpu_custom_call" | custom-call | tf_op jit(solution)/shard_map/pallas_call | solution.py:361
  96.9 6.9 %all-to-all-start.2 = ((f32[8,1,3,120,128]{4,3,2,1,0:T(8,128)}), f32[8,1,3,120,128]{4,3,2,1,0:T(8,128)}, u32[]{:S(2)}, u32[]{:S(2)}) async-start(f32[8,1,3,120,128]{4,3,2,1,0:T(8,128)} %shard_map.90), calls=%async_computation.2 | async-start | bytes 2949120 | tf_op jit(solution)/shard_map/all_to_all | solution.py:352
  103.8 0.0 copy-done.1
  103.8 1.5 %slice_bitcast_fusion = (f32[6,3,120,128]{3,2,1,0:T(8,128)}, f32[6,3,120,128]{3,2,1,0:T(8,128)}) fusion(f32[8,2,3,120,128]{4,3,2,1,0:T(8,128)S(1)} %all_to_all.15.x.own), kind=kLoop, calls=%fused_computation | loop fusion | bytes 4423680 | tf_op jit(solution)/shard_map/squeeze | solution.py:422
  105.4 5.5 %collective-permute-start.2 = (f32[6,3,120,128]{3,2,1,0:T(8,128)}, f32[6,3,120,128]{3,2,1,0:T(8,128)S(1)}, u32[]{:S(2)}, u32[]{:S(2)}) collective-permute-start(f32[6,3,120,128]{3,2,1,0:T(8,128)} %get-tuple-element.19), channel_id=1, source_target_pairs={{0,8},{8,16},{16,24},{24,32},{32,40},{40,48},{48,56},{56,64},{64,7... | collective-permute-start | bytes 3317768 | tf_op jit(solution)/shard_map/ppermute | solution.py:421
  110.9 1.9 %collective-permute-start.3 = (f32[6,3,120,128]{3,2,1,0:T(8,128)}, f32[6,3,120,128]{3,2,1,0:T(8,128)S(1)}, u32[]{:S(2)}, u32[]{:S(2)}) collective-permute-start(f32[6,3,120,128]{3,2,1,0:T(8,128)} %get-tuple-element.18), channel_id=1, source_target_pairs={{8,0},{16,8},{24,16},{32,24},{40,32},{48,40},{56,48},{64,56},{72,6... | collective-permute-start | bytes 3317768 | tf_op jit(solution)/shard_map/ppermute | solution.py:422
  112.9 0.0 copy-done
  112.9 0.1 dynamic-slice_bitcast_fusion
  112.9 0.1 copy.20
  113.0 0.6 pad.4.clone
  113.7 4.6 %shard_map.92 = (f32[8,3,120,128]{3,2,1,0:T(8,128)}, f32[8,8,384]{2,1,0:T(8,128)}, f32[8,8,384]{2,1,0:T(8,128)}) custom-call(f32[64,384]{1,0:T(8,128)} %bitcast.25, s32[8,384]{1,0:T(8,128)} %pbl.3, s32[8,384]{1,0:T(8,128)} %land.1, f32[120,16]{1,0:T(8,128)} %bitcast.27), custom_call_target="tpu_custom_call" | custom-call | tf_op jit(solution)/shard_map/pallas_call | solution.py:402
  118.3 5.3 %collective-permute-done.2.up = f32[6,3,120,128]{3,2,1,0:T(8,128)S(1)} collective-permute-done((f32[6,3,120,128]{3,2,1,0:T(8,128)}, f32[6,3,120,128]{3,2,1,0:T(8,128)S(1)}, u32[]{:S(2)}, u32[]{:S(2)}) %collective-permute-start.2) | collective-permute-done | bytes 1105952 | tf_op jit(solution)/shard_map/ppermute | solution.py:421
  123.6 5.5 %collective-permute-done.3.down = f32[6,3,120,128]{3,2,1,0:T(8,128)S(1)} collective-permute-done((f32[6,3,120,128]{3,2,1,0:T(8,128)}, f32[6,3,120,128]{3,2,1,0:T(8,128)S(1)}, u32[]{:S(2)}, u32[]{:S(2)}) %collective-permute-start.3) | collective-permute-done | bytes 1105952 | tf_op jit(solution)/shard_map/ppermute | solution.py:422
  129.1 0.0 copy-start.3
  129.1 1.3 copy-done.3
  130.4 0.0 copy-start.5
  130.4 1.3 copy-done.5
  131.6 12.5 %shard_map.91 = f32[8,1,3,120,128]{4,3,2,1,0:T(8,128)} custom-call(f32[8,2,3,120,128]{4,3,2,1,0:T(8,128)} %copy-done.1, f32[1,1]{1,0:T(1,128)} %bitcast.3.valid.extra, f32[6,3,120,128]{3,2,1,0:T(8,128)S(1)} %collective-permute-done.2.up, f32[6,3,120,128]{3,2,1,0:T(8,128)S(1)} %collective-permute-done.3.down, f32[3,784,128]{2,1,0:T(8,128)S(1)} %copy-done.3, ...), custom_call_target="tpu_custom_call" | custom-call | tf_op jit(solution)/shard_map/pallas_call | solution.py:379
  144.1 0.0 all-to-all-done.2
  144.1 5.7 %shard_map.93 = (f32[1920,384]{1,0:T(8,128)}, f32[240,384]{1,0:T(8,128)}) custom-call(f32[8,3,120,128]{3,2,1,0:T(8,128)} %bitcast.4.even, f32[8,3,120,128]{3,2,1,0:T(8,128)} %bitcast.24, f32[8,3,120,128]{3,2,1,0:T(8,128)} %get-tuple-element.13.keep, f32[8,8,384]{2,1,0:T(8,128)} %get-tuple-element.14.weven, f32[8,8,384]{2,1,0:T(8,128)} %get-tuple-element.15.wodd, ...), custom_call_target="tpu_custom_call" | custom-call | tf_op jit(solution)/shard_map/pallas_call | solution.py:427
Async XLA Ops:
  0.6 112.2 %copy-start = (f32[11,240]{1,0:T(8,128)S(1)}, f32[11,240]{1,0:T(8,128)}, u32[]{:S(2)}) copy-start(f32[11,240]{1,0:T(8,128)} %param.12) | copy-start | bytes 31684
  4.1 46.4 %all-to-all-start = ((f32[8,3,120,128]{3,2,1,0:T(8,128)}), f32[8,3,120,128]{3,2,1,0:T(8,128)}, u32[]{:S(2)}, u32[]{:S(2)}) async-start(f32[8,3,120,128]{3,2,1,0:T(8,128)} %shard_map.86), calls=%async_computation | async-start | bytes 2949120 | tf_op jit(solution)/shard_map/all_to_all | solution.py:352
  14.7 19.6 %collective-permute-start = (f32[3,784,128]{2,1,0:T(8,128)}, f32[3,784,128]{2,1,0:T(8,128)S(1)}, u32[]{:S(2)}, u32[]{:S(2)}) collective-permute-start(f32[3,784,128]{2,1,0:T(8,128)} %get-tuple-element.11.extra), channel_id=1, source_target_pairs={{0,8},{8,16},{16,24},{24,32},{32,40},{40,48},{48,56},{56,64},{64,7... | collective-permute-start | bytes 3612680 | tf_op jit(solution)/shard_map/ppermute | solution.py:341
  20.5 19.2 %collective-permute-start.1 = (f32[3,784,128]{2,1,0:T(8,128)}, f32[3,784,128]{2,1,0:T(8,128)S(1)}, u32[]{:S(2)}, u32[]{:S(2)}) collective-permute-start(f32[3,784,128]{2,1,0:T(8,128)} %get-tuple-element.10.own), channel_id=1, source_target_pairs={{8,0},{16,8},{24,16},{32,24},{40,32},{48,40},{56,48},{64,56},{72,6... | collective-permute-start | bytes 3612680 | tf_op jit(solution)/shard_map/ppermute | solution.py:342
  34.2 16.3 %copy-start.2 = (f32[3,784,128]{2,1,0:T(8,128)}, f32[3,784,128]{2,1,0:T(8,128)S(1)}, u32[]{:S(2)}) copy-start(f32[3,784,128]{2,1,0:T(8,128)S(1)} %collective-permute-done.up.cup) | copy-start | bytes 3612676
  39.7 10.8 %copy-start.4 = (f32[3,784,128]{2,1,0:T(8,128)}, f32[3,784,128]{2,1,0:T(8,128)S(1)}, u32[]{:S(2)}) copy-start(f32[3,784,128]{2,1,0:T(8,128)S(1)} %collective-permute-done.1.down.cdown) | copy-start | bytes 3612676
  39.7 10.8 %copy-start.6 = (f32[240,240]{1,0:T(8,128)S(1)}, f32[240,240]{1,0:T(8,128)}, u32[]{:S(2)}) copy-start(f32[240,240]{1,0:T(8,128)} %matrix.3) | copy-start | bytes 691204
  92.6 11.2 %copy-start.1 = (f32[8,2,3,120,128]{4,3,2,1,0:T(8,128)}, f32[8,2,3,120,128]{4,3,2,1,0:T(8,128)S(1)}, u32[]{:S(2)}) copy-start(f32[8,2,3,120,128]{4,3,2,1,0:T(8,128)S(1)} %all_to_all.15.x.own) | copy-start | bytes 8847364
  96.9 47.2 %all-to-all-start.2 = ((f32[8,1,3,120,128]{4,3,2,1,0:T(8,128)}), f32[8,1,3,120,128]{4,3,2,1,0:T(8,128)}, u32[]{:S(2)}, u32[]{:S(2)}) async-start(f32[8,1,3,120,128]{4,3,2,1,0:T(8,128)} %shard_map.90), calls=%async_computation.2 | async-start | bytes 2949120 | tf_op jit(solution)/shard_map/all_to_all | solution.py:352
  105.4 18.2 %collective-permute-start.2 = (f32[6,3,120,128]{3,2,1,0:T(8,128)}, f32[6,3,120,128]{3,2,1,0:T(8,128)S(1)}, u32[]{:S(2)}, u32[]{:S(2)}) collective-permute-start(f32[6,3,120,128]{3,2,1,0:T(8,128)} %get-tuple-element.19), channel_id=1, source_target_pairs={{0,8},{8,16},{16,24},{24,32},{32,40},{40,48},{48,56},{56,64},{64,7... | collective-permute-start | bytes 3317768 | tf_op jit(solution)/shard_map/ppermute | solution.py:421
  110.9 18.2 %collective-permute-start.3 = (f32[6,3,120,128]{3,2,1,0:T(8,128)}, f32[6,3,120,128]{3,2,1,0:T(8,128)S(1)}, u32[]{:S(2)}, u32[]{:S(2)}) collective-permute-start(f32[6,3,120,128]{3,2,1,0:T(8,128)} %get-tuple-element.18), channel_id=1, source_target_pairs={{8,0},{16,8},{24,16},{32,24},{40,32},{48,40},{56,48},{64,56},{72,6... | collective-permute-start | bytes 3317768 | tf_op jit(solution)/shard_map/ppermute | solution.py:422
  129.1 1.3 copy-start.3
  130.4 1.3 copy-start.5
